TPU v7x, 256 devices: a whole 4x4x8 slice. The times are simulated.
256 devices in a mesh: gx: 8 (over x, core), gy: 32 (over y, z).
Axes of the slice: x: 4, y: 4, z: 8, core: 2. Of those that a mesh axis runs over, the one named last changes fastest.
Arguments:
- features: bfloat16 [65536, 128], P(('gx', 'gy')), may hold values from -6 to 6
- tile_vals: bfloat16 [16384, 128, 128], P(('gx', 'gy')), may hold values from -0.125 to 0.125
- tile_row: int32 [16384], P(('gx', 'gy')), may hold values from 0 to 511, as said below
- tile_col: int32 [16384], P(('gx', 'gy')), may hold values from 0 to 511, as said below
- tile_work: int32 [16384], P(('gx', 'gy')), may hold values from 0 to 16384, as said below
Outputs:
- product: float32 [65536, 128], P(('gx', 'gy'))
- moved_vals: bfloat16 [8192, 128, 128], P(('gx', 'gy'))
- moved_row: int32 [8192], P(('gx', 'gy'))
- moved_col: int32 [8192], P(('gx', 'gy'))
- moved_work: int32 [8192], P(('gx', 'gy'))
Inputs may be any that keep to these rules, and one draw needn't show every extreme that they name: `tile_work`: on every device the live slots come first; each gx row of 32 devices holds exactly 1024 live tiles, and in every row one device has all 64 slots live. `tile_row`: A tile held by device (a, b) has a row block owned by a device of gx index a. `tile_col`: A tile held by device (a, b) has a column block owned by a device of gy index b.
All inputs are finite; a program needn't handle non-finite values.
Results may differ from a plain program's by a relative error of at most 0.001.
Values may be sent and summed in bfloat16 or wider, within the bound.
No kernel may reach another device: no remote copies, remote signals or barrier semaphores. Data moves between devices by JAX's collectives and lax.ppermute only.
A program may use at most 64 MiB of HBM per device.

v0:
```python
import jax
import jax.numpy as jnp
from jax import lax
from jax.experimental import pallas as pl
from jax.experimental.pallas import tpu as pltpu
from jax.sharding import Mesh
from jax.sharding import PartitionSpec as P

GY = ("y", "z")
GX_GY = ("gx", "y", "z")

ANY = pl.BlockSpec(memory_space=pl.ANY)
SMEM = pl.BlockSpec(memory_space=pltpu.SMEM)
VMEM = pl.BlockSpec(memory_space=pltpu.VMEM)


def in_vmem(array):
    return pltpu.with_memory_space_constraint(array, pltpu.VMEM)


def in_hbm(array):
    return pltpu.with_memory_space_constraint(array, pltpu.HBM)


def vmem(shape, dtype):
    return pltpu.VMEM(shape, dtype)


def limit(mib):
    return pltpu.CompilerParams(vmem_limit_bytes=mib * 2**20)


def shifted(array, axis, by):
    size = lax.axis_size(axis)
    return lax.ppermute(array, axis, [(i, (i + by) % size) for i in range(size)])


def tell_kernel(slots, row_ref, col_ref, work_ref, out_ref):
    work = work_ref[...].reshape(1, slots)
    count = jnp.sum((work > 0).astype(jnp.int32), axis=1, keepdims=True)
    pairs = (
        (row_ref[...].reshape(1, slots), col_ref[...].reshape(1, slots)),
        (work, jnp.broadcast_to(count, (1, slots))),
    )
    for i, pair in enumerate(pairs):
        line = jnp.concatenate(pair, axis=1)
        out_ref[:, i, :] = jnp.broadcast_to(line, (out_ref.shape[0], 2 * slots))


def plan_kernel(peers, slots, me_ref, meta_ref, vals_ref, sent_ref, row_ref, col_ref, work_ref, slot_ref, held, sems, out_sems):
    me = me_ref[0]
    share = slots // peers

    def before(s, total):
        return total + jnp.where(s < me, meta_ref[s, 1, slots], 0)

    first = lax.fori_loop(0, peers, before, jnp.int32(0))
    turn = lax.rem(first, peers)

    groups = sems.shape[0]
    part = peers // groups
    size = part * share

    def start(d, carry):
        for w in range(share):
            tile = lax.rem(d - turn + peers, peers) + w * peers
            pltpu.make_async_copy(vals_ref.at[tile], held.at[d * share + w], sems.at[d // part]).start()
        return carry

    lax.fori_loop(0, peers, start, 0)

    def piece(ref, g):
        return ref.at[pl.ds(g * size, size)]

    leaving = [
        pltpu.make_async_copy(piece(held, g), piece(sent_ref, g), out_sems.at[g]) for g in range(groups)
    ]
    for g, c in enumerate(leaving):
        pltpu.make_async_copy(piece(vals_ref, g), piece(held, g), sems.at[g]).wait()
        c.start()

    def source(s, begin):
        count = meta_ref[s, 1, slots]
        j = lax.rem(me - lax.rem(begin, peers) + peers, peers)
        for w in range(share):
            at = j + w * peers

            @pl.when(at < count)
            def _():
                k = (begin + at) // peers
                row_ref[k] = meta_ref[s, 0, at]
                col_ref[k] = meta_ref[s, 0, slots + at]
                work_ref[k] = meta_ref[s, 1, at]
                slot_ref[k] = s * share + w

        return begin + count

    lax.fori_loop(0, peers, source, jnp.int32(0))

    for c in leaving:
        c.wait()


def keep_kernel(owned, slot_ref, got_ref, out_ref, sems):
    def start(k, carry):
        pltpu.make_async_copy(got_ref.at[slot_ref[k]], out_ref.at[k], sems.at[0]).start()
        return carry

    lax.fori_loop(0, owned, start, 0)
    pltpu.make_async_copy(got_ref.at[pl.ds(0, owned)], out_ref, sems.at[0]).wait()


def coded(x, q_ref, exps_ref, at, row):
    top = jnp.maximum(jnp.max(jnp.abs(x), axis=0, keepdims=True), 1e-30)
    exponent = jnp.ceil(jnp.log2(top))
    scaled = jnp.round(x * jnp.exp2(15.0 - exponent))
    scaled = jnp.minimum(jnp.maximum(scaled, -32767.0), 32767.0)
    q_ref[pl.ds(at, x.shape[0]), :] = scaled.astype(jnp.int32).astype(jnp.int16)
    exps_ref[pl.ds(row, 1), :] = exponent


def product_kernel(gx, gy, groups, steps, me_ref, row_ref, col_ref, work_ref, vals_ref, feats_ref, *refs):
    x_refs, rest = refs[: gx // 2 - 1], refs[gx // 2 - 1 :]
    own_ref, q_refs, (tiles, acc, held, made, exps, sems) = rest[0], rest[1:groups], rest[groups:]
    slots, order, _ = tiles.shape
    per_step = slots // steps
    vblocks = held.shape[0] // gx
    blocks = acc.shape[0]
    span = blocks // groups
    a, y = me_ref[1], me_ref[2]
    cores = 2

    loads = [
        pltpu.make_async_copy(
            vals_ref.at[pl.ds(i * per_step, per_step)], tiles.at[pl.ds(i * per_step, per_step)], sems.at[i]
        )
        for i in range(steps)
    ]
    for c in loads:
        c.start()
    acc[...] = jnp.zeros_like(acc)
    for k, f in enumerate((feats_ref, *x_refs)):
        held[pl.ds(k * cores * vblocks, cores * vblocks)] = f[...]

    pattern = lax.broadcasted_iota(jnp.int32, (order, order), 0) * order + lax.broadcasted_iota(
        jnp.int32, (order, order), 1
    )
    for i in range(steps):
        loads[i].wait()

        def form(t, carry):
            tile = i * per_step + t
            col = col_ref[tile]
            home = lax.div(col, gy * vblocks)
            away = lax.rem(lax.div(a, cores) - lax.div(home, cores) + gx, gx // cores)
            side = lax.rem(a + home, cores)
            place = (away * cores + side) * vblocks + lax.rem(col, vblocks)
            masked = jnp.where(pattern < work_ref[tile], tiles[tile], jnp.zeros((), jnp.bfloat16))
            made[t] = jnp.dot(masked, held[place], preferred_element_type=jnp.float32)
            return carry

        lax.fori_loop(0, per_step, form, 0, unroll=True)

        def add(t, carry):
            row = lax.rem(row_ref[i * per_step + t], blocks)
            acc[row] += made[t]
            return carry

        lax.fori_loop(0, per_step, add, 0, unroll=True)

    def own(i, carry):
        own_ref[pl.ds(i * order, order), :] = acc[y * span + i]
        return carry

    for k, q_ref in enumerate(q_refs, 1):
        base = lax.rem(y + k, groups) * span

        def code(i, carry):
            coded(acc[base + i], q_ref, exps, i * order, i)
            return carry

        lax.fori_loop(0, span, code, 0, unroll=2)
        q_ref[pl.ds(span * order, 16), :] = exps[...].astype(jnp.int32).astype(jnp.int16)
    lax.fori_loop(0, span, own, 0)


def scales_of(ref, at):
    return jnp.exp2(ref[pl.ds(at, 16), :].astype(jnp.int32).astype(jnp.float32) - 15.0)


def middle_kernel(order, groups, me_ref, own_ref, *refs):
    n = len(refs) - groups - 2
    got, own_out, q_refs, scales, exps = refs[:n], refs[n], refs[n + 1 : n + groups], refs[-2], refs[-1]
    rows = own_ref.shape[0]
    span = rows // order // groups
    z = me_ref[3]
    exps[...] = jnp.zeros_like(exps)
    for n, g in enumerate(got):
        scales[pl.ds(16 * n, 16), :] = scales_of(g, rows)

    def total(block):
        at = block * order
        x = own_ref[pl.ds(at, order), :]
        for n, g in enumerate(got):
            part = g[pl.ds(at, order), :].astype(jnp.int32).astype(jnp.float32)
            x = x + part * scales[pl.ds(16 * n + block, 1), :]
        return x

    for i in range(span):
        own_out[pl.ds(i * order, order), :] = total(z * span + i)
    for k, q_ref in enumerate(q_refs, 1):
        base = lax.rem(z + k, groups) * span
        for i in range(span):
            coded(total(base + i), q_ref, exps, i * order, i)
        q_ref[pl.ds(span * order, 16), :] = exps[...].astype(jnp.int32).astype(jnp.int16)


def last_kernel(order, own_ref, *refs):
    got, out_ref = refs[:-1], refs[-1]
    rows = own_ref.shape[0]
    for i in range(rows // order):
        at = i * order
        x = own_ref[pl.ds(at, order), :]
        for g in got:
            part = g[pl.ds(at, order), :].astype(jnp.int32).astype(jnp.float32)
            x = x + part * scales_of(g, rows)[i : i + 1, :]
        out_ref[pl.ds(at, order), :] = x


def on_device(features, tile_vals, tile_row, tile_col, tile_work):
    peers = lax.axis_size(GY)
    gx, ny, nz = (lax.axis_size(axis) for axis in GX_GY)
    slots, order, _ = tile_vals.shape
    owned = slots // 2
    width = features.shape[1]
    vblocks = features.shape[0] // order
    blocks = peers * vblocks
    me = jnp.stack([lax.axis_index(GY), *(lax.axis_index(axis) for axis in GX_GY)]).astype(jnp.int32)

    told = pl.pallas_call(
        lambda *refs: tell_kernel(slots, *refs),
        in_specs=[VMEM] * 3,
        out_specs=VMEM,
        out_shape=vmem((peers, 2, 2 * slots), jnp.int32),
        compiler_params=limit(4),
        name="tell",
    )(tile_row, tile_col, tile_work)

    cores = 2
    mine = features.reshape(vblocks, order, width)
    swap = lax.ppermute(mine, "gx", [(i, i ^ 1) for i in range(gx)])
    meta = lax.all_to_all(told, GY, split_axis=0, concat_axis=0, tiled=True)
    both = jnp.concatenate([mine, swap])
    around = []
    for k in range(1, gx // cores):
        around.append(lax.ppermute(both, "gx", [(i, (i + cores * k) % gx) for i in range(gx)]))

    small = jax.ShapeDtypeStruct((owned,), jnp.int32)
    sent, moved_row, moved_col, moved_work, kept = pl.pallas_call(
        lambda *refs: plan_kernel(peers, slots, *refs),
        in_specs=[SMEM, SMEM, ANY],
        out_specs=[ANY, SMEM, SMEM, SMEM, SMEM],
        out_shape=[pltpu.HBM(tile_vals.shape, tile_vals.dtype), small, small, small, small],
        scratch_shapes=[
            pltpu.VMEM(tile_vals.shape, tile_vals.dtype),
            pltpu.SemaphoreType.DMA((8,)),
            pltpu.SemaphoreType.DMA((8,)),
        ],
        compiler_params=limit(4),
        name="plan",
    )(me, meta, in_hbm(tile_vals))
    got = lax.all_to_all(sent, GY, split_axis=0, concat_axis=0, tiled=True)

    steps = 8
    span = blocks // ny
    i16 = jnp.int16
    own, *coded_y = pl.pallas_call(
        lambda *refs: product_kernel(gx, peers, ny, steps, *refs),
        in_specs=[SMEM] * 4 + [ANY] + [VMEM] * (gx // cores),
        out_specs=[VMEM] * ny,
        out_shape=[vmem((span * order, width), jnp.float32)]
        + [vmem((span * order + 16, width), i16)] * (ny - 1),
        scratch_shapes=[
            pltpu.VMEM((slots, order, order), jnp.bfloat16),
            pltpu.VMEM((blocks, order, width), jnp.float32),
            pltpu.VMEM((gx * vblocks, order, width), jnp.bfloat16),
            pltpu.VMEM((slots // steps, order, width), jnp.float32),
            pltpu.VMEM((span, width), jnp.float32),
            pltpu.SemaphoreType.DMA((steps,)),
        ],
        compiler_params=limit(16),
        name="products",
    )(me, tile_row, tile_col, tile_work, in_hbm(tile_vals), *(in_vmem(f) for f in (both, *around)))
    got_y = [shifted(q, "y", k) for k, q in enumerate(coded_y, 1)]

    own, *coded_z = pl.pallas_call(
        lambda *refs: middle_kernel(order, nz, *refs),
        in_specs=[SMEM] + [VMEM] * ny,
        out_specs=[VMEM] * nz,
        out_shape=[vmem((vblocks * order, width), jnp.float32)]
        + [vmem((vblocks * order + 16, width), i16)] * (nz - 1),
        scratch_shapes=[
            pltpu.VMEM((16 * (ny - 1), width), jnp.float32),
            pltpu.VMEM((16, width), jnp.float32),
        ],
        compiler_params=limit(8),
        name="middle",
    )(me, own, *(in_vmem(g) for g in got_y))
    got_z = [shifted(q, "z", k) for k, q in enumerate(coded_z, 1)]

    product = pl.pallas_call(
        lambda *refs: last_kernel(order, *refs),
        in_specs=[VMEM] * nz,
        out_specs=VMEM,
        out_shape=jax.ShapeDtypeStruct((vblocks * order, width), jnp.float32),
        compiler_params=limit(8),
        name="last",
    )(own, *(in_vmem(g) for g in got_z))

    moved_vals = pl.pallas_call(
        lambda *refs: keep_kernel(owned, *refs),
        in_specs=[SMEM, VMEM],
        out_specs=ANY,
        out_shape=jax.ShapeDtypeStruct((owned, *tile_vals.shape[1:]), tile_vals.dtype),
        scratch_shapes=[pltpu.SemaphoreType.DMA((1,))],
        compiler_params=limit(4),
        name="keep",
    )(kept, in_vmem(got))
    return (product, moved_vals, moved_row, moved_col, moved_work)


def solution(mesh):
    finer = Mesh(mesh.devices.reshape(mesh.shape["gx"], 4, 8), GX_GY)
    in_specs = (P(GX_GY, None), P(GX_GY, None, None), P(GX_GY), P(GX_GY), P(GX_GY))

    return jax.shard_map(on_device, mesh=finer, in_specs=in_specs, out_specs=in_specs, check_vma=False)
```

profile of v0, /device:TPU:40, one launch (start us, length us, event | category | flops | bytes accessed | tf_op | source)
XLA Modules:
  0.0 116.2 jit_solution(17997299029158898532)
XLA Ops:
  0.6 0.6 copy-done
  1.3 0.7 copy-done.2
  1.9 0.7 copy-done.4
  2.6 0.7 tell.1
  3.3 11.2 %all-to-all-start = ((s32[32,2,128]{2,1,0:T(2,128)}), s32[32,2,128]{2,1,0:T(2,128)S(1)}, u32[]{:S(2)}, u32[]{:S(2)}) async-start(s32[32,2,128]{2,1,0:T(2,128)} %tell.1), calls=%async_computation | async-start | bytes 65536 | tf_op jit(solution)/shard_map/all_to_all | solution.py:252
  14.7 7.9 %all-to-all-done.refs_1_ = s32[32,2,128]{2,1,0:T(2,128)S(1)} async-done(((s32[32,2,128]{2,1,0:T(2,128)}), s32[32,2,128]{2,1,0:T(2,128)S(1)}, u32[]{:S(2)}, u32[]{:S(2)}) %all-to-all-start) | async-done | bytes 32800 | tf_op jit(solution)/shard_map/all_to_all | solution.py:252
  22.5 4.4 %plan.1 = (bf16[64,128,128]{2,1,0:T(8,128)(2,1)}, s32[32]{0:T(128)}, s32[32]{0:T(128)}, s32[32]{0:T(128)}, s32[32]{0:T(128)S(1)}) custom-call(s32[4]{0:T(128)S(1)} %pad_add_fusion.refs_0_, s32[32,2,128]{2,1,0:T(2,128)S(1)} %all-to-all-done.refs_1_, bf16[64,128,128]{2,1,0:T(8,128)(2,1)} %refs_2_.5), custom_call_target="tpu_custom_call" | custom-call | tf_op jit(solution)/shard_map/plan/pallas_call | solution.py:259
  27.0 6.0 %all-to-all-start.1 = ((bf16[64,128,128]{2,1,0:T(8,128)(2,1)}), bf16[64,128,128]{2,1,0:T(8,128)(2,1)S(1)}, u32[]{:S(2)}, u32[]{:S(2)}) async-start(bf16[64,128,128]{2,1,0:T(8,128)(2,1)} %get-tuple-element.35), calls=%async_computation.1 | async-start | bytes 4194304 | tf_op jit(solution)/shard_map/all_to_all | solution.py:272
  33.2 1.2 %collective-permute-done = bf16[2,128,128]{2,1,0:T(8,128)(2,1)S(1)} collective-permute-done((bf16[2,128,128]{2,1,0:T(8,128)(2,1)S(1)}, bf16[2,128,128]{2,1,0:T(8,128)(2,1)S(1)}, u32[]{:S(2)}, u32[]{:S(2)}) %collective-permute-start) | collective-permute-done | bytes 65568 | tf_op jit(solution)/shard_map/ppermute | solution.py:251
  34.4 1.6 %collective-permute-start.1 = (bf16[4,128,128]{2,1,0:T(8,128)(2,1)S(1)}, bf16[4,128,128]{2,1,0:T(8,128)(2,1)S(1)}, u32[]{:S(2)}, u32[]{:S(2)}) collective-permute-start(bf16[4,128,128]{2,1,0:T(8,128)(2,1)S(1)} %pad_maximum_fusion.refs_5_), channel_id=1, source_target_pairs={{0,64},{32,96},{64,128},{96,160},{128,192},{160,224},{192,0},{224,... | collective-permute-start | bytes 393224 | tf_op jit(solution)/shard_map/ppermute | solution.py:256
  36.0 2.7 %collective-permute-start.2 = (bf16[4,128,128]{2,1,0:T(8,128)(2,1)S(1)}, bf16[4,128,128]{2,1,0:T(8,128)(2,1)S(1)}, u32[]{:S(2)}, u32[]{:S(2)}) collective-permute-start(bf16[4,128,128]{2,1,0:T(8,128)(2,1)S(1)} %pad_maximum_fusion.refs_5_), channel_id=1, source_target_pairs={{0,128},{32,160},{64,192},{96,224},{128,0},{160,32},{192,64},{224,... | collective-permute-start | bytes 393224 | tf_op jit(solution)/shard_map/ppermute | solution.py:256
  38.7 1.4 %collective-permute-start.3 = (bf16[4,128,128]{2,1,0:T(8,128)(2,1)S(1)}, bf16[4,128,128]{2,1,0:T(8,128)(2,1)S(1)}, u32[]{:S(2)}, u32[]{:S(2)}) collective-permute-start(bf16[4,128,128]{2,1,0:T(8,128)(2,1)S(1)} %pad_maximum_fusion.refs_5_), channel_id=1, source_target_pairs={{0,192},{32,224},{64,0},{96,32},{128,64},{160,96},{192,128},{224,1... | collective-permute-start | bytes 393224 | tf_op jit(solution)/shard_map/ppermute | solution.py:256
  40.2 1.1 collective-permute-done.1.refs_6_
  41.3 3.8 %collective-permute-done.2.refs_7_ = bf16[4,128,128]{2,1,0:T(8,128)(2,1)S(1)} collective-permute-done((bf16[4,128,128]{2,1,0:T(8,128)(2,1)S(1)}, bf16[4,128,128]{2,1,0:T(8,128)(2,1)S(1)}, u32[]{:S(2)}, u32[]{:S(2)}) %collective-permute-start.2) | collective-permute-done | bytes 131104 | tf_op jit(solution)/shard_map/ppermute | solution.py:256
  45.1 4.9 %products.1 = (f32[2048,128]{1,0:T(8,128)S(1)}, s16[2064,128]{1,0:T(8,128)(2,1)S(1)}, s16[2064,128]{1,0:T(8,128)(2,1)S(1)}, s16[2064,128]{1,0:T(8,128)(2,1)S(1)}) custom-call(s32[4]{0:T(128)S(1)} %pad_add_fusion.refs_0_, s32[64]{0:T(128)S(1)} %copy-done.1, s32[64]{0:T(128)S(1)} %copy-done.3, s32[64]{0:T(128)S(1)} %copy-done.5, ...), custom_call_target="tpu_custom_call" | custom-call | tf_op jit(solution)/shard_map/products/pallas_call | solution.py:277
  50.0 1.6 %collective-permute-start.4 = (s16[2064,128]{1,0:T(8,128)(2,1)S(1)}, s16[2064,128]{1,0:T(8,128)(2,1)S(1)}, u32[]{:S(2)}, u32[]{:S(2)}) collective-permute-start(s16[2064,128]{1,0:T(8,128)(2,1)S(1)} %get-tuple-element.23), channel_id=1, source_target_pairs={{0,8},{8,16},{16,24},{24,0},{1,9},{9,17},{17,25},{25,1},{2,10},{10... | collective-permute-start | bytes 1585160 | tf_op jit(solution)/shard_map/ppermute | solution.py:35
  51.6 1.1 collective-permute-start.5
  52.6 2.2 %collective-permute-start.6 = (s16[2064,128]{1,0:T(8,128)(2,1)S(1)}, s16[2064,128]{1,0:T(8,128)(2,1)S(1)}, u32[]{:S(2)}, u32[]{:S(2)}) collective-permute-start(s16[2064,128]{1,0:T(8,128)(2,1)S(1)} %get-tuple-element.25), channel_id=1, source_target_pairs={{0,24},{8,0},{16,8},{24,16},{1,25},{9,1},{17,9},{25,17},{2,26},{10... | collective-permute-start | bytes 1585160 | tf_op jit(solution)/shard_map/ppermute | solution.py:35
  54.9 18.0 %collective-permute-done.4.refs_2_ = s16[2064,128]{1,0:T(8,128)(2,1)S(1)} collective-permute-done((s16[2064,128]{1,0:T(8,128)(2,1)S(1)}, s16[2064,128]{1,0:T(8,128)(2,1)S(1)}, u32[]{:S(2)}, u32[]{:S(2)}) %collective-permute-start.4) | collective-permute-done | bytes 528416 | tf_op jit(solution)/shard_map/ppermute | solution.py:35
  72.8 4.5 %collective-permute-done.5.refs_3_ = s16[2064,128]{1,0:T(8,128)(2,1)S(1)} collective-permute-done((s16[2064,128]{1,0:T(8,128)(2,1)S(1)}, s16[2064,128]{1,0:T(8,128)(2,1)S(1)}, u32[]{:S(2)}, u32[]{:S(2)}) %collective-permute-start.5) | collective-permute-done | bytes 528416 | tf_op jit(solution)/shard_map/ppermute | solution.py:35
  77.4 11.8 %collective-permute-done.6.refs_4_ = s16[2064,128]{1,0:T(8,128)(2,1)S(1)} collective-permute-done((s16[2064,128]{1,0:T(8,128)(2,1)S(1)}, s16[2064,128]{1,0:T(8,128)(2,1)S(1)}, u32[]{:S(2)}, u32[]{:S(2)}) %collective-permute-start.6) | collective-permute-done | bytes 528416 | tf_op jit(solution)/shard_map/ppermute | solution.py:35
  89.1 1.1 middle.1
  90.3 4.0 %collective-permute-start.10 = (s16[272,128]{1,0:T(8,128)(2,1)S(1)}, s16[272,128]{1,0:T(8,128)(2,1)S(1)}, u32[]{:S(2)}, u32[]{:S(2)}) collective-permute-start(s16[272,128]{1,0:T(8,128)(2,1)S(1)} %get-tuple-element.30), channel_id=1, source_target_pairs={{0,4},{1,5},{2,6},{3,7},{4,0},{5,1},{6,2},{7,3},{8,12},{9,13},{10,... | collective-permute-start | bytes 208904 | tf_op jit(solution)/shard_map/ppermute | solution.py:35
  94.3 2.3 %collective-permute-start.11 = (s16[272,128]{1,0:T(8,128)(2,1)S(1)}, s16[272,128]{1,0:T(8,128)(2,1)S(1)}, u32[]{:S(2)}, u32[]{:S(2)}) collective-permute-start(s16[272,128]{1,0:T(8,128)(2,1)S(1)} %get-tuple-element.31), channel_id=1, source_target_pairs={{0,5},{1,6},{2,7},{3,0},{4,1},{5,2},{6,3},{7,4},{8,13},{9,14},{10,... | collective-permute-start | bytes 208904 | tf_op jit(solution)/shard_map/ppermute | solution.py:35
  96.7 2.4 %collective-permute-start.13 = (s16[272,128]{1,0:T(8,128)(2,1)S(1)}, s16[272,128]{1,0:T(8,128)(2,1)S(1)}, u32[]{:S(2)}, u32[]{:S(2)}) collective-permute-start(s16[272,128]{1,0:T(8,128)(2,1)S(1)} %get-tuple-element.33), channel_id=1, source_target_pairs={{0,7},{1,0},{2,1},{3,2},{4,3},{5,4},{6,5},{7,6},{8,15},{9,8},{10,9... | collective-permute-start | bytes 208904 | tf_op jit(solution)/shard_map/ppermute | solution.py:35
  99.1 5.3 %collective-permute-start.8 = (s16[272,128]{1,0:T(8,128)(2,1)S(1)}, s16[272,128]{1,0:T(8,128)(2,1)S(1)}, u32[]{:S(2)}, u32[]{:S(2)}) collective-permute-start(s16[272,128]{1,0:T(8,128)(2,1)S(1)} %get-tuple-element.28), channel_id=1, source_target_pairs={{0,2},{1,3},{2,4},{3,5},{4,6},{5,7},{6,0},{7,1},{8,10},{9,11},{10,... | collective-permute-start | bytes 208904 | tf_op jit(solution)/shard_map/ppermute | solution.py:35
  104.3 2.2 %collective-permute-done.11.refs_5_ = s16[272,128]{1,0:T(8,128)(2,1)S(1)} collective-permute-done((s16[272,128]{1,0:T(8,128)(2,1)S(1)}, s16[272,128]{1,0:T(8,128)(2,1)S(1)}, u32[]{:S(2)}, u32[]{:S(2)}) %collective-permute-start.11) | collective-permute-done | bytes 69664 | tf_op jit(solution)/shard_map/ppermute | solution.py:35
  106.5 0.9 collective-permute-start.9
  107.4 0.2 collective-permute-done.13.refs_7_
  107.7 6.2 %collective-permute-done.9.refs_3_ = s16[272,128]{1,0:T(8,128)(2,1)S(1)} collective-permute-done((s16[272,128]{1,0:T(8,128)(2,1)S(1)}, s16[272,128]{1,0:T(8,128)(2,1)S(1)}, u32[]{:S(2)}, u32[]{:S(2)}) %collective-permute-start.9) | collective-permute-done | bytes 69664 | tf_op jit(solution)/shard_map/ppermute | solution.py:35
  113.9 0.8 last.1
  114.7 1.5 %keep.1 = bf16[32,128,128]{2,1,0:T(8,128)(2,1)} custom-call(s32[32]{0:T(128)S(1)} %get-tuple-element.34.refs_0_, bf16[64,128,128]{2,1,0:T(8,128)(2,1)S(1)} %all-to-all-done.1.refs_1_), custom_call_target="tpu_custom_call" | custom-call | tf_op jit(solution)/shard_map/keep/pallas_call | solution.py:320
  (22 shorter events, 0.3 us)
Async XLA Ops:
  0.6 0.7 copy-start
  1.3 0.7 copy-start.2
  1.9 0.7 copy-start.4
  3.3 19.2 %all-to-all-start = ((s32[32,2,128]{2,1,0:T(2,128)}), s32[32,2,128]{2,1,0:T(2,128)S(1)}, u32[]{:S(2)}, u32[]{:S(2)}) async-start(s32[32,2,128]{2,1,0:T(2,128)} %tell.1), calls=%async_computation | async-start | bytes 65536 | tf_op jit(solution)/shard_map/all_to_all | solution.py:252
  27.0 6.1 %copy-start.6 = (bf16[256,128]{1,0:T(8,128)(2,1)S(1)}, bf16[256,128]{1,0:T(8,128)(2,1)}, u32[]{:S(2)}) copy-start(bf16[256,128]{1,0:T(8,128)(2,1)} %param.5) | copy-start | bytes 196612
  27.0 18.1 %copy-start.1 = (s32[64]{0:T(128)S(1)}, s32[64]{0:T(128)}, u32[]{:S(2)}) copy-start(s32[64]{0:T(128)} %refs_0_.1) | copy-start | bytes 772
  27.0 18.1 %copy-start.3 = (s32[64]{0:T(128)S(1)}, s32[64]{0:T(128)}, u32[]{:S(2)}) copy-start(s32[64]{0:T(128)} %refs_1_.3) | copy-start | bytes 772
  27.0 18.1 %copy-start.5 = (s32[64]{0:T(128)S(1)}, s32[64]{0:T(128)}, u32[]{:S(2)}) copy-start(s32[64]{0:T(128)} %refs_2_.4) | copy-start | bytes 772
  27.0 87.7 %all-to-all-start.1 = ((bf16[64,128,128]{2,1,0:T(8,128)(2,1)}), bf16[64,128,128]{2,1,0:T(8,128)(2,1)S(1)}, u32[]{:S(2)}, u32[]{:S(2)}) async-start(bf16[64,128,128]{2,1,0:T(8,128)(2,1)} %get-tuple-element.35), calls=%async_computation.1 | async-start | bytes 4194304 | tf_op jit(solution)/shard_map/all_to_all | solution.py:272
  33.1 1.3 %collective-permute-start = (bf16[2,128,128]{2,1,0:T(8,128)(2,1)S(1)}, bf16[2,128,128]{2,1,0:T(8,128)(2,1)S(1)}, u32[]{:S(2)}, u32[]{:S(2)}) collective-permute-start(bf16[2,128,128]{2,1,0:T(8,128)(2,1)S(1)} %bitcast.5), channel_id=1, source_target_pairs={{0,32},{32,0},{64,96},{96,64},{128,160},{160,128},{192,224},{224,1... | collective-permute-start | bytes 196616 | tf_op jit(solution)/shard_map/ppermute | solution.py:251
  34.4 6.8 %collective-permute-start.1 = (bf16[4,128,128]{2,1,0:T(8,128)(2,1)S(1)}, bf16[4,128,128]{2,1,0:T(8,128)(2,1)S(1)}, u32[]{:S(2)}, u32[]{:S(2)}) collective-permute-start(bf16[4,128,128]{2,1,0:T(8,128)(2,1)S(1)} %pad_maximum_fusion.refs_5_), channel_id=1, source_target_pairs={{0,64},{32,96},{64,128},{96,160},{128,192},{160,224},{192,0},{224,... | collective-permute-start | bytes 393224 | tf_op jit(solution)/shard_map/ppermute | solution.py:256
  36.0 9.1 %collective-permute-start.2 = (bf16[4,128,128]{2,1,0:T(8,128)(2,1)S(1)}, bf16[4,128,128]{2,1,0:T(8,128)(2,1)S(1)}, u32[]{:S(2)}, u32[]{:S(2)}) collective-permute-start(bf16[4,128,128]{2,1,0:T(8,128)(2,1)S(1)} %pad_maximum_fusion.refs_5_), channel_id=1, source_target_pairs={{0,128},{32,160},{64,192},{96,224},{128,0},{160,32},{192,64},{224,... | collective-permute-start | bytes 393224 | tf_op jit(solution)/shard_map/ppermute | solution.py:256
  38.7 6.3 %collective-permute-start.3 = (bf16[4,128,128]{2,1,0:T(8,128)(2,1)S(1)}, bf16[4,128,128]{2,1,0:T(8,128)(2,1)S(1)}, u32[]{:S(2)}, u32[]{:S(2)}) collective-permute-start(bf16[4,128,128]{2,1,0:T(8,128)(2,1)S(1)} %pad_maximum_fusion.refs_5_), channel_id=1, source_target_pairs={{0,192},{32,224},{64,0},{96,32},{128,64},{160,96},{192,128},{224,1... | collective-permute-start | bytes 393224 | tf_op jit(solution)/shard_map/ppermute | solution.py:256
  50.0 22.8 %collective-permute-start.4 = (s16[2064,128]{1,0:T(8,128)(2,1)S(1)}, s16[2064,128]{1,0:T(8,128)(2,1)S(1)}, u32[]{:S(2)}, u32[]{:S(2)}) collective-permute-start(s16[2064,128]{1,0:T(8,128)(2,1)S(1)} %get-tuple-element.23), channel_id=1, source_target_pairs={{0,8},{8,16},{16,24},{24,0},{1,9},{9,17},{17,25},{25,1},{2,10},{10... | collective-permute-start | bytes 1585160 | tf_op jit(solution)/shard_map/ppermute | solution.py:35
  51.6 25.8 %collective-permute-start.5 = (s16[2064,128]{1,0:T(8,128)(2,1)S(1)}, s16[2064,128]{1,0:T(8,128)(2,1)S(1)}, u32[]{:S(2)}, u32[]{:S(2)}) collective-permute-start(s16[2064,128]{1,0:T(8,128)(2,1)S(1)} %get-tuple-element.24), channel_id=1, source_target_pairs={{0,16},{8,24},{16,0},{24,8},{1,17},{9,25},{17,1},{25,9},{2,18},{10... | collective-permute-start | bytes 1585160 | tf_op jit(solution)/shard_map/ppermute | solution.py:35
  52.6 36.5 %collective-permute-start.6 = (s16[2064,128]{1,0:T(8,128)(2,1)S(1)}, s16[2064,128]{1,0:T(8,128)(2,1)S(1)}, u32[]{:S(2)}, u32[]{:S(2)}) collective-permute-start(s16[2064,128]{1,0:T(8,128)(2,1)S(1)} %get-tuple-element.25), channel_id=1, source_target_pairs={{0,24},{8,0},{16,8},{24,16},{1,25},{9,1},{17,9},{25,17},{2,26},{10... | collective-permute-start | bytes 1585160 | tf_op jit(solution)/shard_map/ppermute | solution.py:35
  90.3 8.8 %collective-permute-start.10 = (s16[272,128]{1,0:T(8,128)(2,1)S(1)}, s16[272,128]{1,0:T(8,128)(2,1)S(1)}, u32[]{:S(2)}, u32[]{:S(2)}) collective-permute-start(s16[272,128]{1,0:T(8,128)(2,1)S(1)} %get-tuple-element.30), channel_id=1, source_target_pairs={{0,4},{1,5},{2,6},{3,7},{4,0},{5,1},{6,2},{7,3},{8,12},{9,13},{10,... | collective-permute-start | bytes 208904 | tf_op jit(solution)/shard_map/ppermute | solution.py:35
  94.3 12.2 %collective-permute-start.11 = (s16[272,128]{1,0:T(8,128)(2,1)S(1)}, s16[272,128]{1,0:T(8,128)(2,1)S(1)}, u32[]{:S(2)}, u32[]{:S(2)}) collective-permute-start(s16[272,128]{1,0:T(8,128)(2,1)S(1)} %get-tuple-element.31), channel_id=1, source_target_pairs={{0,5},{1,6},{2,7},{3,0},{4,1},{5,2},{6,3},{7,4},{8,13},{9,14},{10,... | collective-permute-start | bytes 208904 | tf_op jit(solution)/shard_map/ppermute | solution.py:35
  96.6 10.8 %collective-permute-start.12 = (s16[272,128]{1,0:T(8,128)(2,1)S(1)}, s16[272,128]{1,0:T(8,128)(2,1)S(1)}, u32[]{:S(2)}, u32[]{:S(2)}) collective-permute-start(s16[272,128]{1,0:T(8,128)(2,1)S(1)} %get-tuple-element.32), channel_id=1, source_target_pairs={{0,6},{1,7},{2,0},{3,1},{4,2},{5,3},{6,4},{7,5},{8,14},{9,15},{10,... | collective-permute-start | bytes 208904 | tf_op jit(solution)/shard_map/ppermute | solution.py:35
  96.7 11.0 %collective-permute-start.13 = (s16[272,128]{1,0:T(8,128)(2,1)S(1)}, s16[272,128]{1,0:T(8,128)(2,1)S(1)}, u32[]{:S(2)}, u32[]{:S(2)}) collective-permute-start(s16[272,128]{1,0:T(8,128)(2,1)S(1)} %get-tuple-element.33), channel_id=1, source_target_pairs={{0,7},{1,0},{2,1},{3,2},{4,3},{5,4},{6,5},{7,6},{8,15},{9,8},{10,9... | collective-permute-start | bytes 208904 | tf_op jit(solution)/shard_map/ppermute | solution.py:35
  99.1 8.6 %collective-permute-start.7 = (s16[272,128]{1,0:T(8,128)(2,1)S(1)}, s16[272,128]{1,0:T(8,128)(2,1)S(1)}, u32[]{:S(2)}, u32[]{:S(2)}) collective-permute-start(s16[272,128]{1,0:T(8,128)(2,1)S(1)} %get-tuple-element.27), channel_id=1, source_target_pairs={{0,1},{1,2},{2,3},{3,4},{4,5},{5,6},{6,7},{7,0},{8,9},{9,10},{10,1... | collective-permute-start | bytes 208904 | tf_op jit(solution)/shard_map/ppermute | solution.py:35
  99.1 8.6 %collective-permute-start.8 = (s16[272,128]{1,0:T(8,128)(2,1)S(1)}, s16[272,128]{1,0:T(8,128)(2,1)S(1)}, u32[]{:S(2)}, u32[]{:S(2)}) collective-permute-start(s16[272,128]{1,0:T(8,128)(2,1)S(1)} %get-tuple-element.28), channel_id=1, source_target_pairs={{0,2},{1,3},{2,4},{3,5},{4,6},{5,7},{6,0},{7,1},{8,10},{9,11},{10,... | collective-permute-start | bytes 208904 | tf_op jit(solution)/shard_map/ppermute | solution.py:35
  106.5 7.4 %collective-permute-start.9 = (s16[272,128]{1,0:T(8,128)(2,1)S(1)}, s16[272,128]{1,0:T(8,128)(2,1)S(1)}, u32[]{:S(2)}, u32[]{:S(2)}) collective-permute-start(s16[272,128]{1,0:T(8,128)(2,1)S(1)} %get-tuple-element.29), channel_id=1, source_target_pairs={{0,3},{1,4},{2,5},{3,6},{4,7},{5,0},{6,1},{7,2},{8,11},{9,12},{10,... | collective-permute-start | bytes 208904 | tf_op jit(solution)/shard_map/ppermute | solution.py:35
where the time goes:
time: 117 us; the launch traced here: 116 us
  waiting for transfers between devices  57 us (49%)
  starting transfers between devices  42.9 us (37%)
  Pallas kernels  13.4 us (11%)
  local copies, waits for them, and re-layouts  1.99 us (2%)
    ppermute x10, waiting for transfers between devices, shifted(): lax.ppermute(array, axis, [(i, (i + by) % size) for i in range(size)])  42.9 us
    ppermute x10, starting transfers between devices, shifted(): lax.ppermute(array, axis, [(i, (i + by) % size) for i in range(size)])  19.8 us
    all_to_all x1, starting transfers between devices, on_device(): meta = lax.all_to_all(told, GY, split_axis=0, concat_axis=0, tiled=True)  11.2 us
    all_to_all x1, waiting for transfers between devices, on_device(): meta = lax.all_to_all(told, GY, split_axis=0, concat_axis=0, tiled=True)  7.88 us
    all_to_all x1, starting transfers between devices, on_device(): got = lax.all_to_all(sent, GY, split_axis=0, concat_axis=0, tiled=True)  6.04 us
    ppermute x3, starting transfers between devices, on_device(): lax.ppermute(both, 'gx', [(i, (i + cores * k) % gx) for i in range(gx)])  5.73 us
    ppermute x3, waiting for transfers between devices, on_device(): lax.ppermute(both, 'gx', [(i, (i + cores * k) % gx) for i in range(gx)])  4.91 us
    pallas_call x1, Pallas kernels, on_device(): pl.pallas_call(lambda *refs: product_kernel(gx, peers, ny, steps, *refs),...  4.87 us
  transfers between devices with their start and end apart: 16, of which 10 were waited for; matrix products, arithmetic and copies ran while one was open for 0% of the time, Pallas kernels for 6%

commit v1 on v0

--- a/solution.py
+++ b/solution.py
@@ -35,20 +35,38 @@
     return lax.ppermute(array, axis, [(i, (i + by) % size) for i in range(size)])
 
 
-def tell_kernel(slots, row_ref, col_ref, work_ref, out_ref):
-    work = work_ref[...].reshape(1, slots)
+def tell_kernel(slots, row_ref, col_ref, work_ref, out_ref, held, sems):
+    copies = [
+        pltpu.make_async_copy(ref, held.at[i], sems.at[i]) for i, ref in enumerate((row_ref, col_ref, work_ref))
+    ]
+    for c in copies:
+        c.start()
+    for c in copies:
+        c.wait()
+    row, col, work = (held[i].reshape(1, slots) for i in range(3))
     count = jnp.sum((work > 0).astype(jnp.int32), axis=1, keepdims=True)
-    pairs = (
-        (row_ref[...].reshape(1, slots), col_ref[...].reshape(1, slots)),
-        (work, jnp.broadcast_to(count, (1, slots))),
-    )
-    for i, pair in enumerate(pairs):
+    for i, pair in enumerate(((row, col), (work, jnp.broadcast_to(count, (1, slots))))):
         line = jnp.concatenate(pair, axis=1)
         out_ref[:, i, :] = jnp.broadcast_to(line, (out_ref.shape[0], 2 * slots))
 
 
-def plan_kernel(peers, slots, me_ref, meta_ref, vals_ref, sent_ref, row_ref, col_ref, work_ref, slot_ref, held, sems, out_sems):
-    me = me_ref[0]
+def stage_kernel(vals_ref, out_ref, sems):
+    groups = sems.shape[0]
+    size = vals_ref.shape[0] // groups
+    copies = [
+        pltpu.make_async_copy(
+            vals_ref.at[pl.ds(g * size, size)], out_ref.at[pl.ds(g * size, size)], sems.at[g]
+        )
+        for g in range(groups)
+    ]
+    for c in copies:
+        c.start()
+    for c in copies:
+        c.wait()
+
+
+def plan_kernel(peers, slots, meta_ref, vals_ref, sent_ref, row_ref, col_ref, work_ref, slot_ref, sems):
+    me = lax.axis_index("y") * lax.axis_size("z") + lax.axis_index("z")
     share = slots // peers
 
     def before(s, total):
@@ -56,28 +74,14 @@
 
     first = lax.fori_loop(0, peers, before, jnp.int32(0))
     turn = lax.rem(first, peers)
-
-    groups = sems.shape[0]
-    part = peers // groups
-    size = part * share
 
     def start(d, carry):
         for w in range(share):
             tile = lax.rem(d - turn + peers, peers) + w * peers
-            pltpu.make_async_copy(vals_ref.at[tile], held.at[d * share + w], sems.at[d // part]).start()
+            pltpu.make_async_copy(vals_ref.at[tile], sent_ref.at[d * share + w], sems.at[0]).start()
         return carry
 
-    lax.fori_loop(0, peers, start, 0)
-
-    def piece(ref, g):
-        return ref.at[pl.ds(g * size, size)]
-
-    leaving = [
-        pltpu.make_async_copy(piece(held, g), piece(sent_ref, g), out_sems.at[g]) for g in range(groups)
-    ]
-    for g, c in enumerate(leaving):
-        pltpu.make_async_copy(piece(vals_ref, g), piece(held, g), sems.at[g]).wait()
-        c.start()
+    lax.fori_loop(0, peers, start, 0, unroll=4)
 
     def source(s, begin):
         count = meta_ref[s, 1, slots]
@@ -97,8 +101,7 @@
 
     lax.fori_loop(0, peers, source, jnp.int32(0))
 
-    for c in leaving:
-        c.wait()
+    pltpu.make_async_copy(vals_ref, sent_ref, sems.at[0]).wait()
 
 
 def keep_kernel(owned, slot_ref, got_ref, out_ref, sems):
@@ -119,25 +122,17 @@
     exps_ref[pl.ds(row, 1), :] = exponent
 
 
-def product_kernel(gx, gy, groups, steps, me_ref, row_ref, col_ref, work_ref, vals_ref, feats_ref, *refs):
+def product_kernel(gx, gy, groups, steps, row_ref, col_ref, work_ref, tiles, feats_ref, *refs):
     x_refs, rest = refs[: gx // 2 - 1], refs[gx // 2 - 1 :]
-    own_ref, q_refs, (tiles, acc, held, made, exps, sems) = rest[0], rest[1:groups], rest[groups:]
+    own_ref, q_refs, (acc, held, made, exps) = rest[0], rest[1:groups], rest[groups:]
     slots, order, _ = tiles.shape
     per_step = slots // steps
     vblocks = held.shape[0] // gx
     blocks = acc.shape[0]
     span = blocks // groups
-    a, y = me_ref[1], me_ref[2]
+    a, y = lax.axis_index("gx"), lax.axis_index("y")
     cores = 2
 
-    loads = [
-        pltpu.make_async_copy(
-            vals_ref.at[pl.ds(i * per_step, per_step)], tiles.at[pl.ds(i * per_step, per_step)], sems.at[i]
-        )
-        for i in range(steps)
-    ]
-    for c in loads:
-        c.start()
     acc[...] = jnp.zeros_like(acc)
     for k, f in enumerate((feats_ref, *x_refs)):
         held[pl.ds(k * cores * vblocks, cores * vblocks)] = f[...]
@@ -146,7 +141,6 @@
         jnp.int32, (order, order), 1
     )
     for i in range(steps):
-        loads[i].wait()
 
         def form(t, carry):
             tile = i * per_step + t
@@ -188,12 +182,12 @@
     return jnp.exp2(ref[pl.ds(at, 16), :].astype(jnp.int32).astype(jnp.float32) - 15.0)
 
 
-def middle_kernel(order, groups, me_ref, own_ref, *refs):
+def middle_kernel(order, groups, own_ref, *refs):
     n = len(refs) - groups - 2
     got, own_out, q_refs, scales, exps = refs[:n], refs[n], refs[n + 1 : n + groups], refs[-2], refs[-1]
     rows = own_ref.shape[0]
     span = rows // order // groups
-    z = me_ref[3]
+    z = lax.axis_index("z")
     exps[...] = jnp.zeros_like(exps)
     for n, g in enumerate(got):
         scales[pl.ds(16 * n, 16), :] = scales_of(g, rows)
@@ -235,22 +229,30 @@
     width = features.shape[1]
     vblocks = features.shape[0] // order
     blocks = peers * vblocks
-    me = jnp.stack([lax.axis_index(GY), *(lax.axis_index(axis) for axis in GX_GY)]).astype(jnp.int32)
-
     told = pl.pallas_call(
         lambda *refs: tell_kernel(slots, *refs),
-        in_specs=[VMEM] * 3,
+        in_specs=[ANY] * 3,
         out_specs=VMEM,
-        out_shape=vmem((peers, 2, 2 * slots), jnp.int32),
+        out_shape=jax.ShapeDtypeStruct((peers, 2, 2 * slots), jnp.int32),
+        scratch_shapes=[pltpu.VMEM((3, slots), jnp.int32), pltpu.SemaphoreType.DMA((3,))],
         compiler_params=limit(4),
         name="tell",
-    )(tile_row, tile_col, tile_work)
+    )(*(in_hbm(t) for t in (tile_row, tile_col, tile_work)))
 
     cores = 2
     mine = features.reshape(vblocks, order, width)
     swap = lax.ppermute(mine, "gx", [(i, i ^ 1) for i in range(gx)])
     meta = lax.all_to_all(told, GY, split_axis=0, concat_axis=0, tiled=True)
     both = jnp.concatenate([mine, swap])
+    tiles = pl.pallas_call(
+        stage_kernel,
+        in_specs=[ANY],
+        out_specs=VMEM,
+        out_shape=vmem(tile_vals.shape, tile_vals.dtype),
+        scratch_shapes=[pltpu.SemaphoreType.DMA((8,))],
+        compiler_params=limit(4),
+        name="stage",
+    )(in_hbm(tile_vals))
     around = []
     for k in range(1, gx // cores):
         around.append(lax.ppermute(both, "gx", [(i, (i + cores * k) % gx) for i in range(gx)]))
@@ -258,17 +260,13 @@
     small = jax.ShapeDtypeStruct((owned,), jnp.int32)
     sent, moved_row, moved_col, moved_work, kept = pl.pallas_call(
         lambda *refs: plan_kernel(peers, slots, *refs),
-        in_specs=[SMEM, SMEM, ANY],
+        in_specs=[SMEM, VMEM],
         out_specs=[ANY, SMEM, SMEM, SMEM, SMEM],
         out_shape=[pltpu.HBM(tile_vals.shape, tile_vals.dtype), small, small, small, small],
-        scratch_shapes=[
-            pltpu.VMEM(tile_vals.shape, tile_vals.dtype),
-            pltpu.SemaphoreType.DMA((8,)),
-            pltpu.SemaphoreType.DMA((8,)),
-        ],
+        scratch_shapes=[pltpu.SemaphoreType.DMA((1,))],
         compiler_params=limit(4),
         name="plan",
-    )(me, meta, in_hbm(tile_vals))
+    )(meta, in_vmem(tiles))
     got = lax.all_to_all(sent, GY, split_axis=0, concat_axis=0, tiled=True)
 
     steps = 8
@@ -276,26 +274,26 @@
     i16 = jnp.int16
     own, *coded_y = pl.pallas_call(
         lambda *refs: product_kernel(gx, peers, ny, steps, *refs),
-        in_specs=[SMEM] * 4 + [ANY] + [VMEM] * (gx // cores),
+        in_specs=[SMEM] * 3 + [VMEM] * (1 + gx // cores),
         out_specs=[VMEM] * ny,
         out_shape=[vmem((span * order, width), jnp.float32)]
         + [vmem((span * order + 16, width), i16)] * (ny - 1),
         scratch_shapes=[
-            pltpu.VMEM((slots, order, order), jnp.bfloat16),
             pltpu.VMEM((blocks, order, width), jnp.float32),
             pltpu.VMEM((gx * vblocks, order, width), jnp.bfloat16),
             pltpu.VMEM((slots // steps, order, width), jnp.float32),
             pltpu.VMEM((span, width), jnp.float32),
-            pltpu.SemaphoreType.DMA((steps,)),
         ],
         compiler_params=limit(16),
         name="products",
-    )(me, tile_row, tile_col, tile_work, in_hbm(tile_vals), *(in_vmem(f) for f in (both, *around)))
-    got_y = [shifted(q, "y", k) for k, q in enumerate(coded_y, 1)]
+    )(tile_row, tile_col, tile_work, *(in_vmem(f) for f in (tiles, both, *around)))
+    got_y = []
+    for k, q in enumerate(coded_y, 1):
+        got_y.append(shifted(q, "y", k))
 
     own, *coded_z = pl.pallas_call(
         lambda *refs: middle_kernel(order, nz, *refs),
-        in_specs=[SMEM] + [VMEM] * ny,
+        in_specs=[VMEM] * ny,
         out_specs=[VMEM] * nz,
         out_shape=[vmem((vblocks * order, width), jnp.float32)]
         + [vmem((vblocks * order + 16, width), i16)] * (nz - 1),
@@ -305,7 +303,7 @@
         ],
         compiler_params=limit(8),
         name="middle",
-    )(me, own, *(in_vmem(g) for g in got_y))
+    )(own, *(in_vmem(g) for g in got_y))
     got_z = [shifted(q, "z", k) for k, q in enumerate(coded_z, 1)]
 
     product = pl.pallas_call(

time: 117 us -> 114 us (0.974)
  waiting for transfers between devices: 57 us -> 54.2 us
  starting transfers between devices: 42.9 us -> 45.3 us
  local copies, waits for them, and re-layouts: 1.99 us -> 0.03 us
    unnamed x14 -> x8, local copies, waits for them, and re-layouts: 1.99 us -> 0.03 us
    pallas_call x2 -> x3, Pallas kernels: 1.86 us -> 3.61 us  [the longest x1 1.58 us: on_device(): pl.pallas_call(stage_kernel, in_specs=[ANY], out_specs=VMEM, out_shape=vm...]
    ppermute x10, starting transfers between devices: 19.8 us -> 21.5 us  [shifted(): lax.ppermute(array, axis, [(i, (i + by) % size) for i in range(size)])]
    pallas_call x1, Pallas kernels: 4.87 us -> 3.3 us  [on_device(): pl.pallas_call(lambda *refs: product_kernel(gx, peers, ny, steps, *refs),...]
    all_to_all x1, waiting for transfers between devices: 7.88 us -> 6.38 us  [on_device(): meta = lax.all_to_all(told, GY, split_axis=0, concat_axis=0, tiled=True)]
    ppermute x10, waiting for transfers between devices: 42.9 us -> 41.6 us  [shifted(): lax.ppermute(array, axis, [(i, (i + by) % size) for i in range(size)])]
  transfers between devices with their start and end apart: 16 -> 16, of which waited for: 10 -> 9; matrix products, arithmetic and copies ran while one was open for 0% -> 0% of each run, Pallas kernels for 6% -> 6%
where the time goes in v1:
time: 114 us
  waiting for transfers between devices  54.2 us (48%)
  starting transfers between devices  45.3 us (40%)
  Pallas kernels  13.6 us (12%)
    ppermute x10, waiting for transfers between devices, shifted(): lax.ppermute(array, axis, [(i, (i + by) % size) for i in range(size)])  41.6 us
    ppermute x10, starting transfers between devices, shifted(): lax.ppermute(array, axis, [(i, (i + by) % size) for i in range(size)])  21.5 us
    all_to_all x1, starting transfers between devices, on_device(): meta = lax.all_to_all(told, GY, split_axis=0, concat_axis=0, tiled=True)  11.3 us
    all_to_all x1, starting transfers between devices, on_device(): got = lax.all_to_all(sent, GY, split_axis=0, concat_axis=0, tiled=True)  6.73 us
    all_to_all x1, waiting for transfers between devices, on_device(): meta = lax.all_to_all(told, GY, split_axis=0, concat_axis=0, tiled=True)  6.38 us
    ppermute x3, starting transfers between devices, on_device(): lax.ppermute(both, 'gx', [(i, (i + cores * k) % gx) for i in range(gx)])  5.73 us
    ppermute x3, waiting for transfers between devices, on_device(): lax.ppermute(both, 'gx', [(i, (i + cores * k) % gx) for i in range(gx)])  4.91 us
    pallas_call x1, Pallas kernels, on_device(): pl.pallas_call(lambda *refs: plan_kernel(peers, slots, *refs), in_specs=[...  3.36 us
  transfers between devices with their start and end apart: 16, of which 9 were waited for; matrix products, arithmetic and copies ran while one was open for 0% of the time, Pallas kernels for 6%

profile of v1, /device:TPU:40, one launch (start us, length us, event | category | flops | bytes accessed | tf_op | source)
XLA Modules:
  0.0 113.8 jit_solution(14498611919867202822)
XLA Ops:
  0.6 1.4 %tell.1 = s32[32,2,128]{2,1,0:T(2,128)} custom-call(s32[64]{0:T(128)} %refs_0_.3, s32[64]{0:T(128)} %refs_1_.3, s32[64]{0:T(128)} %refs_2_.3), custom_call_target="tpu_custom_call" | custom-call | tf_op jit(solution)/shard_map/tell/pallas_call | solution.py:232
  2.1 11.3 %all-to-all-start = ((s32[32,2,128]{2,1,0:T(2,128)}), s32[32,2,128]{2,1,0:T(2,128)S(1)}, u32[]{:S(2)}, u32[]{:S(2)}) async-start(s32[32,2,128]{2,1,0:T(2,128)} %tell.1), calls=%async_computation | async-start | bytes 65536 | tf_op jit(solution)/shard_map/all_to_all | solution.py:245
  13.3 1.6 %stage.1.refs_3_.refs_1_ = bf16[64,128,128]{2,1,0:T(8,128)(2,1)S(1)} custom-call(bf16[64,128,128]{2,1,0:T(8,128)(2,1)} %vals_ref.1), custom_call_target="tpu_custom_call" | custom-call | tf_op jit(solution)/shard_map/stage/pallas_call | solution.py:247
  14.9 6.4 %all-to-all-done.refs_0_ = s32[32,2,128]{2,1,0:T(2,128)S(1)} async-done(((s32[32,2,128]{2,1,0:T(2,128)}), s32[32,2,128]{2,1,0:T(2,128)S(1)}, u32[]{:S(2)}, u32[]{:S(2)}) %all-to-all-start) | async-done | bytes 32800 | tf_op jit(solution)/shard_map/all_to_all | solution.py:245
  21.3 3.4 %plan.1 = (bf16[64,128,128]{2,1,0:T(8,128)(2,1)}, s32[32]{0:T(128)}, s32[32]{0:T(128)}, s32[32]{0:T(128)}, s32[32]{0:T(128)S(1)}) custom-call(s32[32,2,128]{2,1,0:T(2,128)S(1)} %all-to-all-done.refs_0_, bf16[64,128,128]{2,1,0:T(8,128)(2,1)S(1)} %stage.1.refs_3_.refs_1_), custom_call_target="tpu_custom_call" | custom-call | tf_op jit(solution)/shard_map/plan/pallas_call | solution.py:261
  24.7 6.7 %all-to-all-start.1 = ((bf16[64,128,128]{2,1,0:T(8,128)(2,1)}), bf16[64,128,128]{2,1,0:T(8,128)(2,1)}, u32[]{:S(2)}, u32[]{:S(2)}) async-start(bf16[64,128,128]{2,1,0:T(8,128)(2,1)} %get-tuple-element.35), calls=%async_computation.1 | async-start | bytes 4194304 | tf_op jit(solution)/shard_map/all_to_all | solution.py:270
  31.5 0.1 collective-permute-start
  31.6 1.2 %collective-permute-done = bf16[2,128,128]{2,1,0:T(8,128)(2,1)S(1)} collective-permute-done((bf16[2,128,128]{2,1,0:T(8,128)(2,1)S(1)}, bf16[2,128,128]{2,1,0:T(8,128)(2,1)S(1)}, u32[]{:S(2)}, u32[]{:S(2)}) %collective-permute-start) | collective-permute-done | bytes 65568 | tf_op jit(solution)/shard_map/ppermute | solution.py:244
  32.8 1.6 %collective-permute-start.1 = (bf16[4,128,128]{2,1,0:T(8,128)(2,1)S(1)}, bf16[4,128,128]{2,1,0:T(8,128)(2,1)S(1)}, u32[]{:S(2)}, u32[]{:S(2)}) collective-permute-start(bf16[4,128,128]{2,1,0:T(8,128)(2,1)S(1)} %pad_maximum_fusion.refs_4_), channel_id=1, source_target_pairs={{0,64},{32,96},{64,128},{96,160},{128,192},{160,224},{192,0},{224,... | collective-permute-start | bytes 393224 | tf_op jit(solution)/shard_map/ppermute | solution.py:258
  34.4 2.7 %collective-permute-start.2 = (bf16[4,128,128]{2,1,0:T(8,128)(2,1)S(1)}, bf16[4,128,128]{2,1,0:T(8,128)(2,1)S(1)}, u32[]{:S(2)}, u32[]{:S(2)}) collective-permute-start(bf16[4,128,128]{2,1,0:T(8,128)(2,1)S(1)} %pad_maximum_fusion.refs_4_), channel_id=1, source_target_pairs={{0,128},{32,160},{64,192},{96,224},{128,0},{160,32},{192,64},{224,... | collective-permute-start | bytes 393224 | tf_op jit(solution)/shard_map/ppermute | solution.py:258
  37.1 1.4 %collective-permute-start.3 = (bf16[4,128,128]{2,1,0:T(8,128)(2,1)S(1)}, bf16[4,128,128]{2,1,0:T(8,128)(2,1)S(1)}, u32[]{:S(2)}, u32[]{:S(2)}) collective-permute-start(bf16[4,128,128]{2,1,0:T(8,128)(2,1)S(1)} %pad_maximum_fusion.refs_4_), channel_id=1, source_target_pairs={{0,192},{32,224},{64,0},{96,32},{128,64},{160,96},{192,128},{224,1... | collective-permute-start | bytes 393224 | tf_op jit(solution)/shard_map/ppermute | solution.py:258
  38.6 1.1 collective-permute-done.1.refs_5_
  39.7 3.8 %collective-permute-done.2.refs_6_ = bf16[4,128,128]{2,1,0:T(8,128)(2,1)S(1)} collective-permute-done((bf16[4,128,128]{2,1,0:T(8,128)(2,1)S(1)}, bf16[4,128,128]{2,1,0:T(8,128)(2,1)S(1)}, u32[]{:S(2)}, u32[]{:S(2)}) %collective-permute-start.2) | collective-permute-done | bytes 131104 | tf_op jit(solution)/shard_map/ppermute | solution.py:258
  43.5 3.3 %products.1 = (f32[2048,128]{1,0:T(8,128)S(1)}, s16[2064,128]{1,0:T(8,128)(2,1)S(1)}, s16[2064,128]{1,0:T(8,128)(2,1)S(1)}, s16[2064,128]{1,0:T(8,128)(2,1)S(1)}) custom-call(s32[64]{0:T(128)S(1)} %copy-done, s32[64]{0:T(128)S(1)} %copy-done.1, s32[64]{0:T(128)S(1)} %copy-done.2, bf16[64,128,128]{2,1,0:T(8,128)(2,1)S(1)} %stage.1.refs_3_.refs_1_, ...), custom_call_target="tpu_custom_call" | custom-call | tf_op jit(solution)/shard_map/products/pallas_call | solution.py:275
  46.8 1.6 %collective-permute-start.4 = (s16[2064,128]{1,0:T(8,128)(2,1)S(1)}, s16[2064,128]{1,0:T(8,128)(2,1)S(1)}, u32[]{:S(2)}, u32[]{:S(2)}) collective-permute-start(s16[2064,128]{1,0:T(8,128)(2,1)S(1)} %get-tuple-element.23), channel_id=1, source_target_pairs={{0,8},{8,16},{16,24},{24,0},{1,9},{9,17},{17,25},{25,1},{2,10},{10... | collective-permute-start | bytes 1585160 | tf_op jit(solution)/shard_map/ppermute | solution.py:35
  48.4 1.1 collective-permute-start.5
  49.4 2.2 %collective-permute-start.6 = (s16[2064,128]{1,0:T(8,128)(2,1)S(1)}, s16[2064,128]{1,0:T(8,128)(2,1)S(1)}, u32[]{:S(2)}, u32[]{:S(2)}) collective-permute-start(s16[2064,128]{1,0:T(8,128)(2,1)S(1)} %get-tuple-element.25), channel_id=1, source_target_pairs={{0,24},{8,0},{16,8},{24,16},{1,25},{9,1},{17,9},{25,17},{2,26},{10... | collective-permute-start | bytes 1585160 | tf_op jit(solution)/shard_map/ppermute | solution.py:35
  51.7 18.6 %collective-permute-done.4.refs_1_ = s16[2064,128]{1,0:T(8,128)(2,1)S(1)} collective-permute-done((s16[2064,128]{1,0:T(8,128)(2,1)S(1)}, s16[2064,128]{1,0:T(8,128)(2,1)S(1)}, u32[]{:S(2)}, u32[]{:S(2)}) %collective-permute-start.4) | collective-permute-done | bytes 528416 | tf_op jit(solution)/shard_map/ppermute | solution.py:35
  70.3 4.5 %collective-permute-done.5.refs_2_ = s16[2064,128]{1,0:T(8,128)(2,1)S(1)} collective-permute-done((s16[2064,128]{1,0:T(8,128)(2,1)S(1)}, s16[2064,128]{1,0:T(8,128)(2,1)S(1)}, u32[]{:S(2)}, u32[]{:S(2)}) %collective-permute-start.5) | collective-permute-done | bytes 528416 | tf_op jit(solution)/shard_map/ppermute | solution.py:35
  74.8 11.7 %collective-permute-done.6.refs_3_ = s16[2064,128]{1,0:T(8,128)(2,1)S(1)} collective-permute-done((s16[2064,128]{1,0:T(8,128)(2,1)S(1)}, s16[2064,128]{1,0:T(8,128)(2,1)S(1)}, u32[]{:S(2)}, u32[]{:S(2)}) %collective-permute-start.6) | collective-permute-done | bytes 528416 | tf_op jit(solution)/shard_map/ppermute | solution.py:35
  86.5 0.6 middle.1
  87.1 3.9 %collective-permute-start.10 = (s16[272,128]{1,0:T(8,128)(2,1)S(1)}, s16[272,128]{1,0:T(8,128)(2,1)S(1)}, u32[]{:S(2)}, u32[]{:S(2)}) collective-permute-start(s16[272,128]{1,0:T(8,128)(2,1)S(1)} %get-tuple-element.30), channel_id=1, source_target_pairs={{0,4},{1,5},{2,6},{3,7},{4,0},{5,1},{6,2},{7,3},{8,12},{9,13},{10,... | collective-permute-start | bytes 208904 | tf_op jit(solution)/shard_map/ppermute | solution.py:35
  91.0 2.7 %collective-permute-start.11 = (s16[272,128]{1,0:T(8,128)(2,1)S(1)}, s16[272,128]{1,0:T(8,128)(2,1)S(1)}, u32[]{:S(2)}, u32[]{:S(2)}) collective-permute-start(s16[272,128]{1,0:T(8,128)(2,1)S(1)} %get-tuple-element.31), channel_id=1, source_target_pairs={{0,5},{1,6},{2,7},{3,0},{4,1},{5,2},{6,3},{7,4},{8,13},{9,14},{10,... | collective-permute-start | bytes 208904 | tf_op jit(solution)/shard_map/ppermute | solution.py:35
  93.6 0.5 collective-permute-start.12
  94.1 1.9 %collective-permute-start.13 = (s16[272,128]{1,0:T(8,128)(2,1)S(1)}, s16[272,128]{1,0:T(8,128)(2,1)S(1)}, u32[]{:S(2)}, u32[]{:S(2)}) collective-permute-start(s16[272,128]{1,0:T(8,128)(2,1)S(1)} %get-tuple-element.33), channel_id=1, source_target_pairs={{0,7},{1,0},{2,1},{3,2},{4,3},{5,4},{6,5},{7,6},{8,15},{9,8},{10,9... | collective-permute-start | bytes 208904 | tf_op jit(solution)/shard_map/ppermute | solution.py:35
  96.0 0.1 collective-permute-start.7
  96.1 5.3 %collective-permute-start.8 = (s16[272,128]{1,0:T(8,128)(2,1)S(1)}, s16[272,128]{1,0:T(8,128)(2,1)S(1)}, u32[]{:S(2)}, u32[]{:S(2)}) collective-permute-start(s16[272,128]{1,0:T(8,128)(2,1)S(1)} %get-tuple-element.28), channel_id=1, source_target_pairs={{0,2},{1,3},{2,4},{3,5},{4,6},{5,7},{6,0},{7,1},{8,10},{9,11},{10,... | collective-permute-start | bytes 208904 | tf_op jit(solution)/shard_map/ppermute | solution.py:35
  101.4 1.8 %collective-permute-done.11.refs_5_ = s16[272,128]{1,0:T(8,128)(2,1)S(1)} collective-permute-done((s16[272,128]{1,0:T(8,128)(2,1)S(1)}, s16[272,128]{1,0:T(8,128)(2,1)S(1)}, u32[]{:S(2)}, u32[]{:S(2)}) %collective-permute-start.11) | collective-permute-done | bytes 69664 | tf_op jit(solution)/shard_map/ppermute | solution.py:35
  103.2 2.3 %collective-permute-start.9 = (s16[272,128]{1,0:T(8,128)(2,1)S(1)}, s16[272,128]{1,0:T(8,128)(2,1)S(1)}, u32[]{:S(2)}, u32[]{:S(2)}) collective-permute-start(s16[272,128]{1,0:T(8,128)(2,1)S(1)} %get-tuple-element.29), channel_id=1, source_target_pairs={{0,3},{1,4},{2,5},{3,6},{4,7},{5,0},{6,1},{7,2},{8,11},{9,12},{10,... | collective-permute-start | bytes 208904 | tf_op jit(solution)/shard_map/ppermute | solution.py:35
  105.5 5.0 %collective-permute-done.9.refs_3_ = s16[272,128]{1,0:T(8,128)(2,1)S(1)} collective-permute-done((s16[272,128]{1,0:T(8,128)(2,1)S(1)}, s16[272,128]{1,0:T(8,128)(2,1)S(1)}, u32[]{:S(2)}, u32[]{:S(2)}) %collective-permute-start.9) | collective-permute-done | bytes 69664 | tf_op jit(solution)/shard_map/ppermute | solution.py:35
  110.5 0.8 last.1
  111.3 2.6 %keep.1 = bf16[32,128,128]{2,1,0:T(8,128)(2,1)} custom-call(s32[32]{0:T(128)S(1)} %get-tuple-element.34.refs_0_, bf16[64,128,128]{2,1,0:T(8,128)(2,1)} %all-to-all-done.1.refs_1_), custom_call_target="tpu_custom_call" | custom-call | tf_op jit(solution)/shard_map/keep/pallas_call | solution.py:318
  (16 shorter events, 0.1 us)
Async XLA Ops:
  2.1 19.2 %all-to-all-start = ((s32[32,2,128]{2,1,0:T(2,128)}), s32[32,2,128]{2,1,0:T(2,128)S(1)}, u32[]{:S(2)}, u32[]{:S(2)}) async-start(s32[32,2,128]{2,1,0:T(2,128)} %tell.1), calls=%async_computation | async-start | bytes 65536 | tf_op jit(solution)/shard_map/all_to_all | solution.py:245
  24.7 6.8 %copy-start.3 = (bf16[256,128]{1,0:T(8,128)(2,1)S(1)}, bf16[256,128]{1,0:T(8,128)(2,1)}, u32[]{:S(2)}) copy-start(bf16[256,128]{1,0:T(8,128)(2,1)} %param.5) | copy-start | bytes 196612
  24.7 18.8 %copy-start = (s32[64]{0:T(128)S(1)}, s32[64]{0:T(128)}, u32[]{:S(2)}) copy-start(s32[64]{0:T(128)} %refs_0_.3) | copy-start | bytes 772
  24.7 18.8 %copy-start.1 = (s32[64]{0:T(128)S(1)}, s32[64]{0:T(128)}, u32[]{:S(2)}) copy-start(s32[64]{0:T(128)} %refs_1_.3) | copy-start | bytes 772
  24.7 18.8 %copy-start.2 = (s32[64]{0:T(128)S(1)}, s32[64]{0:T(128)}, u32[]{:S(2)}) copy-start(s32[64]{0:T(128)} %refs_2_.3) | copy-start | bytes 772
  24.7 86.6 %all-to-all-start.1 = ((bf16[64,128,128]{2,1,0:T(8,128)(2,1)}), bf16[64,128,128]{2,1,0:T(8,128)(2,1)}, u32[]{:S(2)}, u32[]{:S(2)}) async-start(bf16[64,128,128]{2,1,0:T(8,128)(2,1)} %get-tuple-element.35), calls=%async_computation.1 | async-start | bytes 4194304 | tf_op jit(solution)/shard_map/all_to_all | solution.py:270
  31.5 1.3 %collective-permute-start = (bf16[2,128,128]{2,1,0:T(8,128)(2,1)S(1)}, bf16[2,128,128]{2,1,0:T(8,128)(2,1)S(1)}, u32[]{:S(2)}, u32[]{:S(2)}) collective-permute-start(bf16[2,128,128]{2,1,0:T(8,128)(2,1)S(1)} %bitcast.1), channel_id=1, source_target_pairs={{0,32},{32,0},{64,96},{96,64},{128,160},{160,128},{192,224},{224,1... | collective-permute-start | bytes 196616 | tf_op jit(solution)/shard_map/ppermute | solution.py:244
  32.8 6.8 %collective-permute-start.1 = (bf16[4,128,128]{2,1,0:T(8,128)(2,1)S(1)}, bf16[4,128,128]{2,1,0:T(8,128)(2,1)S(1)}, u32[]{:S(2)}, u32[]{:S(2)}) collective-permute-start(bf16[4,128,128]{2,1,0:T(8,128)(2,1)S(1)} %pad_maximum_fusion.refs_4_), channel_id=1, source_target_pairs={{0,64},{32,96},{64,128},{96,160},{128,192},{160,224},{192,0},{224,... | collective-permute-start | bytes 393224 | tf_op jit(solution)/shard_map/ppermute | solution.py:258
  34.4 9.1 %collective-permute-start.2 = (bf16[4,128,128]{2,1,0:T(8,128)(2,1)S(1)}, bf16[4,128,128]{2,1,0:T(8,128)(2,1)S(1)}, u32[]{:S(2)}, u32[]{:S(2)}) collective-permute-start(bf16[4,128,128]{2,1,0:T(8,128)(2,1)S(1)} %pad_maximum_fusion.refs_4_), channel_id=1, source_target_pairs={{0,128},{32,160},{64,192},{96,224},{128,0},{160,32},{192,64},{224,... | collective-permute-start | bytes 393224 | tf_op jit(solution)/shard_map/ppermute | solution.py:258
  37.1 6.3 %collective-permute-start.3 = (bf16[4,128,128]{2,1,0:T(8,128)(2,1)S(1)}, bf16[4,128,128]{2,1,0:T(8,128)(2,1)S(1)}, u32[]{:S(2)}, u32[]{:S(2)}) collective-permute-start(bf16[4,128,128]{2,1,0:T(8,128)(2,1)S(1)} %pad_maximum_fusion.refs_4_), channel_id=1, source_target_pairs={{0,192},{32,224},{64,0},{96,32},{128,64},{160,96},{192,128},{224,1... | collective-permute-start | bytes 393224 | tf_op jit(solution)/shard_map/ppermute | solution.py:258
  46.8 23.5 %collective-permute-start.4 = (s16[2064,128]{1,0:T(8,128)(2,1)S(1)}, s16[2064,128]{1,0:T(8,128)(2,1)S(1)}, u32[]{:S(2)}, u32[]{:S(2)}) collective-permute-start(s16[2064,128]{1,0:T(8,128)(2,1)S(1)} %get-tuple-element.23), channel_id=1, source_target_pairs={{0,8},{8,16},{16,24},{24,0},{1,9},{9,17},{17,25},{25,1},{2,10},{10... | collective-permute-start | bytes 1585160 | tf_op jit(solution)/shard_map/ppermute | solution.py:35
  48.4 26.4 %collective-permute-start.5 = (s16[2064,128]{1,0:T(8,128)(2,1)S(1)}, s16[2064,128]{1,0:T(8,128)(2,1)S(1)}, u32[]{:S(2)}, u32[]{:S(2)}) collective-permute-start(s16[2064,128]{1,0:T(8,128)(2,1)S(1)} %get-tuple-element.24), channel_id=1, source_target_pairs={{0,16},{8,24},{16,0},{24,8},{1,17},{9,25},{17,1},{25,9},{2,18},{10... | collective-permute-start | bytes 1585160 | tf_op jit(solution)/shard_map/ppermute | solution.py:35
  49.4 37.1 %collective-permute-start.6 = (s16[2064,128]{1,0:T(8,128)(2,1)S(1)}, s16[2064,128]{1,0:T(8,128)(2,1)S(1)}, u32[]{:S(2)}, u32[]{:S(2)}) collective-permute-start(s16[2064,128]{1,0:T(8,128)(2,1)S(1)} %get-tuple-element.25), channel_id=1, source_target_pairs={{0,24},{8,0},{16,8},{24,16},{1,25},{9,1},{17,9},{25,17},{2,26},{10... | collective-permute-start | bytes 1585160 | tf_op jit(solution)/shard_map/ppermute | solution.py:35
  87.1 9.0 %collective-permute-start.10 = (s16[272,128]{1,0:T(8,128)(2,1)S(1)}, s16[272,128]{1,0:T(8,128)(2,1)S(1)}, u32[]{:S(2)}, u32[]{:S(2)}) collective-permute-start(s16[272,128]{1,0:T(8,128)(2,1)S(1)} %get-tuple-element.30), channel_id=1, source_target_pairs={{0,4},{1,5},{2,6},{3,7},{4,0},{5,1},{6,2},{7,3},{8,12},{9,13},{10,... | collective-permute-start | bytes 208904 | tf_op jit(solution)/shard_map/ppermute | solution.py:35
  91.0 12.2 %collective-permute-start.11 = (s16[272,128]{1,0:T(8,128)(2,1)S(1)}, s16[272,128]{1,0:T(8,128)(2,1)S(1)}, u32[]{:S(2)}, u32[]{:S(2)}) collective-permute-start(s16[272,128]{1,0:T(8,128)(2,1)S(1)} %get-tuple-element.31), channel_id=1, source_target_pairs={{0,5},{1,6},{2,7},{3,0},{4,1},{5,2},{6,3},{7,4},{8,13},{9,14},{10,... | collective-permute-start | bytes 208904 | tf_op jit(solution)/shard_map/ppermute | solution.py:35
  93.6 11.8 %collective-permute-start.12 = (s16[272,128]{1,0:T(8,128)(2,1)S(1)}, s16[272,128]{1,0:T(8,128)(2,1)S(1)}, u32[]{:S(2)}, u32[]{:S(2)}) collective-permute-start(s16[272,128]{1,0:T(8,128)(2,1)S(1)} %get-tuple-element.32), channel_id=1, source_target_pairs={{0,6},{1,7},{2,0},{3,1},{4,2},{5,3},{6,4},{7,5},{8,14},{9,15},{10,... | collective-permute-start | bytes 208904 | tf_op jit(solution)/shard_map/ppermute | solution.py:35
  94.1 11.4 %collective-permute-start.13 = (s16[272,128]{1,0:T(8,128)(2,1)S(1)}, s16[272,128]{1,0:T(8,128)(2,1)S(1)}, u32[]{:S(2)}, u32[]{:S(2)}) collective-permute-start(s16[272,128]{1,0:T(8,128)(2,1)S(1)} %get-tuple-element.33), channel_id=1, source_target_pairs={{0,7},{1,0},{2,1},{3,2},{4,3},{5,4},{6,5},{7,6},{8,15},{9,8},{10,9... | collective-permute-start | bytes 208904 | tf_op jit(solution)/shard_map/ppermute | solution.py:35
  96.0 9.5 %collective-permute-start.7 = (s16[272,128]{1,0:T(8,128)(2,1)S(1)}, s16[272,128]{1,0:T(8,128)(2,1)S(1)}, u32[]{:S(2)}, u32[]{:S(2)}) collective-permute-start(s16[272,128]{1,0:T(8,128)(2,1)S(1)} %get-tuple-element.27), channel_id=1, source_target_pairs={{0,1},{1,2},{2,3},{3,4},{4,5},{5,6},{6,7},{7,0},{8,9},{9,10},{10,1... | collective-permute-start | bytes 208904 | tf_op jit(solution)/shard_map/ppermute | solution.py:35
  96.1 9.4 %collective-permute-start.8 = (s16[272,128]{1,0:T(8,128)(2,1)S(1)}, s16[272,128]{1,0:T(8,128)(2,1)S(1)}, u32[]{:S(2)}, u32[]{:S(2)}) collective-permute-start(s16[272,128]{1,0:T(8,128)(2,1)S(1)} %get-tuple-element.28), channel_id=1, source_target_pairs={{0,2},{1,3},{2,4},{3,5},{4,6},{5,7},{6,0},{7,1},{8,10},{9,11},{10,... | collective-permute-start | bytes 208904 | tf_op jit(solution)/shard_map/ppermute | solution.py:35
  103.2 7.3 %collective-permute-start.9 = (s16[272,128]{1,0:T(8,128)(2,1)S(1)}, s16[272,128]{1,0:T(8,128)(2,1)S(1)}, u32[]{:S(2)}, u32[]{:S(2)}) collective-permute-start(s16[272,128]{1,0:T(8,128)(2,1)S(1)} %get-tuple-element.29), channel_id=1, source_target_pairs={{0,3},{1,4},{2,5},{3,6},{4,7},{5,0},{6,1},{7,2},{8,11},{9,12},{10,... | collective-permute-start | bytes 208904 | tf_op jit(solution)/shard_map/ppermute | solution.py:35

commit v2 on v1

--- a/solution.py
+++ b/solution.py
@@ -122,9 +122,8 @@
     exps_ref[pl.ds(row, 1), :] = exponent
 
 
-def product_kernel(gx, gy, groups, steps, row_ref, col_ref, work_ref, tiles, feats_ref, *refs):
-    x_refs, rest = refs[: gx // 2 - 1], refs[gx // 2 - 1 :]
-    own_ref, q_refs, (acc, held, made, exps) = rest[0], rest[1:groups], rest[groups:]
+def product_kernel(gx, gy, groups, steps, row_ref, col_ref, work_ref, tiles, feats_ref, swap_ref, *refs):
+    own_ref, q_refs, (acc, held, made, exps) = refs[0], refs[1:-4], refs[-4:]
     slots, order, _ = tiles.shape
     per_step = slots // steps
     vblocks = held.shape[0] // gx
@@ -132,10 +131,12 @@
     span = blocks // groups
     a, y = lax.axis_index("gx"), lax.axis_index("y")
     cores = 2
+    halves = vblocks
+    each = span // halves
 
     acc[...] = jnp.zeros_like(acc)
-    for k, f in enumerate((feats_ref, *x_refs)):
-        held[pl.ds(k * cores * vblocks, cores * vblocks)] = f[...]
+    for k, f in enumerate((feats_ref, swap_ref)):
+        held[pl.ds(k * f.shape[0], f.shape[0])] = f[...]
 
     pattern = lax.broadcasted_iota(jnp.int32, (order, order), 0) * order + lax.broadcasted_iota(
         jnp.int32, (order, order), 1
@@ -148,7 +149,7 @@
             home = lax.div(col, gy * vblocks)
             away = lax.rem(lax.div(a, cores) - lax.div(home, cores) + gx, gx // cores)
             side = lax.rem(a + home, cores)
-            place = (away * cores + side) * vblocks + lax.rem(col, vblocks)
+            place = (side * (gx // cores) + away) * vblocks + lax.rem(col, vblocks)
             masked = jnp.where(pattern < work_ref[tile], tiles[tile], jnp.zeros((), jnp.bfloat16))
             made[t] = jnp.dot(masked, held[place], preferred_element_type=jnp.float32)
             return carry
@@ -166,59 +167,55 @@
         own_ref[pl.ds(i * order, order), :] = acc[y * span + i]
         return carry
 
-    for k, q_ref in enumerate(q_refs, 1):
-        base = lax.rem(y + k, groups) * span
+    for n, q_ref in enumerate(q_refs):
+        base = lax.rem(y + 1 + n % (groups - 1), groups) * span + n // (groups - 1)
 
         def code(i, carry):
-            coded(acc[base + i], q_ref, exps, i * order, i)
+            coded(acc[base + i * halves], q_ref, exps, i * order, i)
             return carry
 
-        lax.fori_loop(0, span, code, 0, unroll=2)
-        q_ref[pl.ds(span * order, 16), :] = exps[...].astype(jnp.int32).astype(jnp.int16)
+        lax.fori_loop(0, each, code, 0, unroll=2)
+        q_ref[pl.ds(each * order, each), :] = exps[...].astype(jnp.int32).astype(jnp.int16)
     lax.fori_loop(0, span, own, 0)
 
 
 def scales_of(ref, at):
-    return jnp.exp2(ref[pl.ds(at, 16), :].astype(jnp.int32).astype(jnp.float32) - 15.0)
-
-
-def middle_kernel(order, groups, own_ref, *refs):
-    n = len(refs) - groups - 2
-    got, own_out, q_refs, scales, exps = refs[:n], refs[n], refs[n + 1 : n + groups], refs[-2], refs[-1]
-    rows = own_ref.shape[0]
-    span = rows // order // groups
+    exps = ref[pl.ds(at, ref.shape[0] - at), :].astype(jnp.int32).astype(jnp.float32)
+    return jnp.exp2(exps - 15.0)
+
+
+def middle_kernel(order, halves, half, own_ref, *refs):
+    got, own_out, q_refs, scales, exps = refs[:3], refs[3], refs[4:-2], refs[-2], refs[-1]
+    groups = len(q_refs) + 1
+    rows = groups * order
     z = lax.axis_index("z")
     exps[...] = jnp.zeros_like(exps)
     for n, g in enumerate(got):
-        scales[pl.ds(16 * n, 16), :] = scales_of(g, rows)
+        scales[pl.ds(groups * n, groups), :] = scales_of(g, rows)
 
     def total(block):
-        at = block * order
-        x = own_ref[pl.ds(at, order), :]
+        x = own_ref[pl.ds((block * halves + half) * order, order), :]
         for n, g in enumerate(got):
-            part = g[pl.ds(at, order), :].astype(jnp.int32).astype(jnp.float32)
-            x = x + part * scales[pl.ds(16 * n + block, 1), :]
+            part = g[pl.ds(block * order, order), :].astype(jnp.int32).astype(jnp.float32)
+            x = x + part * scales[pl.ds(groups * n + block, 1), :]
         return x
 
-    for i in range(span):
-        own_out[pl.ds(i * order, order), :] = total(z * span + i)
+    own_out[...] = total(z)
     for k, q_ref in enumerate(q_refs, 1):
-        base = lax.rem(z + k, groups) * span
-        for i in range(span):
-            coded(total(base + i), q_ref, exps, i * order, i)
-        q_ref[pl.ds(span * order, 16), :] = exps[...].astype(jnp.int32).astype(jnp.int16)
-
-
-def last_kernel(order, own_ref, *refs):
-    got, out_ref = refs[:-1], refs[-1]
-    rows = own_ref.shape[0]
-    for i in range(rows // order):
-        at = i * order
-        x = own_ref[pl.ds(at, order), :]
+        coded(total(lax.rem(z + k, groups)), q_ref, exps, 0, 0)
+        q_ref[pl.ds(order, exps.shape[0]), :] = exps[...].astype(jnp.int32).astype(jnp.int16)
+
+
+def last_kernel(order, halves, *refs):
+    out_ref = refs[-1]
+    each = (len(refs) - 1) // halves
+    for h in range(halves):
+        own, got = refs[h * each], refs[h * each + 1 : (h + 1) * each]
+        x = own[...]
         for g in got:
-            part = g[pl.ds(at, order), :].astype(jnp.int32).astype(jnp.float32)
-            x = x + part * scales_of(g, rows)[i : i + 1, :]
-        out_ref[pl.ds(at, order), :] = x
+            part = g[pl.ds(0, order), :].astype(jnp.int32).astype(jnp.float32)
+            x = x + part * scales_of(g, order)[0:1, :]
+        out_ref[pl.ds(h * order, order), :] = x
 
 
 def on_device(features, tile_vals, tile_row, tile_col, tile_work):
@@ -240,10 +237,12 @@
     )(*(in_hbm(t) for t in (tile_row, tile_col, tile_work)))
 
     cores = 2
-    mine = features.reshape(vblocks, order, width)
-    swap = lax.ppermute(mine, "gx", [(i, i ^ 1) for i in range(gx)])
+    mine = [features.reshape(vblocks, order, width)]
+    for k in range(1, gx // cores):
+        mine.append(lax.ppermute(mine[0], "gx", [(i, (i + cores * k) % gx) for i in range(gx)]))
     meta = lax.all_to_all(told, GY, split_axis=0, concat_axis=0, tiled=True)
-    both = jnp.concatenate([mine, swap])
+    feats = jnp.concatenate(mine)
+    swapped = lax.ppermute(feats, "gx", [(i, i ^ 1) for i in range(gx)])
     tiles = pl.pallas_call(
         stage_kernel,
         in_specs=[ANY],
@@ -253,10 +252,6 @@
         compiler_params=limit(4),
         name="stage",
     )(in_hbm(tile_vals))
-    around = []
-    for k in range(1, gx // cores):
-        around.append(lax.ppermute(both, "gx", [(i, (i + cores * k) % gx) for i in range(gx)]))
-
     small = jax.ShapeDtypeStruct((owned,), jnp.int32)
     sent, moved_row, moved_col, moved_work, kept = pl.pallas_call(
         lambda *refs: plan_kernel(peers, slots, *refs),
@@ -271,49 +266,52 @@
 
     steps = 8
     span = blocks // ny
+    halves = vblocks
     i16 = jnp.int16
     own, *coded_y = pl.pallas_call(
         lambda *refs: product_kernel(gx, peers, ny, steps, *refs),
-        in_specs=[SMEM] * 3 + [VMEM] * (1 + gx // cores),
-        out_specs=[VMEM] * ny,
+        in_specs=[SMEM] * 3 + [VMEM] * 3,
+        out_specs=[VMEM] * (1 + halves * (ny - 1)),
         out_shape=[vmem((span * order, width), jnp.float32)]
-        + [vmem((span * order + 16, width), i16)] * (ny - 1),
+        + [vmem((nz * order + nz, width), i16)] * (halves * (ny - 1)),
         scratch_shapes=[
             pltpu.VMEM((blocks, order, width), jnp.float32),
             pltpu.VMEM((gx * vblocks, order, width), jnp.bfloat16),
             pltpu.VMEM((slots // steps, order, width), jnp.float32),
-            pltpu.VMEM((span, width), jnp.float32),
+            pltpu.VMEM((nz, width), jnp.float32),
         ],
         compiler_params=limit(16),
         name="products",
-    )(tile_row, tile_col, tile_work, *(in_vmem(f) for f in (tiles, both, *around)))
-    got_y = []
-    for k, q in enumerate(coded_y, 1):
-        got_y.append(shifted(q, "y", k))
-
-    own, *coded_z = pl.pallas_call(
-        lambda *refs: middle_kernel(order, nz, *refs),
-        in_specs=[VMEM] * ny,
-        out_specs=[VMEM] * nz,
-        out_shape=[vmem((vblocks * order, width), jnp.float32)]
-        + [vmem((vblocks * order + 16, width), i16)] * (nz - 1),
-        scratch_shapes=[
-            pltpu.VMEM((16 * (ny - 1), width), jnp.float32),
-            pltpu.VMEM((16, width), jnp.float32),
-        ],
-        compiler_params=limit(8),
-        name="middle",
-    )(own, *(in_vmem(g) for g in got_y))
-    got_z = [shifted(q, "z", k) for k, q in enumerate(coded_z, 1)]
+    )(tile_row, tile_col, tile_work, *(in_vmem(f) for f in (tiles, feats, swapped)))
+
+    pieces = []
+    for h in range(halves):
+        got_y = []
+        for k in range(1, ny):
+            got_y.append(shifted(coded_y[h * (ny - 1) + k - 1], "y", k))
+        own_z, *coded_z = pl.pallas_call(
+            lambda *refs: middle_kernel(order, halves, h, *refs),
+            in_specs=[VMEM] * ny,
+            out_specs=[VMEM] * nz,
+            out_shape=[vmem((order, width), jnp.float32)] + [vmem((order + 8, width), i16)] * (nz - 1),
+            scratch_shapes=[
+                pltpu.VMEM((nz * (ny - 1), width), jnp.float32),
+                pltpu.VMEM((8, width), jnp.float32),
+            ],
+            compiler_params=limit(8),
+        )(in_vmem(own), *(in_vmem(g) for g in got_y))
+        pieces.append(own_z)
+        for k, q in enumerate(coded_z, 1):
+            pieces.append(shifted(q, "z", k))
 
     product = pl.pallas_call(
-        lambda *refs: last_kernel(order, *refs),
-        in_specs=[VMEM] * nz,
+        lambda *refs: last_kernel(order, halves, *refs),
+        in_specs=[VMEM] * len(pieces),
         out_specs=VMEM,
         out_shape=jax.ShapeDtypeStruct((vblocks * order, width), jnp.float32),
         compiler_params=limit(8),
         name="last",
-    )(own, *(in_vmem(g) for g in got_z))
+    )(*(in_vmem(g) for g in pieces))
 
     moved_vals = pl.pallas_call(
         lambda *refs: keep_kernel(owned, *refs),

time: 114 us -> 118 us (1.035); the launches traced: 114 us -> 116 us
  starting transfers between devices: 45.3 us -> 68 us
  waiting for transfers between devices: 54.2 us -> 33.3 us
    ppermute x10 -> x20, starting transfers between devices: 21.5 us -> 44.2 us  [shifted(): lax.ppermute(array, axis, [(i, (i + by) % size) for i in range(size)])]
    ppermute x10 -> x20, waiting for transfers between devices: 41.6 us -> 22.6 us  [shifted(): lax.ppermute(array, axis, [(i, (i + by) % size) for i in range(size)])]
    ppermute x4, waiting for transfers between devices: 6.15 us -> 4.35 us  [the longest x3 2.83 us: on_device(): lax.ppermute(mine[0], 'gx', [(i, (i + cores * k) % gx) for i in range(gx)])]
  transfers between devices with their start and end apart: 16 -> 26, of which waited for: 9 -> 11; matrix products, arithmetic and copies ran while one was open for 0% -> 0% of each run, Pallas kernels for 6% -> 5%
where the time goes in v2:
time: 118 us; the launch traced here: 116 us
  starting transfers between devices  68 us (58%)
  waiting for transfers between devices  33.3 us (28%)
  Pallas kernels  13.6 us (12%)
    ppermute x20, starting transfers between devices, shifted(): lax.ppermute(array, axis, [(i, (i + by) % size) for i in range(size)])  44.2 us
    ppermute x20, waiting for transfers between devices, shifted(): lax.ppermute(array, axis, [(i, (i + by) % size) for i in range(size)])  22.6 us
    all_to_all x1, starting transfers between devices, on_device(): meta = lax.all_to_all(told, GY, split_axis=0, concat_axis=0, tiled=True)  11.3 us
    all_to_all x1, starting transfers between devices, on_device(): got = lax.all_to_all(sent, GY, split_axis=0, concat_axis=0, tiled=True)  6.72 us
    all_to_all x1, waiting for transfers between devices, on_device(): meta = lax.all_to_all(told, GY, split_axis=0, concat_axis=0, tiled=True)  6.38 us
    ppermute x3, starting transfers between devices, on_device(): lax.ppermute(mine[0], 'gx', [(i, (i + cores * k) % gx) for i in range(gx)])  5.73 us
    pallas_call x1, Pallas kernels, on_device(): pl.pallas_call(lambda *refs: plan_kernel(peers, slots, *refs), in_specs=[...  3.36 us
    pallas_call x1, Pallas kernels, on_device(): pl.pallas_call(lambda *refs: product_kernel(gx, peers, ny, steps, *refs),...  3.29 us
  transfers between devices with their start and end apart: 26, of which 11 were waited for; matrix products, arithmetic and copies ran while one was open for 0% of the time, Pallas kernels for 5%

profile of v2, /device:TPU:40, one launch (start us, length us, event | category | flops | bytes accessed | tf_op | source)
XLA Modules:
  0.0 116.0 jit_solution(11747475541430809827)
XLA Ops:
  0.6 1.4 %tell.1 = s32[32,2,128]{2,1,0:T(2,128)} custom-call(s32[64]{0:T(128)} %refs_0_.3, s32[64]{0:T(128)} %refs_1_.3, s32[64]{0:T(128)} %refs_2_.3), custom_call_target="tpu_custom_call" | custom-call | tf_op jit(solution)/shard_map/tell/pallas_call | solution.py:229
  2.1 11.3 %all-to-all-start = ((s32[32,2,128]{2,1,0:T(2,128)}), s32[32,2,128]{2,1,0:T(2,128)S(1)}, u32[]{:S(2)}, u32[]{:S(2)}) async-start(s32[32,2,128]{2,1,0:T(2,128)} %tell.1), calls=%async_computation | async-start | bytes 65536 | tf_op jit(solution)/shard_map/all_to_all | solution.py:243
  13.3 1.6 %stage.1.refs_3_.refs_1_ = bf16[64,128,128]{2,1,0:T(8,128)(2,1)S(1)} custom-call(bf16[64,128,128]{2,1,0:T(8,128)(2,1)} %vals_ref.1), custom_call_target="tpu_custom_call" | custom-call | tf_op jit(solution)/shard_map/stage/pallas_call | solution.py:246
  14.9 6.4 %all-to-all-done.refs_0_ = s32[32,2,128]{2,1,0:T(2,128)S(1)} async-done(((s32[32,2,128]{2,1,0:T(2,128)}), s32[32,2,128]{2,1,0:T(2,128)S(1)}, u32[]{:S(2)}, u32[]{:S(2)}) %all-to-all-start) | async-done | bytes 32800 | tf_op jit(solution)/shard_map/all_to_all | solution.py:243
  21.3 3.4 %plan.1 = (bf16[64,128,128]{2,1,0:T(8,128)(2,1)}, s32[32]{0:T(128)}, s32[32]{0:T(128)}, s32[32]{0:T(128)}, s32[32]{0:T(128)S(1)}) custom-call(s32[32,2,128]{2,1,0:T(2,128)S(1)} %all-to-all-done.refs_0_, bf16[64,128,128]{2,1,0:T(8,128)(2,1)S(1)} %stage.1.refs_3_.refs_1_), custom_call_target="tpu_custom_call" | custom-call | tf_op jit(solution)/shard_map/plan/pallas_call | solution.py:256
  24.7 6.7 %all-to-all-start.1 = ((bf16[64,128,128]{2,1,0:T(8,128)(2,1)}), bf16[64,128,128]{2,1,0:T(8,128)(2,1)}, u32[]{:S(2)}, u32[]{:S(2)}) async-start(bf16[64,128,128]{2,1,0:T(8,128)(2,1)} %get-tuple-element.57), calls=%async_computation.1 | async-start | bytes 4194304 | tf_op jit(solution)/shard_map/all_to_all | solution.py:265
  31.5 1.6 %collective-permute-start = (bf16[2,128,128]{2,1,0:T(8,128)(2,1)S(1)}, bf16[2,128,128]{2,1,0:T(8,128)(2,1)S(1)}, u32[]{:S(2)}, u32[]{:S(2)}) collective-permute-start(bf16[2,128,128]{2,1,0:T(8,128)(2,1)S(1)} %bitcast.1), channel_id=1, source_target_pairs={{0,64},{32,96},{64,128},{96,160},{128,192},{160,224},{192,0},{224,... | collective-permute-start | bytes 196616 | tf_op jit(solution)/shard_map/ppermute | solution.py:242
  33.0 2.7 %collective-permute-start.1 = (bf16[2,128,128]{2,1,0:T(8,128)(2,1)S(1)}, bf16[2,128,128]{2,1,0:T(8,128)(2,1)S(1)}, u32[]{:S(2)}, u32[]{:S(2)}) collective-permute-start(bf16[2,128,128]{2,1,0:T(8,128)(2,1)S(1)} %bitcast.2), channel_id=1, source_target_pairs={{0,128},{32,160},{64,192},{96,224},{128,0},{160,32},{192,64},{224,... | collective-permute-start | bytes 196616 | tf_op jit(solution)/shard_map/ppermute | solution.py:242
  35.8 1.4 %collective-permute-start.2 = (bf16[2,128,128]{2,1,0:T(8,128)(2,1)S(1)}, bf16[2,128,128]{2,1,0:T(8,128)(2,1)S(1)}, u32[]{:S(2)}, u32[]{:S(2)}) collective-permute-start(bf16[2,128,128]{2,1,0:T(8,128)(2,1)S(1)} %bitcast.3), channel_id=1, source_target_pairs={{0,192},{32,224},{64,0},{96,32},{128,64},{160,96},{192,128},{224,1... | collective-permute-start | bytes 196616 | tf_op jit(solution)/shard_map/ppermute | solution.py:242
  37.2 1.6 %collective-permute-done.1 = bf16[2,128,128]{2,1,0:T(8,128)(2,1)S(1)} collective-permute-done((bf16[2,128,128]{2,1,0:T(8,128)(2,1)S(1)}, bf16[2,128,128]{2,1,0:T(8,128)(2,1)S(1)}, u32[]{:S(2)}, u32[]{:S(2)}) %collective-permute-start.1) | collective-permute-done | bytes 65568 | tf_op jit(solution)/shard_map/ppermute | solution.py:242
  38.8 1.2 %collective-permute-done.2 = bf16[2,128,128]{2,1,0:T(8,128)(2,1)S(1)} collective-permute-done((bf16[2,128,128]{2,1,0:T(8,128)(2,1)S(1)}, bf16[2,128,128]{2,1,0:T(8,128)(2,1)S(1)}, u32[]{:S(2)}, u32[]{:S(2)}) %collective-permute-start.2) | collective-permute-done | bytes 65568 | tf_op jit(solution)/shard_map/ppermute | solution.py:242
  40.2 1.5 %collective-permute-done.3.refs_5_ = bf16[8,128,128]{2,1,0:T(8,128)(2,1)S(1)} collective-permute-done((bf16[8,128,128]{2,1,0:T(8,128)(2,1)S(1)}, bf16[8,128,128]{2,1,0:T(8,128)(2,1)S(1)}, u32[]{:S(2)}, u32[]{:S(2)}) %collective-permute-start.3) | collective-permute-done | bytes 262176 | tf_op jit(solution)/shard_map/ppermute | solution.py:245
  41.7 3.3 %products.1 = (f32[2048,128]{1,0:T(8,128)S(1)}, s16[1032,128]{1,0:T(8,128)(2,1)S(1)}, s16[1032,128]{1,0:T(8,128)(2,1)S(1)}, s16[1032,128]{1,0:T(8,128)(2,1)S(1)}...) custom-call(s32[64]{0:T(128)S(1)} %copy-done, s32[64]{0:T(128)S(1)} %copy-done.1, ...), custom_call_target="tpu_custom_call" | custom-call | tf_op jit(solution)/shard_map/products/pallas_call | solution.py:271
  45.0 1.6 %collective-permute-start.14 = (s16[1032,128]{1,0:T(8,128)(2,1)S(1)}, s16[1032,128]{1,0:T(8,128)(2,1)S(1)}, u32[]{:S(2)}, u32[]{:S(2)}) collective-permute-start(s16[1032,128]{1,0:T(8,128)(2,1)S(1)} %get-tuple-element.45), channel_id=1, source_target_pairs={{0,8},{8,16},{16,24},{24,0},{1,9},{9,17},{17,25},{25,1},{2,10},{10... | collective-permute-start | bytes 792584 | tf_op jit(solution)/shard_map/ppermute | solution.py:35
  47.6 2.2 %collective-permute-start.16 = (s16[1032,128]{1,0:T(8,128)(2,1)S(1)}, s16[1032,128]{1,0:T(8,128)(2,1)S(1)}, u32[]{:S(2)}, u32[]{:S(2)}) collective-permute-start(s16[1032,128]{1,0:T(8,128)(2,1)S(1)} %get-tuple-element.47), channel_id=1, source_target_pairs={{0,24},{8,0},{16,8},{24,16},{1,25},{9,1},{17,9},{25,17},{2,26},{10... | collective-permute-start | bytes 792584 | tf_op jit(solution)/shard_map/ppermute | solution.py:35
  49.9 3.5 %collective-permute-start.5 = (s16[1032,128]{1,0:T(8,128)(2,1)S(1)}, s16[1032,128]{1,0:T(8,128)(2,1)S(1)}, u32[]{:S(2)}, u32[]{:S(2)}) collective-permute-start(s16[1032,128]{1,0:T(8,128)(2,1)S(1)} %get-tuple-element.35), channel_id=1, source_target_pairs={{0,16},{8,24},{16,0},{24,8},{1,17},{9,25},{17,1},{25,9},{2,18},{10... | collective-permute-start | bytes 792584 | tf_op jit(solution)/shard_map/ppermute | solution.py:35
  53.4 8.8 %collective-permute-done.14.refs_1_ = s16[1032,128]{1,0:T(8,128)(2,1)S(1)} collective-permute-done((s16[1032,128]{1,0:T(8,128)(2,1)S(1)}, s16[1032,128]{1,0:T(8,128)(2,1)S(1)}, u32[]{:S(2)}, u32[]{:S(2)}) %collective-permute-start.14) | collective-permute-done | bytes 264224 | tf_op jit(solution)/shard_map/ppermute | solution.py:35
  62.2 2.5 %collective-permute-start.6 = (s16[1032,128]{1,0:T(8,128)(2,1)S(1)}, s16[1032,128]{1,0:T(8,128)(2,1)S(1)}, u32[]{:S(2)}, u32[]{:S(2)}) collective-permute-start(s16[1032,128]{1,0:T(8,128)(2,1)S(1)} %get-tuple-element.36), channel_id=1, source_target_pairs={{0,24},{8,0},{16,8},{24,16},{1,25},{9,1},{17,9},{25,17},{2,26},{10... | collective-permute-start | bytes 792584 | tf_op jit(solution)/shard_map/ppermute | solution.py:35
  64.6 1.9 %collective-permute-done.15.refs_2_ = s16[1032,128]{1,0:T(8,128)(2,1)S(1)} collective-permute-done((s16[1032,128]{1,0:T(8,128)(2,1)S(1)}, s16[1032,128]{1,0:T(8,128)(2,1)S(1)}, u32[]{:S(2)}, u32[]{:S(2)}) %collective-permute-start.15) | collective-permute-done | bytes 264224 | tf_op jit(solution)/shard_map/ppermute | solution.py:35
  66.5 6.8 %collective-permute-done.16.refs_3_ = s16[1032,128]{1,0:T(8,128)(2,1)S(1)} collective-permute-done((s16[1032,128]{1,0:T(8,128)(2,1)S(1)}, s16[1032,128]{1,0:T(8,128)(2,1)S(1)}, u32[]{:S(2)}, u32[]{:S(2)}) %collective-permute-start.16) | collective-permute-done | bytes 264224 | tf_op jit(solution)/shard_map/ppermute | solution.py:35
  73.8 10.4 %collective-permute-start.18 = (s16[136,128]{1,0:T(8,128)(2,1)S(1)}, s16[136,128]{1,0:T(8,128)(2,1)S(1)}, u32[]{:S(2)}, u32[]{:S(2)}) collective-permute-start(s16[136,128]{1,0:T(8,128)(2,1)S(1)} %get-tuple-element.50), channel_id=1, source_target_pairs={{0,2},{1,3},{2,4},{3,5},{4,6},{5,7},{6,0},{7,1},{8,10},{9,11},{10,... | collective-permute-start | bytes 104456 | tf_op jit(solution)/shard_map/ppermute | solution.py:35
  84.5 6.1 %collective-permute-start.20 = (s16[136,128]{1,0:T(8,128)(2,1)S(1)}, s16[136,128]{1,0:T(8,128)(2,1)S(1)}, u32[]{:S(2)}, u32[]{:S(2)}) collective-permute-start(s16[136,128]{1,0:T(8,128)(2,1)S(1)} %get-tuple-element.52), channel_id=1, source_target_pairs={{0,4},{1,5},{2,6},{3,7},{4,0},{5,1},{6,2},{7,3},{8,12},{9,13},{10,... | collective-permute-start | bytes 104456 | tf_op jit(solution)/shard_map/ppermute | solution.py:35
  91.0 1.6 %collective-permute-start.22 = (s16[136,128]{1,0:T(8,128)(2,1)S(1)}, s16[136,128]{1,0:T(8,128)(2,1)S(1)}, u32[]{:S(2)}, u32[]{:S(2)}) collective-permute-start(s16[136,128]{1,0:T(8,128)(2,1)S(1)} %get-tuple-element.54), channel_id=1, source_target_pairs={{0,6},{1,7},{2,0},{3,1},{4,2},{5,3},{6,4},{7,5},{8,14},{9,15},{10,... | collective-permute-start | bytes 104456 | tf_op jit(solution)/shard_map/ppermute | solution.py:35
  92.6 3.0 %collective-permute-start.23 = (s16[136,128]{1,0:T(8,128)(2,1)S(1)}, s16[136,128]{1,0:T(8,128)(2,1)S(1)}, u32[]{:S(2)}, u32[]{:S(2)}) collective-permute-start(s16[136,128]{1,0:T(8,128)(2,1)S(1)} %get-tuple-element.55), channel_id=1, source_target_pairs={{0,7},{1,0},{2,1},{3,2},{4,3},{5,4},{6,5},{7,6},{8,15},{9,8},{10,9... | collective-permute-start | bytes 104456 | tf_op jit(solution)/shard_map/ppermute | solution.py:35
  95.6 2.1 %collective-permute-start.10 = (s16[136,128]{1,0:T(8,128)(2,1)S(1)}, s16[136,128]{1,0:T(8,128)(2,1)S(1)}, u32[]{:S(2)}, u32[]{:S(2)}) collective-permute-start(s16[136,128]{1,0:T(8,128)(2,1)S(1)} %get-tuple-element.41), channel_id=1, source_target_pairs={{0,4},{1,5},{2,6},{3,7},{4,0},{5,1},{6,2},{7,3},{8,12},{9,13},{10,... | collective-permute-start | bytes 104456 | tf_op jit(solution)/shard_map/ppermute | solution.py:35
  97.6 1.5 %collective-permute-start.11 = (s16[136,128]{1,0:T(8,128)(2,1)S(1)}, s16[136,128]{1,0:T(8,128)(2,1)S(1)}, u32[]{:S(2)}, u32[]{:S(2)}) collective-permute-start(s16[136,128]{1,0:T(8,128)(2,1)S(1)} %get-tuple-element.42), channel_id=1, source_target_pairs={{0,5},{1,6},{2,7},{3,0},{4,1},{5,2},{6,3},{7,4},{8,13},{9,14},{10,... | collective-permute-start | bytes 104456 | tf_op jit(solution)/shard_map/ppermute | solution.py:35
  99.3 3.3 %collective-permute-start.12 = (s16[136,128]{1,0:T(8,128)(2,1)S(1)}, s16[136,128]{1,0:T(8,128)(2,1)S(1)}, u32[]{:S(2)}, u32[]{:S(2)}) collective-permute-start(s16[136,128]{1,0:T(8,128)(2,1)S(1)} %get-tuple-element.43), channel_id=1, source_target_pairs={{0,6},{1,7},{2,0},{3,1},{4,2},{5,3},{6,4},{7,5},{8,14},{9,15},{10,... | collective-permute-start | bytes 104456 | tf_op jit(solution)/shard_map/ppermute | solution.py:35
  102.7 1.9 %collective-permute-start.13 = (s16[136,128]{1,0:T(8,128)(2,1)S(1)}, s16[136,128]{1,0:T(8,128)(2,1)S(1)}, u32[]{:S(2)}, u32[]{:S(2)}) collective-permute-start(s16[136,128]{1,0:T(8,128)(2,1)S(1)} %get-tuple-element.44), channel_id=1, source_target_pairs={{0,7},{1,0},{2,1},{3,2},{4,3},{5,4},{6,5},{7,6},{8,15},{9,8},{10,9... | collective-permute-start | bytes 104456 | tf_op jit(solution)/shard_map/ppermute | solution.py:35
  105.5 2.1 %collective-permute-start.9 = (s16[136,128]{1,0:T(8,128)(2,1)S(1)}, s16[136,128]{1,0:T(8,128)(2,1)S(1)}, u32[]{:S(2)}, u32[]{:S(2)}) collective-permute-start(s16[136,128]{1,0:T(8,128)(2,1)S(1)} %get-tuple-element.40), channel_id=1, source_target_pairs={{0,3},{1,4},{2,5},{3,6},{4,7},{5,0},{6,1},{7,2},{8,11},{9,12},{10,... | collective-permute-start | bytes 104456 | tf_op jit(solution)/shard_map/ppermute | solution.py:35
  108.6 2.2 %collective-permute-done.8.refs_2_ = s16[136,128]{1,0:T(8,128)(2,1)S(1)} collective-permute-done((s16[136,128]{1,0:T(8,128)(2,1)S(1)}, s16[136,128]{1,0:T(8,128)(2,1)S(1)}, u32[]{:S(2)}, u32[]{:S(2)}) %collective-permute-start.8) | collective-permute-done | bytes 34848 | tf_op jit(solution)/shard_map/ppermute | solution.py:35
  110.8 1.7 %collective-permute-done.9.refs_3_ = s16[136,128]{1,0:T(8,128)(2,1)S(1)} collective-permute-done((s16[136,128]{1,0:T(8,128)(2,1)S(1)}, s16[136,128]{1,0:T(8,128)(2,1)S(1)}, u32[]{:S(2)}, u32[]{:S(2)}) %collective-permute-start.9) | collective-permute-done | bytes 34848 | tf_op jit(solution)/shard_map/ppermute | solution.py:35
  113.3 2.6 %keep.1 = bf16[32,128,128]{2,1,0:T(8,128)(2,1)} custom-call(s32[32]{0:T(128)S(1)} %get-tuple-element.56.refs_0_, bf16[64,128,128]{2,1,0:T(8,128)(2,1)} %all-to-all-done.1.refs_1_), custom_call_target="tpu_custom_call" | custom-call | tf_op jit(solution)/shard_map/keep/pallas_call | solution.py:316
  (37 shorter events, 5.2 us)
Async XLA Ops:
  2.1 19.2 %all-to-all-start = ((s32[32,2,128]{2,1,0:T(2,128)}), s32[32,2,128]{2,1,0:T(2,128)S(1)}, u32[]{:S(2)}, u32[]{:S(2)}) async-start(s32[32,2,128]{2,1,0:T(2,128)} %tell.1), calls=%async_computation | async-start | bytes 65536 | tf_op jit(solution)/shard_map/all_to_all | solution.py:243
  24.7 6.8 %copy-start.3 = (bf16[256,128]{1,0:T(8,128)(2,1)S(1)}, bf16[256,128]{1,0:T(8,128)(2,1)}, u32[]{:S(2)}) copy-start(bf16[256,128]{1,0:T(8,128)(2,1)} %param.5) | copy-start | bytes 196612
  24.7 17.0 %copy-start = (s32[64]{0:T(128)S(1)}, s32[64]{0:T(128)}, u32[]{:S(2)}) copy-start(s32[64]{0:T(128)} %refs_0_.3) | copy-start | bytes 772
  24.7 17.0 %copy-start.1 = (s32[64]{0:T(128)S(1)}, s32[64]{0:T(128)}, u32[]{:S(2)}) copy-start(s32[64]{0:T(128)} %refs_1_.3) | copy-start | bytes 772
  24.7 17.0 %copy-start.2 = (s32[64]{0:T(128)S(1)}, s32[64]{0:T(128)}, u32[]{:S(2)}) copy-start(s32[64]{0:T(128)} %refs_2_.3) | copy-start | bytes 772
  24.7 88.6 %all-to-all-start.1 = ((bf16[64,128,128]{2,1,0:T(8,128)(2,1)}), bf16[64,128,128]{2,1,0:T(8,128)(2,1)}, u32[]{:S(2)}, u32[]{:S(2)}) async-start(bf16[64,128,128]{2,1,0:T(8,128)(2,1)} %get-tuple-element.57), calls=%async_computation.1 | async-start | bytes 4194304 | tf_op jit(solution)/shard_map/all_to_all | solution.py:265
  31.5 5.7 %collective-permute-start = (bf16[2,128,128]{2,1,0:T(8,128)(2,1)S(1)}, bf16[2,128,128]{2,1,0:T(8,128)(2,1)S(1)}, u32[]{:S(2)}, u32[]{:S(2)}) collective-permute-start(bf16[2,128,128]{2,1,0:T(8,128)(2,1)S(1)} %bitcast.1), channel_id=1, source_target_pairs={{0,64},{32,96},{64,128},{96,160},{128,192},{160,224},{192,0},{224,... | collective-permute-start | bytes 196616 | tf_op jit(solution)/shard_map/ppermute | solution.py:242
  33.0 5.8 %collective-permute-start.1 = (bf16[2,128,128]{2,1,0:T(8,128)(2,1)S(1)}, bf16[2,128,128]{2,1,0:T(8,128)(2,1)S(1)}, u32[]{:S(2)}, u32[]{:S(2)}) collective-permute-start(bf16[2,128,128]{2,1,0:T(8,128)(2,1)S(1)} %bitcast.2), channel_id=1, source_target_pairs={{0,128},{32,160},{64,192},{96,224},{128,0},{160,32},{192,64},{224,... | collective-permute-start | bytes 196616 | tf_op jit(solution)/shard_map/ppermute | solution.py:242
  35.8 4.3 %collective-permute-start.2 = (bf16[2,128,128]{2,1,0:T(8,128)(2,1)S(1)}, bf16[2,128,128]{2,1,0:T(8,128)(2,1)S(1)}, u32[]{:S(2)}, u32[]{:S(2)}) collective-permute-start(bf16[2,128,128]{2,1,0:T(8,128)(2,1)S(1)} %bitcast.3), channel_id=1, source_target_pairs={{0,192},{32,224},{64,0},{96,32},{128,64},{160,96},{192,128},{224,1... | collective-permute-start | bytes 196616 | tf_op jit(solution)/shard_map/ppermute | solution.py:242
  40.1 1.6 %collective-permute-start.3 = (bf16[8,128,128]{2,1,0:T(8,128)(2,1)S(1)}, bf16[8,128,128]{2,1,0:T(8,128)(2,1)S(1)}, u32[]{:S(2)}, u32[]{:S(2)}) collective-permute-start(bf16[8,128,128]{2,1,0:T(8,128)(2,1)S(1)} %pad_maximum_fusion.refs_4_), channel_id=1, source_target_pairs={{0,32},{32,0},{64,96},{96,64},{128,160},{160,128},{192,224},{224,1... | collective-permute-start | bytes 786440 | tf_op jit(solution)/shard_map/ppermute | solution.py:245
  45.0 17.2 %collective-permute-start.14 = (s16[1032,128]{1,0:T(8,128)(2,1)S(1)}, s16[1032,128]{1,0:T(8,128)(2,1)S(1)}, u32[]{:S(2)}, u32[]{:S(2)}) collective-permute-start(s16[1032,128]{1,0:T(8,128)(2,1)S(1)} %get-tuple-element.45), channel_id=1, source_target_pairs={{0,8},{8,16},{16,24},{24,0},{1,9},{9,17},{17,25},{25,1},{2,10},{10... | collective-permute-start | bytes 792584 | tf_op jit(solution)/shard_map/ppermute | solution.py:35
  46.6 19.9 %collective-permute-start.15 = (s16[1032,128]{1,0:T(8,128)(2,1)S(1)}, s16[1032,128]{1,0:T(8,128)(2,1)S(1)}, u32[]{:S(2)}, u32[]{:S(2)}) collective-permute-start(s16[1032,128]{1,0:T(8,128)(2,1)S(1)} %get-tuple-element.46), channel_id=1, source_target_pairs={{0,16},{8,24},{16,0},{24,8},{1,17},{9,25},{17,1},{25,9},{2,18},{10... | collective-permute-start | bytes 792584 | tf_op jit(solution)/shard_map/ppermute | solution.py:35
  47.6 25.7 %collective-permute-start.16 = (s16[1032,128]{1,0:T(8,128)(2,1)S(1)}, s16[1032,128]{1,0:T(8,128)(2,1)S(1)}, u32[]{:S(2)}, u32[]{:S(2)}) collective-permute-start(s16[1032,128]{1,0:T(8,128)(2,1)S(1)} %get-tuple-element.47), channel_id=1, source_target_pairs={{0,24},{8,0},{16,8},{24,16},{1,25},{9,1},{17,9},{25,17},{2,26},{10... | collective-permute-start | bytes 792584 | tf_op jit(solution)/shard_map/ppermute | solution.py:35
  49.9 34.3 %collective-permute-start.4 = (s16[1032,128]{1,0:T(8,128)(2,1)S(1)}, s16[1032,128]{1,0:T(8,128)(2,1)S(1)}, u32[]{:S(2)}, u32[]{:S(2)}) collective-permute-start(s16[1032,128]{1,0:T(8,128)(2,1)S(1)} %get-tuple-element.34), channel_id=1, source_target_pairs={{0,8},{8,16},{16,24},{24,0},{1,9},{9,17},{17,25},{25,1},{2,10},{10... | collective-permute-start | bytes 792584 | tf_op jit(solution)/shard_map/ppermute | solution.py:35
  49.9 34.6 %collective-permute-start.5 = (s16[1032,128]{1,0:T(8,128)(2,1)S(1)}, s16[1032,128]{1,0:T(8,128)(2,1)S(1)}, u32[]{:S(2)}, u32[]{:S(2)}) collective-permute-start(s16[1032,128]{1,0:T(8,128)(2,1)S(1)} %get-tuple-element.35), channel_id=1, source_target_pairs={{0,16},{8,24},{16,0},{24,8},{1,17},{9,25},{17,1},{25,9},{2,18},{10... | collective-permute-start | bytes 792584 | tf_op jit(solution)/shard_map/ppermute | solution.py:35
  62.2 28.5 %collective-permute-start.6 = (s16[1032,128]{1,0:T(8,128)(2,1)S(1)}, s16[1032,128]{1,0:T(8,128)(2,1)S(1)}, u32[]{:S(2)}, u32[]{:S(2)}) collective-permute-start(s16[1032,128]{1,0:T(8,128)(2,1)S(1)} %get-tuple-element.36), channel_id=1, source_target_pairs={{0,24},{8,0},{16,8},{24,16},{1,25},{9,1},{17,9},{25,17},{2,26},{10... | collective-permute-start | bytes 792584 | tf_op jit(solution)/shard_map/ppermute | solution.py:35
  73.7 17.3 %collective-permute-start.17 = (s16[136,128]{1,0:T(8,128)(2,1)S(1)}, s16[136,128]{1,0:T(8,128)(2,1)S(1)}, u32[]{:S(2)}, u32[]{:S(2)}) collective-permute-start(s16[136,128]{1,0:T(8,128)(2,1)S(1)} %get-tuple-element.49), channel_id=1, source_target_pairs={{0,1},{1,2},{2,3},{3,4},{4,5},{5,6},{6,7},{7,0},{8,9},{9,10},{10,1... | collective-permute-start | bytes 104456 | tf_op jit(solution)/shard_map/ppermute | solution.py:35
  73.8 18.7 %collective-permute-start.18 = (s16[136,128]{1,0:T(8,128)(2,1)S(1)}, s16[136,128]{1,0:T(8,128)(2,1)S(1)}, u32[]{:S(2)}, u32[]{:S(2)}) collective-permute-start(s16[136,128]{1,0:T(8,128)(2,1)S(1)} %get-tuple-element.50), channel_id=1, source_target_pairs={{0,2},{1,3},{2,4},{3,5},{4,6},{5,7},{6,0},{7,1},{8,10},{9,11},{10,... | collective-permute-start | bytes 104456 | tf_op jit(solution)/shard_map/ppermute | solution.py:35
  84.2 11.3 %collective-permute-start.19 = (s16[136,128]{1,0:T(8,128)(2,1)S(1)}, s16[136,128]{1,0:T(8,128)(2,1)S(1)}, u32[]{:S(2)}, u32[]{:S(2)}) collective-permute-start(s16[136,128]{1,0:T(8,128)(2,1)S(1)} %get-tuple-element.51), channel_id=1, source_target_pairs={{0,3},{1,4},{2,5},{3,6},{4,7},{5,0},{6,1},{7,2},{8,11},{9,12},{10,... | collective-permute-start | bytes 104456 | tf_op jit(solution)/shard_map/ppermute | solution.py:35
  84.5 13.2 %collective-permute-start.20 = (s16[136,128]{1,0:T(8,128)(2,1)S(1)}, s16[136,128]{1,0:T(8,128)(2,1)S(1)}, u32[]{:S(2)}, u32[]{:S(2)}) collective-permute-start(s16[136,128]{1,0:T(8,128)(2,1)S(1)} %get-tuple-element.52), channel_id=1, source_target_pairs={{0,4},{1,5},{2,6},{3,7},{4,0},{5,1},{6,2},{7,3},{8,12},{9,13},{10,... | collective-permute-start | bytes 104456 | tf_op jit(solution)/shard_map/ppermute | solution.py:35
  90.6 8.7 %collective-permute-start.21 = (s16[136,128]{1,0:T(8,128)(2,1)S(1)}, s16[136,128]{1,0:T(8,128)(2,1)S(1)}, u32[]{:S(2)}, u32[]{:S(2)}) collective-permute-start(s16[136,128]{1,0:T(8,128)(2,1)S(1)} %get-tuple-element.53), channel_id=1, source_target_pairs={{0,5},{1,6},{2,7},{3,0},{4,1},{5,2},{6,3},{7,4},{8,13},{9,14},{10,... | collective-permute-start | bytes 104456 | tf_op jit(solution)/shard_map/ppermute | solution.py:35
  91.0 11.7 %collective-permute-start.22 = (s16[136,128]{1,0:T(8,128)(2,1)S(1)}, s16[136,128]{1,0:T(8,128)(2,1)S(1)}, u32[]{:S(2)}, u32[]{:S(2)}) collective-permute-start(s16[136,128]{1,0:T(8,128)(2,1)S(1)} %get-tuple-element.54), channel_id=1, source_target_pairs={{0,6},{1,7},{2,0},{3,1},{4,2},{5,3},{6,4},{7,5},{8,14},{9,15},{10,... | collective-permute-start | bytes 104456 | tf_op jit(solution)/shard_map/ppermute | solution.py:35
  92.6 12.0 %collective-permute-start.23 = (s16[136,128]{1,0:T(8,128)(2,1)S(1)}, s16[136,128]{1,0:T(8,128)(2,1)S(1)}, u32[]{:S(2)}, u32[]{:S(2)}) collective-permute-start(s16[136,128]{1,0:T(8,128)(2,1)S(1)} %get-tuple-element.55), channel_id=1, source_target_pairs={{0,7},{1,0},{2,1},{3,2},{4,3},{5,4},{6,5},{7,6},{8,15},{9,8},{10,9... | collective-permute-start | bytes 104456 | tf_op jit(solution)/shard_map/ppermute | solution.py:35
  95.6 9.2 %collective-permute-start.10 = (s16[136,128]{1,0:T(8,128)(2,1)S(1)}, s16[136,128]{1,0:T(8,128)(2,1)S(1)}, u32[]{:S(2)}, u32[]{:S(2)}) collective-permute-start(s16[136,128]{1,0:T(8,128)(2,1)S(1)} %get-tuple-element.41), channel_id=1, source_target_pairs={{0,4},{1,5},{2,6},{3,7},{4,0},{5,1},{6,2},{7,3},{8,12},{9,13},{10,... | collective-permute-start | bytes 104456 | tf_op jit(solution)/shard_map/ppermute | solution.py:35
  97.6 7.9 %collective-permute-start.11 = (s16[136,128]{1,0:T(8,128)(2,1)S(1)}, s16[136,128]{1,0:T(8,128)(2,1)S(1)}, u32[]{:S(2)}, u32[]{:S(2)}) collective-permute-start(s16[136,128]{1,0:T(8,128)(2,1)S(1)} %get-tuple-element.42), channel_id=1, source_target_pairs={{0,5},{1,6},{2,7},{3,0},{4,1},{5,2},{6,3},{7,4},{8,13},{9,14},{10,... | collective-permute-start | bytes 104456 | tf_op jit(solution)/shard_map/ppermute | solution.py:35
  99.3 8.3 %collective-permute-start.12 = (s16[136,128]{1,0:T(8,128)(2,1)S(1)}, s16[136,128]{1,0:T(8,128)(2,1)S(1)}, u32[]{:S(2)}, u32[]{:S(2)}) collective-permute-start(s16[136,128]{1,0:T(8,128)(2,1)S(1)} %get-tuple-element.43), channel_id=1, source_target_pairs={{0,6},{1,7},{2,0},{3,1},{4,2},{5,3},{6,4},{7,5},{8,14},{9,15},{10,... | collective-permute-start | bytes 104456 | tf_op jit(solution)/shard_map/ppermute | solution.py:35
  102.7 5.0 %collective-permute-start.13 = (s16[136,128]{1,0:T(8,128)(2,1)S(1)}, s16[136,128]{1,0:T(8,128)(2,1)S(1)}, u32[]{:S(2)}, u32[]{:S(2)}) collective-permute-start(s16[136,128]{1,0:T(8,128)(2,1)S(1)} %get-tuple-element.44), channel_id=1, source_target_pairs={{0,7},{1,0},{2,1},{3,2},{4,3},{5,4},{6,5},{7,6},{8,15},{9,8},{10,9... | collective-permute-start | bytes 104456 | tf_op jit(solution)/shard_map/ppermute | solution.py:35
  104.6 3.9 %collective-permute-start.7 = (s16[136,128]{1,0:T(8,128)(2,1)S(1)}, s16[136,128]{1,0:T(8,128)(2,1)S(1)}, u32[]{:S(2)}, u32[]{:S(2)}) collective-permute-start(s16[136,128]{1,0:T(8,128)(2,1)S(1)} %get-tuple-element.38), channel_id=1, source_target_pairs={{0,1},{1,2},{2,3},{3,4},{4,5},{5,6},{6,7},{7,0},{8,9},{9,10},{10,1... | collective-permute-start | bytes 104456 | tf_op jit(solution)/shard_map/ppermute | solution.py:35
  104.7 6.1 %collective-permute-start.8 = (s16[136,128]{1,0:T(8,128)(2,1)S(1)}, s16[136,128]{1,0:T(8,128)(2,1)S(1)}, u32[]{:S(2)}, u32[]{:S(2)}) collective-permute-start(s16[136,128]{1,0:T(8,128)(2,1)S(1)} %get-tuple-element.39), channel_id=1, source_target_pairs={{0,2},{1,3},{2,4},{3,5},{4,6},{5,7},{6,0},{7,1},{8,10},{9,11},{10,... | collective-permute-start | bytes 104456 | tf_op jit(solution)/shard_map/ppermute | solution.py:35
  105.5 7.0 %collective-permute-start.9 = (s16[136,128]{1,0:T(8,128)(2,1)S(1)}, s16[136,128]{1,0:T(8,128)(2,1)S(1)}, u32[]{:S(2)}, u32[]{:S(2)}) collective-permute-start(s16[136,128]{1,0:T(8,128)(2,1)S(1)} %get-tuple-element.40), channel_id=1, source_target_pairs={{0,3},{1,4},{2,5},{3,6},{4,7},{5,0},{6,1},{7,2},{8,11},{9,12},{10,... | collective-permute-start | bytes 104456 | tf_op jit(solution)/shard_map/ppermute | solution.py:35

commit v3 on v1

--- a/solution.py
+++ b/solution.py
@@ -122,9 +122,8 @@
     exps_ref[pl.ds(row, 1), :] = exponent
 
 
-def product_kernel(gx, gy, groups, steps, row_ref, col_ref, work_ref, tiles, feats_ref, *refs):
-    x_refs, rest = refs[: gx // 2 - 1], refs[gx // 2 - 1 :]
-    own_ref, q_refs, (acc, held, made, exps) = rest[0], rest[1:groups], rest[groups:]
+def product_kernel(gx, gy, groups, steps, row_ref, col_ref, work_ref, tiles, feats_ref, swap_ref, *refs):
+    own_ref, q_refs, (acc, held, made, exps) = refs[0], refs[1:-4], refs[-4:]
     slots, order, _ = tiles.shape
     per_step = slots // steps
     vblocks = held.shape[0] // gx
@@ -134,8 +133,8 @@
     cores = 2
 
     acc[...] = jnp.zeros_like(acc)
-    for k, f in enumerate((feats_ref, *x_refs)):
-        held[pl.ds(k * cores * vblocks, cores * vblocks)] = f[...]
+    for k, f in enumerate((feats_ref, swap_ref)):
+        held[pl.ds(k * f.shape[0], f.shape[0])] = f[...]
 
     pattern = lax.broadcasted_iota(jnp.int32, (order, order), 0) * order + lax.broadcasted_iota(
         jnp.int32, (order, order), 1
@@ -148,7 +147,7 @@
             home = lax.div(col, gy * vblocks)
             away = lax.rem(lax.div(a, cores) - lax.div(home, cores) + gx, gx // cores)
             side = lax.rem(a + home, cores)
-            place = (away * cores + side) * vblocks + lax.rem(col, vblocks)
+            place = (side * (gx // cores) + away) * vblocks + lax.rem(col, vblocks)
             masked = jnp.where(pattern < work_ref[tile], tiles[tile], jnp.zeros((), jnp.bfloat16))
             made[t] = jnp.dot(masked, held[place], preferred_element_type=jnp.float32)
             return carry
@@ -174,51 +173,73 @@
             return carry
 
         lax.fori_loop(0, span, code, 0, unroll=2)
-        q_ref[pl.ds(span * order, 16), :] = exps[...].astype(jnp.int32).astype(jnp.int16)
+        q_ref[pl.ds(span * order, span), :] = exps[...].astype(jnp.int32).astype(jnp.int16)
     lax.fori_loop(0, span, own, 0)
 
 
 def scales_of(ref, at):
-    return jnp.exp2(ref[pl.ds(at, 16), :].astype(jnp.int32).astype(jnp.float32) - 15.0)
-
-
-def middle_kernel(order, groups, own_ref, *refs):
-    n = len(refs) - groups - 2
-    got, own_out, q_refs, scales, exps = refs[:n], refs[n], refs[n + 1 : n + groups], refs[-2], refs[-1]
-    rows = own_ref.shape[0]
-    span = rows // order // groups
+    exps = ref[pl.ds(at, ref.shape[0] - at), :].astype(jnp.int32).astype(jnp.float32)
+    return jnp.exp2(exps - 15.0)
+
+
+def part_of(ref, i, order, count):
+    x = ref[pl.ds(i * order, order), :].astype(jnp.int32).astype(jnp.float32)
+    return x * scales_of(ref, count * order)[i : i + 1, :]
+
+
+def store_exps(q_ref, exps, count, order):
+    q_ref[pl.ds(count * order, exps.shape[0]), :] = exps[...].astype(jnp.int32).astype(jnp.int16)
+
+
+def middle_kernel(order, vblocks, own_ref, *refs):
+    got, part_ref, q_refs, scales, exps = refs[:-5], refs[-5], refs[-4:-2], refs[-2], refs[-1]
+    blocks = part_ref.shape[0] // order
+    owners = blocks // vblocks
     z = lax.axis_index("z")
     exps[...] = jnp.zeros_like(exps)
     for n, g in enumerate(got):
-        scales[pl.ds(16 * n, 16), :] = scales_of(g, rows)
-
-    def total(block):
+        scales[pl.ds(blocks * n, blocks), :] = scales_of(g, blocks * order)
+
+    def add(block, carry):
         at = block * order
         x = own_ref[pl.ds(at, order), :]
         for n, g in enumerate(got):
             part = g[pl.ds(at, order), :].astype(jnp.int32).astype(jnp.float32)
-            x = x + part * scales[pl.ds(16 * n + block, 1), :]
-        return x
-
-    for i in range(span):
-        own_out[pl.ds(i * order, order), :] = total(z * span + i)
-    for k, q_ref in enumerate(q_refs, 1):
-        base = lax.rem(z + k, groups) * span
-        for i in range(span):
-            coded(total(base + i), q_ref, exps, i * order, i)
-        q_ref[pl.ds(span * order, 16), :] = exps[...].astype(jnp.int32).astype(jnp.int16)
-
-
-def last_kernel(order, own_ref, *refs):
-    got, out_ref = refs[:-1], refs[-1]
-    rows = own_ref.shape[0]
-    for i in range(rows // order):
-        at = i * order
-        x = own_ref[pl.ds(at, order), :]
-        for g in got:
-            part = g[pl.ds(at, order), :].astype(jnp.int32).astype(jnp.float32)
-            x = x + part * scales_of(g, rows)[i : i + 1, :]
-        out_ref[pl.ds(at, order), :] = x
+            x = x + part * scales[pl.ds(blocks * n + block, 1), :]
+        part_ref[pl.ds(at, order), :] = x
+        return carry
+
+    lax.fori_loop(0, blocks, add, 0, unroll=2)
+    far = lax.rem(z + owners // 2, owners) * vblocks
+    for v, q_ref in enumerate(q_refs):
+        coded(part_ref[pl.ds((far + v) * order, order), :], q_ref, exps, 0, 0)
+        store_exps(q_ref, exps, 1, order)
+
+
+def ring_kernel(order, vblocks, away, first, part_ref, right_ref, left_ref, to_right, to_left, exps):
+    owners = part_ref.shape[0] // order // vblocks
+    z = lax.axis_index("z")
+    exps[...] = jnp.zeros_like(exps)
+    ways = ((right_ref, to_right, away, 0), (left_ref, to_left, owners - away, 1))
+    for got, q_ref, by, side in ways:
+        base = lax.rem(z + by, owners) * vblocks
+        for v in range(vblocks):
+            x = part_ref[pl.ds((base + v) * order, order), :]
+            if not first:
+                x = x + part_of(got, v, order, vblocks)
+            elif v == side:
+                x = x + part_of(got, 0, order, 1)
+            coded(x, q_ref, exps, v * order, v)
+        store_exps(q_ref, exps, vblocks, order)
+
+
+def last_kernel(order, vblocks, part_ref, right_ref, left_ref, out_ref):
+    base = lax.axis_index("z") * vblocks
+    for v in range(vblocks):
+        x = part_ref[pl.ds((base + v) * order, order), :]
+        for got in (right_ref, left_ref):
+            x = x + part_of(got, v, order, vblocks)
+        out_ref[pl.ds(v * order, order), :] = x
 
 
 def on_device(features, tile_vals, tile_row, tile_col, tile_work):
@@ -240,10 +261,12 @@
     )(*(in_hbm(t) for t in (tile_row, tile_col, tile_work)))
 
     cores = 2
-    mine = features.reshape(vblocks, order, width)
-    swap = lax.ppermute(mine, "gx", [(i, i ^ 1) for i in range(gx)])
+    mine = [features.reshape(vblocks, order, width)]
+    for k in range(1, gx // cores):
+        mine.append(lax.ppermute(mine[0], "gx", [(i, (i + cores * k) % gx) for i in range(gx)]))
     meta = lax.all_to_all(told, GY, split_axis=0, concat_axis=0, tiled=True)
-    both = jnp.concatenate([mine, swap])
+    feats = jnp.concatenate(mine)
+    swapped = lax.ppermute(feats, "gx", [(i, i ^ 1) for i in range(gx)])
     tiles = pl.pallas_call(
         stage_kernel,
         in_specs=[ANY],
@@ -253,10 +276,6 @@
         compiler_params=limit(4),
         name="stage",
     )(in_hbm(tile_vals))
-    around = []
-    for k in range(1, gx // cores):
-        around.append(lax.ppermute(both, "gx", [(i, (i + cores * k) % gx) for i in range(gx)]))
-
     small = jax.ShapeDtypeStruct((owned,), jnp.int32)
     sent, moved_row, moved_col, moved_work, kept = pl.pallas_call(
         lambda *refs: plan_kernel(peers, slots, *refs),
@@ -274,10 +293,10 @@
     i16 = jnp.int16
     own, *coded_y = pl.pallas_call(
         lambda *refs: product_kernel(gx, peers, ny, steps, *refs),
-        in_specs=[SMEM] * 3 + [VMEM] * (1 + gx // cores),
+        in_specs=[SMEM] * 3 + [VMEM] * 3,
         out_specs=[VMEM] * ny,
         out_shape=[vmem((span * order, width), jnp.float32)]
-        + [vmem((span * order + 16, width), i16)] * (ny - 1),
+        + [vmem((span * order + span, width), i16)] * (ny - 1),
         scratch_shapes=[
             pltpu.VMEM((blocks, order, width), jnp.float32),
             pltpu.VMEM((gx * vblocks, order, width), jnp.bfloat16),
@@ -286,34 +305,43 @@
         ],
         compiler_params=limit(16),
         name="products",
-    )(tile_row, tile_col, tile_work, *(in_vmem(f) for f in (tiles, both, *around)))
+    )(tile_row, tile_col, tile_work, *(in_vmem(f) for f in (tiles, feats, swapped)))
     got_y = []
     for k, q in enumerate(coded_y, 1):
         got_y.append(shifted(q, "y", k))
 
-    own, *coded_z = pl.pallas_call(
-        lambda *refs: middle_kernel(order, nz, *refs),
+    def line(count):
+        return vmem((count * order + 8, width), i16)
+
+    part, *coded_z = pl.pallas_call(
+        lambda *refs: middle_kernel(order, vblocks, *refs),
         in_specs=[VMEM] * ny,
-        out_specs=[VMEM] * nz,
-        out_shape=[vmem((vblocks * order, width), jnp.float32)]
-        + [vmem((vblocks * order + 16, width), i16)] * (nz - 1),
-        scratch_shapes=[
-            pltpu.VMEM((16 * (ny - 1), width), jnp.float32),
-            pltpu.VMEM((16, width), jnp.float32),
-        ],
+        out_specs=[VMEM] * 3,
+        out_shape=[vmem((span * order, width), jnp.float32), line(1), line(1)],
+        scratch_shapes=[pltpu.VMEM((span * (ny - 1), width), jnp.float32), pltpu.VMEM((8, width), jnp.float32)],
         compiler_params=limit(8),
         name="middle",
-    )(own, *(in_vmem(g) for g in got_y))
-    got_z = [shifted(q, "z", k) for k, q in enumerate(coded_z, 1)]
-
+    )(*(in_vmem(g) for g in (own, *got_y)))
+    for away in range(nz // 2 - 1, 0, -1):
+        ring = [shifted(coded_z[0], "z", 1), shifted(coded_z[1], "z", -1)]
+        first = away == nz // 2 - 1
+        coded_z = pl.pallas_call(
+            lambda *refs: ring_kernel(order, vblocks, away, first, *refs),
+            in_specs=[VMEM] * 3,
+            out_specs=[VMEM] * 2,
+            out_shape=[line(vblocks)] * 2,
+            scratch_shapes=[pltpu.VMEM((8, width), jnp.float32)],
+            compiler_params=limit(4),
+        )(*(in_vmem(g) for g in (part, *ring)))
+    ring = [shifted(coded_z[0], "z", 1), shifted(coded_z[1], "z", -1)]
     product = pl.pallas_call(
-        lambda *refs: last_kernel(order, *refs),
-        in_specs=[VMEM] * nz,
+        lambda *refs: last_kernel(order, vblocks, *refs),
+        in_specs=[VMEM] * 3,
         out_specs=VMEM,
         out_shape=jax.ShapeDtypeStruct((vblocks * order, width), jnp.float32),
-        compiler_params=limit(8),
+        compiler_params=limit(4),
         name="last",
-    )(own, *(in_vmem(g) for g in got_z))
+    )(*(in_vmem(g) for g in (part, *ring)))
 
     moved_vals = pl.pallas_call(
         lambda *refs: keep_kernel(owned, *refs),

time: 114 us -> 119 us (1.044)
  waiting for transfers between devices: 54.2 us -> 63.8 us
  starting transfers between devices: 45.3 us -> 39.7 us
    ppermute x10 -> x11, waiting for transfers between devices: 41.6 us -> 53.1 us  [shifted(): lax.ppermute(array, axis, [(i, (i + by) % size) for i in range(size)])]
    ppermute x10 -> x11, starting transfers between devices: 21.5 us -> 15.9 us  [shifted(): lax.ppermute(array, axis, [(i, (i + by) % size) for i in range(size)])]
    ppermute x4, waiting for transfers between devices: 6.15 us -> 4.35 us  [the longest x3 2.83 us: on_device(): lax.ppermute(mine[0], 'gx', [(i, (i + cores * k) % gx) for i in range(gx)])]
  transfers between devices with their start and end apart: 16 -> 17, of which waited for: 9 -> 15; matrix products, arithmetic and copies ran while one was open for 0% -> 0% of each run, Pallas kernels for 6% -> 5%
where the time goes in v3:
time: 119 us; the launch traced here: 118 us
  waiting for transfers between devices  63.8 us (54%)
  starting transfers between devices  39.7 us (33%)
  Pallas kernels  13.7 us (12%)
    ppermute x11, waiting for transfers between devices, shifted(): lax.ppermute(array, axis, [(i, (i + by) % size) for i in range(size)])  53.1 us
    ppermute x11, starting transfers between devices, shifted(): lax.ppermute(array, axis, [(i, (i + by) % size) for i in range(size)])  15.9 us
    all_to_all x1, starting transfers between devices, on_device(): meta = lax.all_to_all(told, GY, split_axis=0, concat_axis=0, tiled=True)  11.3 us
    all_to_all x1, starting transfers between devices, on_device(): got = lax.all_to_all(sent, GY, split_axis=0, concat_axis=0, tiled=True)  6.73 us
    all_to_all x1, waiting for transfers between devices, on_device(): meta = lax.all_to_all(told, GY, split_axis=0, concat_axis=0, tiled=True)  6.38 us
    ppermute x3, starting transfers between devices, on_device(): lax.ppermute(mine[0], 'gx', [(i, (i + cores * k) % gx) for i in range(gx)])  5.73 us
    pallas_call x1, Pallas kernels, on_device(): pl.pallas_call(lambda *refs: plan_kernel(peers, slots, *refs), in_specs=[...  3.36 us
    pallas_call x1, Pallas kernels, on_device(): pl.pallas_call(lambda *refs: product_kernel(gx, peers, ny, steps, *refs),...  3.29 us
  transfers between devices with their start and end apart: 17, of which 15 were waited for; matrix products, arithmetic and copies ran while one was open for 0% of the time, Pallas kernels for 5%

profile of v3, /device:TPU:40, one launch (start us, length us, event | category | flops | bytes accessed | tf_op | source)
XLA Modules:
  0.0 118.1 jit_solution(9907347346334743188)
XLA Ops:
  0.6 1.4 %tell.1 = s32[32,2,128]{2,1,0:T(2,128)} custom-call(s32[64]{0:T(128)} %refs_0_.3, s32[64]{0:T(128)} %refs_1_.3, s32[64]{0:T(128)} %refs_2_.3), custom_call_target="tpu_custom_call" | custom-call | tf_op jit(solution)/shard_map/tell/pallas_call | solution.py:253
  2.1 11.3 %all-to-all-start = ((s32[32,2,128]{2,1,0:T(2,128)}), s32[32,2,128]{2,1,0:T(2,128)S(1)}, u32[]{:S(2)}, u32[]{:S(2)}) async-start(s32[32,2,128]{2,1,0:T(2,128)} %tell.1), calls=%async_computation | async-start | bytes 65536 | tf_op jit(solution)/shard_map/all_to_all | solution.py:267
  13.3 1.6 %stage.1.refs_3_.refs_1_ = bf16[64,128,128]{2,1,0:T(8,128)(2,1)S(1)} custom-call(bf16[64,128,128]{2,1,0:T(8,128)(2,1)} %vals_ref.1), custom_call_target="tpu_custom_call" | custom-call | tf_op jit(solution)/shard_map/stage/pallas_call | solution.py:270
  14.9 6.4 %all-to-all-done.refs_0_ = s32[32,2,128]{2,1,0:T(2,128)S(1)} async-done(((s32[32,2,128]{2,1,0:T(2,128)}), s32[32,2,128]{2,1,0:T(2,128)S(1)}, u32[]{:S(2)}, u32[]{:S(2)}) %all-to-all-start) | async-done | bytes 32800 | tf_op jit(solution)/shard_map/all_to_all | solution.py:267
  21.3 3.4 %plan.1 = (bf16[64,128,128]{2,1,0:T(8,128)(2,1)}, s32[32]{0:T(128)}, s32[32]{0:T(128)}, s32[32]{0:T(128)}, s32[32]{0:T(128)S(1)}) custom-call(s32[32,2,128]{2,1,0:T(2,128)S(1)} %all-to-all-done.refs_0_, bf16[64,128,128]{2,1,0:T(8,128)(2,1)S(1)} %stage.1.refs_3_.refs_1_), custom_call_target="tpu_custom_call" | custom-call | tf_op jit(solution)/shard_map/plan/pallas_call | solution.py:280
  24.7 6.7 %all-to-all-start.1 = ((bf16[64,128,128]{2,1,0:T(8,128)(2,1)}), bf16[64,128,128]{2,1,0:T(8,128)(2,1)}, u32[]{:S(2)}, u32[]{:S(2)}) async-start(bf16[64,128,128]{2,1,0:T(8,128)(2,1)} %get-tuple-element.37), calls=%async_computation.1 | async-start | bytes 4194304 | tf_op jit(solution)/shard_map/all_to_all | solution.py:289
  31.5 1.6 %collective-permute-start = (bf16[2,128,128]{2,1,0:T(8,128)(2,1)S(1)}, bf16[2,128,128]{2,1,0:T(8,128)(2,1)S(1)}, u32[]{:S(2)}, u32[]{:S(2)}) collective-permute-start(bf16[2,128,128]{2,1,0:T(8,128)(2,1)S(1)} %bitcast.1), channel_id=1, source_target_pairs={{0,64},{32,96},{64,128},{96,160},{128,192},{160,224},{192,0},{224,... | collective-permute-start | bytes 196616 | tf_op jit(solution)/shard_map/ppermute | solution.py:266
  33.0 2.7 %collective-permute-start.1 = (bf16[2,128,128]{2,1,0:T(8,128)(2,1)S(1)}, bf16[2,128,128]{2,1,0:T(8,128)(2,1)S(1)}, u32[]{:S(2)}, u32[]{:S(2)}) collective-permute-start(bf16[2,128,128]{2,1,0:T(8,128)(2,1)S(1)} %bitcast.2), channel_id=1, source_target_pairs={{0,128},{32,160},{64,192},{96,224},{128,0},{160,32},{192,64},{224,... | collective-permute-start | bytes 196616 | tf_op jit(solution)/shard_map/ppermute | solution.py:266
  35.8 1.4 %collective-permute-start.2 = (bf16[2,128,128]{2,1,0:T(8,128)(2,1)S(1)}, bf16[2,128,128]{2,1,0:T(8,128)(2,1)S(1)}, u32[]{:S(2)}, u32[]{:S(2)}) collective-permute-start(bf16[2,128,128]{2,1,0:T(8,128)(2,1)S(1)} %bitcast.3), channel_id=1, source_target_pairs={{0,192},{32,224},{64,0},{96,32},{128,64},{160,96},{192,128},{224,1... | collective-permute-start | bytes 196616 | tf_op jit(solution)/shard_map/ppermute | solution.py:266
  37.2 1.6 %collective-permute-done.1 = bf16[2,128,128]{2,1,0:T(8,128)(2,1)S(1)} collective-permute-done((bf16[2,128,128]{2,1,0:T(8,128)(2,1)S(1)}, bf16[2,128,128]{2,1,0:T(8,128)(2,1)S(1)}, u32[]{:S(2)}, u32[]{:S(2)}) %collective-permute-start.1) | collective-permute-done | bytes 65568 | tf_op jit(solution)/shard_map/ppermute | solution.py:266
  38.8 1.2 %collective-permute-done.2 = bf16[2,128,128]{2,1,0:T(8,128)(2,1)S(1)} collective-permute-done((bf16[2,128,128]{2,1,0:T(8,128)(2,1)S(1)}, bf16[2,128,128]{2,1,0:T(8,128)(2,1)S(1)}, u32[]{:S(2)}, u32[]{:S(2)}) %collective-permute-start.2) | collective-permute-done | bytes 65568 | tf_op jit(solution)/shard_map/ppermute | solution.py:266
  40.2 1.5 %collective-permute-done.3.refs_5_ = bf16[8,128,128]{2,1,0:T(8,128)(2,1)S(1)} collective-permute-done((bf16[8,128,128]{2,1,0:T(8,128)(2,1)S(1)}, bf16[8,128,128]{2,1,0:T(8,128)(2,1)S(1)}, u32[]{:S(2)}, u32[]{:S(2)}) %collective-permute-start.3) | collective-permute-done | bytes 262176 | tf_op jit(solution)/shard_map/ppermute | solution.py:269
  41.7 3.3 %products.1 = (f32[2048,128]{1,0:T(8,128)S(1)}, s16[2064,128]{1,0:T(8,128)(2,1)S(1)}, s16[2064,128]{1,0:T(8,128)(2,1)S(1)}, s16[2064,128]{1,0:T(8,128)(2,1)S(1)}) custom-call(s32[64]{0:T(128)S(1)} %copy-done, s32[64]{0:T(128)S(1)} %copy-done.1, s32[64]{0:T(128)S(1)} %copy-done.2, bf16[64,128,128]{2,1,0:T(8,128)(2,1)S(1)} %stage.1.refs_3_.refs_1_, ...), custom_call_target="tpu_custom_call" | custom-call | tf_op jit(solution)/shard_map/products/pallas_call | solution.py:294
  45.0 1.6 %collective-permute-start.4 = (s16[2064,128]{1,0:T(8,128)(2,1)S(1)}, s16[2064,128]{1,0:T(8,128)(2,1)S(1)}, u32[]{:S(2)}, u32[]{:S(2)}) collective-permute-start(s16[2064,128]{1,0:T(8,128)(2,1)S(1)} %get-tuple-element.24), channel_id=1, source_target_pairs={{0,8},{8,16},{16,24},{24,0},{1,9},{9,17},{17,25},{25,1},{2,10},{10... | collective-permute-start | bytes 1585160 | tf_op jit(solution)/shard_map/ppermute | solution.py:35
  46.6 1.1 collective-permute-start.5
  47.6 2.2 %collective-permute-start.6 = (s16[2064,128]{1,0:T(8,128)(2,1)S(1)}, s16[2064,128]{1,0:T(8,128)(2,1)S(1)}, u32[]{:S(2)}, u32[]{:S(2)}) collective-permute-start(s16[2064,128]{1,0:T(8,128)(2,1)S(1)} %get-tuple-element.26), channel_id=1, source_target_pairs={{0,24},{8,0},{16,8},{24,16},{1,25},{9,1},{17,9},{25,17},{2,26},{10... | collective-permute-start | bytes 1585160 | tf_op jit(solution)/shard_map/ppermute | solution.py:35
  49.9 19.3 %collective-permute-done.4.refs_1_ = s16[2064,128]{1,0:T(8,128)(2,1)S(1)} collective-permute-done((s16[2064,128]{1,0:T(8,128)(2,1)S(1)}, s16[2064,128]{1,0:T(8,128)(2,1)S(1)}, u32[]{:S(2)}, u32[]{:S(2)}) %collective-permute-start.4) | collective-permute-done | bytes 528416 | tf_op jit(solution)/shard_map/ppermute | solution.py:35
  69.1 4.4 %collective-permute-done.5.refs_2_ = s16[2064,128]{1,0:T(8,128)(2,1)S(1)} collective-permute-done((s16[2064,128]{1,0:T(8,128)(2,1)S(1)}, s16[2064,128]{1,0:T(8,128)(2,1)S(1)}, u32[]{:S(2)}, u32[]{:S(2)}) %collective-permute-start.5) | collective-permute-done | bytes 528416 | tf_op jit(solution)/shard_map/ppermute | solution.py:35
  73.6 12.2 %collective-permute-done.6.refs_3_ = s16[2064,128]{1,0:T(8,128)(2,1)S(1)} collective-permute-done((s16[2064,128]{1,0:T(8,128)(2,1)S(1)}, s16[2064,128]{1,0:T(8,128)(2,1)S(1)}, u32[]{:S(2)}, u32[]{:S(2)}) %collective-permute-start.6) | collective-permute-done | bytes 528416 | tf_op jit(solution)/shard_map/ppermute | solution.py:35
  86.3 2.2 %collective-permute-start.7 = (s16[136,128]{1,0:T(8,128)(2,1)S(1)}, s16[136,128]{1,0:T(8,128)(2,1)S(1)}, u32[]{:S(2)}, u32[]{:S(2)}) collective-permute-start(s16[136,128]{1,0:T(8,128)(2,1)S(1)} %get-tuple-element.28), channel_id=1, source_target_pairs={{0,1},{1,2},{2,3},{3,4},{4,5},{5,6},{6,7},{7,0},{8,9},{9,10},{10,1... | collective-permute-start | bytes 104456 | tf_op jit(solution)/shard_map/ppermute | solution.py:35
  88.6 1.8 %collective-permute-done.7.refs_1_ = s16[136,128]{1,0:T(8,128)(2,1)S(1)} collective-permute-done((s16[136,128]{1,0:T(8,128)(2,1)S(1)}, s16[136,128]{1,0:T(8,128)(2,1)S(1)}, u32[]{:S(2)}, u32[]{:S(2)}) %collective-permute-start.7) | collective-permute-done | bytes 34848 | tf_op jit(solution)/shard_map/ppermute | solution.py:35
  90.3 2.2 %collective-permute-done.8.refs_2_ = s16[136,128]{1,0:T(8,128)(2,1)S(1)} collective-permute-done((s16[136,128]{1,0:T(8,128)(2,1)S(1)}, s16[136,128]{1,0:T(8,128)(2,1)S(1)}, u32[]{:S(2)}, u32[]{:S(2)}) %collective-permute-start.8) | collective-permute-done | bytes 34848 | tf_op jit(solution)/shard_map/ppermute | solution.py:35
  92.7 2.0 %collective-permute-start.9 = (s16[264,128]{1,0:T(8,128)(2,1)S(1)}, s16[264,128]{1,0:T(8,128)(2,1)S(1)}, u32[]{:S(2)}, u32[]{:S(2)}) collective-permute-start(s16[264,128]{1,0:T(8,128)(2,1)S(1)} %get-tuple-element.30), channel_id=1, source_target_pairs={{0,1},{1,2},{2,3},{3,4},{4,5},{5,6},{6,7},{7,0},{8,9},{9,10},{10,1... | collective-permute-start | bytes 202760 | tf_op jit(solution)/shard_map/ppermute | solution.py:35
  94.7 2.3 %collective-permute-done.10.refs_2_ = s16[264,128]{1,0:T(8,128)(2,1)S(1)} collective-permute-done((s16[264,128]{1,0:T(8,128)(2,1)S(1)}, s16[264,128]{1,0:T(8,128)(2,1)S(1)}, u32[]{:S(2)}, u32[]{:S(2)}) %collective-permute-start.10) | collective-permute-done | bytes 67616 | tf_op jit(solution)/shard_map/ppermute | solution.py:35
  97.5 2.3 %collective-permute-start.11 = (s16[264,128]{1,0:T(8,128)(2,1)S(1)}, s16[264,128]{1,0:T(8,128)(2,1)S(1)}, u32[]{:S(2)}, u32[]{:S(2)}) collective-permute-start(s16[264,128]{1,0:T(8,128)(2,1)S(1)} %get-tuple-element.32), channel_id=1, source_target_pairs={{0,1},{1,2},{2,3},{3,4},{4,5},{5,6},{6,7},{7,0},{8,9},{9,10},{10,1... | collective-permute-start | bytes 202760 | tf_op jit(solution)/shard_map/ppermute | solution.py:35
  99.8 1.1 collective-permute-start.12
  100.9 2.2 %collective-permute-done.11.refs_1_ = s16[264,128]{1,0:T(8,128)(2,1)S(1)} collective-permute-done((s16[264,128]{1,0:T(8,128)(2,1)S(1)}, s16[264,128]{1,0:T(8,128)(2,1)S(1)}, u32[]{:S(2)}, u32[]{:S(2)}) %collective-permute-start.11) | collective-permute-done | bytes 67616 | tf_op jit(solution)/shard_map/ppermute | solution.py:35
  103.1 2.2 %collective-permute-done.12.refs_2_ = s16[264,128]{1,0:T(8,128)(2,1)S(1)} collective-permute-done((s16[264,128]{1,0:T(8,128)(2,1)S(1)}, s16[264,128]{1,0:T(8,128)(2,1)S(1)}, u32[]{:S(2)}, u32[]{:S(2)}) %collective-permute-start.12) | collective-permute-done | bytes 67616 | tf_op jit(solution)/shard_map/ppermute | solution.py:35
  105.4 3.3 %collective-permute-start.13 = (s16[264,128]{1,0:T(8,128)(2,1)S(1)}, s16[264,128]{1,0:T(8,128)(2,1)S(1)}, u32[]{:S(2)}, u32[]{:S(2)}) collective-permute-start(s16[264,128]{1,0:T(8,128)(2,1)S(1)} %get-tuple-element.34), channel_id=1, source_target_pairs={{0,1},{1,2},{2,3},{3,4},{4,5},{5,6},{6,7},{7,0},{8,9},{9,10},{10,1... | collective-permute-start | bytes 202760 | tf_op jit(solution)/shard_map/ppermute | solution.py:35
  108.7 1.9 %collective-permute-done.13.refs_1_ = s16[264,128]{1,0:T(8,128)(2,1)S(1)} collective-permute-done((s16[264,128]{1,0:T(8,128)(2,1)S(1)}, s16[264,128]{1,0:T(8,128)(2,1)S(1)}, u32[]{:S(2)}, u32[]{:S(2)}) %collective-permute-start.13) | collective-permute-done | bytes 67616 | tf_op jit(solution)/shard_map/ppermute | solution.py:35
  110.6 4.2 %collective-permute-done.14.refs_2_ = s16[264,128]{1,0:T(8,128)(2,1)S(1)} collective-permute-done((s16[264,128]{1,0:T(8,128)(2,1)S(1)}, s16[264,128]{1,0:T(8,128)(2,1)S(1)}, u32[]{:S(2)}, u32[]{:S(2)}) %collective-permute-start.14) | collective-permute-done | bytes 67616 | tf_op jit(solution)/shard_map/ppermute | solution.py:35
  115.6 2.6 %keep.1 = bf16[32,128,128]{2,1,0:T(8,128)(2,1)} custom-call(s32[32]{0:T(128)S(1)} %get-tuple-element.36.refs_0_, bf16[64,128,128]{2,1,0:T(8,128)(2,1)} %all-to-all-done.1.refs_1_), custom_call_target="tpu_custom_call" | custom-call | tf_op jit(solution)/shard_map/keep/pallas_call | solution.py:346
  (21 shorter events, 2.2 us)
Async XLA Ops:
  2.1 19.2 %all-to-all-start = ((s32[32,2,128]{2,1,0:T(2,128)}), s32[32,2,128]{2,1,0:T(2,128)S(1)}, u32[]{:S(2)}, u32[]{:S(2)}) async-start(s32[32,2,128]{2,1,0:T(2,128)} %tell.1), calls=%async_computation | async-start | bytes 65536 | tf_op jit(solution)/shard_map/all_to_all | solution.py:267
  24.7 6.8 %copy-start.3 = (bf16[256,128]{1,0:T(8,128)(2,1)S(1)}, bf16[256,128]{1,0:T(8,128)(2,1)}, u32[]{:S(2)}) copy-start(bf16[256,128]{1,0:T(8,128)(2,1)} %param.5) | copy-start | bytes 196612
  24.7 17.0 %copy-start = (s32[64]{0:T(128)S(1)}, s32[64]{0:T(128)}, u32[]{:S(2)}) copy-start(s32[64]{0:T(128)} %refs_0_.3) | copy-start | bytes 772
  24.7 17.0 %copy-start.1 = (s32[64]{0:T(128)S(1)}, s32[64]{0:T(128)}, u32[]{:S(2)}) copy-start(s32[64]{0:T(128)} %refs_1_.3) | copy-start | bytes 772
  24.7 17.0 %copy-start.2 = (s32[64]{0:T(128)S(1)}, s32[64]{0:T(128)}, u32[]{:S(2)}) copy-start(s32[64]{0:T(128)} %refs_2_.3) | copy-start | bytes 772
  24.7 90.9 %all-to-all-start.1 = ((bf16[64,128,128]{2,1,0:T(8,128)(2,1)}), bf16[64,128,128]{2,1,0:T(8,128)(2,1)}, u32[]{:S(2)}, u32[]{:S(2)}) async-start(bf16[64,128,128]{2,1,0:T(8,128)(2,1)} %get-tuple-element.37), calls=%async_computation.1 | async-start | bytes 4194304 | tf_op jit(solution)/shard_map/all_to_all | solution.py:289
  31.5 5.7 %collective-permute-start = (bf16[2,128,128]{2,1,0:T(8,128)(2,1)S(1)}, bf16[2,128,128]{2,1,0:T(8,128)(2,1)S(1)}, u32[]{:S(2)}, u32[]{:S(2)}) collective-permute-start(bf16[2,128,128]{2,1,0:T(8,128)(2,1)S(1)} %bitcast.1), channel_id=1, source_target_pairs={{0,64},{32,96},{64,128},{96,160},{128,192},{160,224},{192,0},{224,... | collective-permute-start | bytes 196616 | tf_op jit(solution)/shard_map/ppermute | solution.py:266
  33.0 5.8 %collective-permute-start.1 = (bf16[2,128,128]{2,1,0:T(8,128)(2,1)S(1)}, bf16[2,128,128]{2,1,0:T(8,128)(2,1)S(1)}, u32[]{:S(2)}, u32[]{:S(2)}) collective-permute-start(bf16[2,128,128]{2,1,0:T(8,128)(2,1)S(1)} %bitcast.2), channel_id=1, source_target_pairs={{0,128},{32,160},{64,192},{96,224},{128,0},{160,32},{192,64},{224,... | collective-permute-start | bytes 196616 | tf_op jit(solution)/shard_map/ppermute | solution.py:266
  35.8 4.3 %collective-permute-start.2 = (bf16[2,128,128]{2,1,0:T(8,128)(2,1)S(1)}, bf16[2,128,128]{2,1,0:T(8,128)(2,1)S(1)}, u32[]{:S(2)}, u32[]{:S(2)}) collective-permute-start(bf16[2,128,128]{2,1,0:T(8,128)(2,1)S(1)} %bitcast.3), channel_id=1, source_target_pairs={{0,192},{32,224},{64,0},{96,32},{128,64},{160,96},{192,128},{224,1... | collective-permute-start | bytes 196616 | tf_op jit(solution)/shard_map/ppermute | solution.py:266
  40.1 1.6 %collective-permute-start.3 = (bf16[8,128,128]{2,1,0:T(8,128)(2,1)S(1)}, bf16[8,128,128]{2,1,0:T(8,128)(2,1)S(1)}, u32[]{:S(2)}, u32[]{:S(2)}) collective-permute-start(bf16[8,128,128]{2,1,0:T(8,128)(2,1)S(1)} %pad_maximum_fusion.refs_4_), channel_id=1, source_target_pairs={{0,32},{32,0},{64,96},{96,64},{128,160},{160,128},{192,224},{224,1... | collective-permute-start | bytes 786440 | tf_op jit(solution)/shard_map/ppermute | solution.py:269
  45.0 24.2 %collective-permute-start.4 = (s16[2064,128]{1,0:T(8,128)(2,1)S(1)}, s16[2064,128]{1,0:T(8,128)(2,1)S(1)}, u32[]{:S(2)}, u32[]{:S(2)}) collective-permute-start(s16[2064,128]{1,0:T(8,128)(2,1)S(1)} %get-tuple-element.24), channel_id=1, source_target_pairs={{0,8},{8,16},{16,24},{24,0},{1,9},{9,17},{17,25},{25,1},{2,10},{10... | collective-permute-start | bytes 1585160 | tf_op jit(solution)/shard_map/ppermute | solution.py:35
  46.6 27.0 %collective-permute-start.5 = (s16[2064,128]{1,0:T(8,128)(2,1)S(1)}, s16[2064,128]{1,0:T(8,128)(2,1)S(1)}, u32[]{:S(2)}, u32[]{:S(2)}) collective-permute-start(s16[2064,128]{1,0:T(8,128)(2,1)S(1)} %get-tuple-element.25), channel_id=1, source_target_pairs={{0,16},{8,24},{16,0},{24,8},{1,17},{9,25},{17,1},{25,9},{2,18},{10... | collective-permute-start | bytes 1585160 | tf_op jit(solution)/shard_map/ppermute | solution.py:35
  47.6 38.2 %collective-permute-start.6 = (s16[2064,128]{1,0:T(8,128)(2,1)S(1)}, s16[2064,128]{1,0:T(8,128)(2,1)S(1)}, u32[]{:S(2)}, u32[]{:S(2)}) collective-permute-start(s16[2064,128]{1,0:T(8,128)(2,1)S(1)} %get-tuple-element.26), channel_id=1, source_target_pairs={{0,24},{8,0},{16,8},{24,16},{1,25},{9,1},{17,9},{25,17},{2,26},{10... | collective-permute-start | bytes 1585160 | tf_op jit(solution)/shard_map/ppermute | solution.py:35
  86.3 4.0 %collective-permute-start.7 = (s16[136,128]{1,0:T(8,128)(2,1)S(1)}, s16[136,128]{1,0:T(8,128)(2,1)S(1)}, u32[]{:S(2)}, u32[]{:S(2)}) collective-permute-start(s16[136,128]{1,0:T(8,128)(2,1)S(1)} %get-tuple-element.28), channel_id=1, source_target_pairs={{0,1},{1,2},{2,3},{3,4},{4,5},{5,6},{6,7},{7,0},{8,9},{9,10},{10,1... | collective-permute-start | bytes 104456 | tf_op jit(solution)/shard_map/ppermute | solution.py:35
  88.6 3.9 %collective-permute-start.8 = (s16[136,128]{1,0:T(8,128)(2,1)S(1)}, s16[136,128]{1,0:T(8,128)(2,1)S(1)}, u32[]{:S(2)}, u32[]{:S(2)}) collective-permute-start(s16[136,128]{1,0:T(8,128)(2,1)S(1)} %get-tuple-element.29), channel_id=1, source_target_pairs={{0,7},{1,0},{2,1},{3,2},{4,3},{5,4},{6,5},{7,6},{8,15},{9,8},{10,9... | collective-permute-start | bytes 104456 | tf_op jit(solution)/shard_map/ppermute | solution.py:35
  92.6 4.4 %collective-permute-start.10 = (s16[264,128]{1,0:T(8,128)(2,1)S(1)}, s16[264,128]{1,0:T(8,128)(2,1)S(1)}, u32[]{:S(2)}, u32[]{:S(2)}) collective-permute-start(s16[264,128]{1,0:T(8,128)(2,1)S(1)} %get-tuple-element.31), channel_id=1, source_target_pairs={{0,7},{1,0},{2,1},{3,2},{4,3},{5,4},{6,5},{7,6},{8,15},{9,8},{10,9... | collective-permute-start | bytes 202760 | tf_op jit(solution)/shard_map/ppermute | solution.py:35
  92.7 4.7 %collective-permute-start.9 = (s16[264,128]{1,0:T(8,128)(2,1)S(1)}, s16[264,128]{1,0:T(8,128)(2,1)S(1)}, u32[]{:S(2)}, u32[]{:S(2)}) collective-permute-start(s16[264,128]{1,0:T(8,128)(2,1)S(1)} %get-tuple-element.30), channel_id=1, source_target_pairs={{0,1},{1,2},{2,3},{3,4},{4,5},{5,6},{6,7},{7,0},{8,9},{9,10},{10,1... | collective-permute-start | bytes 202760 | tf_op jit(solution)/shard_map/ppermute | solution.py:35
  97.5 5.6 %collective-permute-start.11 = (s16[264,128]{1,0:T(8,128)(2,1)S(1)}, s16[264,128]{1,0:T(8,128)(2,1)S(1)}, u32[]{:S(2)}, u32[]{:S(2)}) collective-permute-start(s16[264,128]{1,0:T(8,128)(2,1)S(1)} %get-tuple-element.32), channel_id=1, source_target_pairs={{0,1},{1,2},{2,3},{3,4},{4,5},{5,6},{6,7},{7,0},{8,9},{9,10},{10,1... | collective-permute-start | bytes 202760 | tf_op jit(solution)/shard_map/ppermute | solution.py:35
  99.8 5.5 %collective-permute-start.12 = (s16[264,128]{1,0:T(8,128)(2,1)S(1)}, s16[264,128]{1,0:T(8,128)(2,1)S(1)}, u32[]{:S(2)}, u32[]{:S(2)}) collective-permute-start(s16[264,128]{1,0:T(8,128)(2,1)S(1)} %get-tuple-element.33), channel_id=1, source_target_pairs={{0,7},{1,0},{2,1},{3,2},{4,3},{5,4},{6,5},{7,6},{8,15},{9,8},{10,9... | collective-permute-start | bytes 202760 | tf_op jit(solution)/shard_map/ppermute | solution.py:35
  105.4 5.2 %collective-permute-start.13 = (s16[264,128]{1,0:T(8,128)(2,1)S(1)}, s16[264,128]{1,0:T(8,128)(2,1)S(1)}, u32[]{:S(2)}, u32[]{:S(2)}) collective-permute-start(s16[264,128]{1,0:T(8,128)(2,1)S(1)} %get-tuple-element.34), channel_id=1, source_target_pairs={{0,1},{1,2},{2,3},{3,4},{4,5},{5,6},{6,7},{7,0},{8,9},{9,10},{10,1... | collective-permute-start | bytes 202760 | tf_op jit(solution)/shard_map/ppermute | solution.py:35
  108.7 6.2 %collective-permute-start.14 = (s16[264,128]{1,0:T(8,128)(2,1)S(1)}, s16[264,128]{1,0:T(8,128)(2,1)S(1)}, u32[]{:S(2)}, u32[]{:S(2)}) collective-permute-start(s16[264,128]{1,0:T(8,128)(2,1)S(1)} %get-tuple-element.35), channel_id=1, source_target_pairs={{0,7},{1,0},{2,1},{3,2},{4,3},{5,4},{6,5},{7,6},{8,15},{9,8},{10,9... | collective-permute-start | bytes 202760 | tf_op jit(solution)/shard_map/ppermute | solution.py:35

commit v4 on v3

--- a/solution.py
+++ b/solution.py
@@ -65,23 +65,35 @@
         c.wait()
 
 
-def plan_kernel(peers, slots, meta_ref, vals_ref, sent_ref, row_ref, col_ref, work_ref, slot_ref, sems):
-    me = lax.axis_index("y") * lax.axis_size("z") + lax.axis_index("z")
+def place_of():
+    return lax.axis_index("y") * lax.axis_size("z") + lax.axis_index("z")
+
+
+def plan_kernel(peers, slots, meta_ref, vals_ref, sent_ref, sems):
+    me = place_of()
     share = slots // peers
 
     def before(s, total):
         return total + jnp.where(s < me, meta_ref[s, 1, slots], 0)
 
-    first = lax.fori_loop(0, peers, before, jnp.int32(0))
+    first = lax.fori_loop(0, peers, before, jnp.int32(0), unroll=8)
     turn = lax.rem(first, peers)
 
     def start(d, carry):
+        at = lax.rem(d - turn + peers, peers)
         for w in range(share):
-            tile = lax.rem(d - turn + peers, peers) + w * peers
-            pltpu.make_async_copy(vals_ref.at[tile], sent_ref.at[d * share + w], sems.at[0]).start()
+            pltpu.make_async_copy(
+                vals_ref.at[at + w * peers], sent_ref.at[d * share + w], sems.at[0]
+            ).start()
         return carry
 
-    lax.fori_loop(0, peers, start, 0, unroll=4)
+    lax.fori_loop(0, peers, start, 0, unroll=8)
+    pltpu.make_async_copy(vals_ref, sent_ref, sems.at[0]).wait()
+
+
+def list_kernel(peers, slots, meta_ref, row_ref, col_ref, work_ref, slot_ref):
+    me = place_of()
+    share = slots // peers
 
     def source(s, begin):
         count = meta_ref[s, 1, slots]
@@ -91,7 +103,7 @@
 
             @pl.when(at < count)
             def _():
-                k = (begin + at) // peers
+                k = lax.div(begin + at, peers)
                 row_ref[k] = meta_ref[s, 0, at]
                 col_ref[k] = meta_ref[s, 0, slots + at]
                 work_ref[k] = meta_ref[s, 1, at]
@@ -100,8 +112,6 @@
         return begin + count
 
     lax.fori_loop(0, peers, source, jnp.int32(0))
-
-    pltpu.make_async_copy(vals_ref, sent_ref, sems.at[0]).wait()
 
 
 def keep_kernel(owned, slot_ref, got_ref, out_ref, sems):
@@ -123,7 +133,7 @@
 
 
 def product_kernel(gx, gy, groups, steps, row_ref, col_ref, work_ref, tiles, feats_ref, swap_ref, *refs):
-    own_ref, q_refs, (acc, held, made, exps) = refs[0], refs[1:-4], refs[-4:]
+    own_ref, rest_ref, right_ref, left_ref, acc, held, made, exps, sems = refs
     slots, order, _ = tiles.shape
     per_step = slots // steps
     vblocks = held.shape[0] // gx
@@ -161,20 +171,32 @@
 
         lax.fori_loop(0, per_step, add, 0, unroll=True)
 
-    def own(i, carry):
-        own_ref[pl.ds(i * order, order), :] = acc[y * span + i]
-        return carry
-
-    for k, q_ref in enumerate(q_refs, 1):
-        base = lax.rem(y + k, groups) * span
-
-        def code(i, carry):
-            coded(acc[base + i], q_ref, exps, i * order, i)
-            return carry
-
-        lax.fori_loop(0, span, code, 0, unroll=2)
-        q_ref[pl.ds(span * order, span), :] = exps[...].astype(jnp.int32).astype(jnp.int16)
-    lax.fori_loop(0, span, own, 0)
+    half = span // 2
+    there, behind = (lax.rem(y + k, groups) * span for k in (1, groups - 1))
+    far = lax.rem(y + groups // 2, groups) * span
+    leaving = [
+        pltpu.make_async_copy(acc.at[pl.ds(at, n)], ref, sems.at[i])
+        for i, (at, n, ref) in enumerate(
+            (
+                (y * span, span, own_ref),
+                (there, half, rest_ref.at[pl.ds(0, half)]),
+                (behind + half, half, rest_ref.at[pl.ds(half, half)]),
+            )
+        )
+    ]
+    for c in leaving:
+        c.start()
+    for q_ref, starts in ((right_ref, (far, there + half)), (left_ref, (far + half, behind))):
+        for n, base in enumerate(starts):
+
+            def code(i, carry):
+                coded(acc[base + i], q_ref, exps, (n * half + i) * order, n * half + i)
+                return carry
+
+            lax.fori_loop(0, half, code, 0, unroll=2)
+        store_exps(q_ref, exps, span, order)
+    for c in leaving:
+        c.wait()
 
 
 def scales_of(ref, at):
@@ -191,54 +213,61 @@
     q_ref[pl.ds(count * order, exps.shape[0]), :] = exps[...].astype(jnp.int32).astype(jnp.int16)
 
 
-def middle_kernel(order, vblocks, own_ref, *refs):
-    got, part_ref, q_refs, scales, exps = refs[:-5], refs[-5], refs[-4:-2], refs[-2], refs[-1]
-    blocks = part_ref.shape[0] // order
-    owners = blocks // vblocks
+def relay_kernel(order, rest_ref, low_ref, high_ref, right_ref, left_ref, scales, exps):
+    span = rest_ref.shape[0]
+    half = span // 2
+    for side, (got, q_ref) in enumerate(((low_ref, right_ref), (high_ref, left_ref))):
+        scales[...] = scales_of(got, span * order)
+
+        def add(i, carry):
+            part = got[pl.ds(i * order, order), :].astype(jnp.int32).astype(jnp.float32)
+            x = rest_ref[side * half + i] + part * scales[pl.ds(i, 1), :]
+            coded(x, q_ref, exps, i * order, i)
+            return carry
+
+        lax.fori_loop(0, half, add, 0, unroll=2)
+        store_exps(q_ref, exps, half, order)
+
+
+def middle_kernel(order, vblocks, own_ref, low_ref, high_ref, low2_ref, high2_ref, out_ref, *refs):
+    q_refs, (total, scales, exps) = refs[:-3], refs[-3:]
+    span = own_ref.shape[0]
+    half = span // 2
+    owners = span // vblocks
     z = lax.axis_index("z")
     exps[...] = jnp.zeros_like(exps)
-    for n, g in enumerate(got):
-        scales[pl.ds(blocks * n, blocks), :] = scales_of(g, blocks * order)
-
-    def add(block, carry):
-        at = block * order
-        x = own_ref[pl.ds(at, order), :]
-        for n, g in enumerate(got):
-            part = g[pl.ds(at, order), :].astype(jnp.int32).astype(jnp.float32)
-            x = x + part * scales[pl.ds(blocks * n + block, 1), :]
-        part_ref[pl.ds(at, order), :] = x
-        return carry
-
-    lax.fori_loop(0, blocks, add, 0, unroll=2)
-    far = lax.rem(z + owners // 2, owners) * vblocks
-    for v, q_ref in enumerate(q_refs):
-        coded(part_ref[pl.ds((far + v) * order, order), :], q_ref, exps, 0, 0)
-        store_exps(q_ref, exps, 1, order)
-
-
-def ring_kernel(order, vblocks, away, first, part_ref, right_ref, left_ref, to_right, to_left, exps):
-    owners = part_ref.shape[0] // order // vblocks
-    z = lax.axis_index("z")
-    exps[...] = jnp.zeros_like(exps)
-    ways = ((right_ref, to_right, away, 0), (left_ref, to_left, owners - away, 1))
-    for got, q_ref, by, side in ways:
-        base = lax.rem(z + by, owners) * vblocks
+    scales[pl.ds(0, half), :] = scales_of(high_ref, span * order)[half:, :]
+    scales[pl.ds(half, half), :] = scales_of(low_ref, span * order)[half:, :]
+    scales[pl.ds(span, half), :] = scales_of(low2_ref, half * order)
+    scales[pl.ds(span + half, half), :] = scales_of(high2_ref, half * order)
+
+    def part(ref, at, scale):
+        x = ref[pl.ds(at * order, order), :].astype(jnp.int32).astype(jnp.float32)
+        return x * scales[pl.ds(scale, 1), :]
+
+    for side, (near, last) in enumerate(((high_ref, low2_ref), (low_ref, high2_ref))):
+
+        def add(i, carry):
+            at = side * half + i
+            total[at] = own_ref[at] + part(near, half + i, at) + part(last, i, span + at)
+            return carry
+
+        lax.fori_loop(0, half, add, 0, unroll=2)
+    for v in range(vblocks):
+        out_ref[pl.ds(v * order, order), :] = total[z * vblocks + v]
+    for k, q_ref in enumerate(q_refs, 1):
+        base = lax.rem(z + k, owners) * vblocks
         for v in range(vblocks):
-            x = part_ref[pl.ds((base + v) * order, order), :]
-            if not first:
-                x = x + part_of(got, v, order, vblocks)
-            elif v == side:
-                x = x + part_of(got, 0, order, 1)
-            coded(x, q_ref, exps, v * order, v)
+            coded(total[base + v], q_ref, exps, v * order, v)
         store_exps(q_ref, exps, vblocks, order)
 
 
-def last_kernel(order, vblocks, part_ref, right_ref, left_ref, out_ref):
-    base = lax.axis_index("z") * vblocks
+def last_kernel(order, vblocks, own_ref, *refs):
+    got, out_ref = refs[:-1], refs[-1]
     for v in range(vblocks):
-        x = part_ref[pl.ds((base + v) * order, order), :]
-        for got in (right_ref, left_ref):
-            x = x + part_of(got, v, order, vblocks)
+        x = own_ref[pl.ds(v * order, order), :]
+        for g in got:
+            x = x + part_of(g, v, order, vblocks)
         out_ref[pl.ds(v * order, order), :] = x
 
 
@@ -277,71 +306,82 @@
         name="stage",
     )(in_hbm(tile_vals))
     small = jax.ShapeDtypeStruct((owned,), jnp.int32)
-    sent, moved_row, moved_col, moved_work, kept = pl.pallas_call(
+    sent = pl.pallas_call(
         lambda *refs: plan_kernel(peers, slots, *refs),
         in_specs=[SMEM, VMEM],
-        out_specs=[ANY, SMEM, SMEM, SMEM, SMEM],
-        out_shape=[pltpu.HBM(tile_vals.shape, tile_vals.dtype), small, small, small, small],
+        out_specs=ANY,
+        out_shape=pltpu.HBM(tile_vals.shape, tile_vals.dtype),
         scratch_shapes=[pltpu.SemaphoreType.DMA((1,))],
         compiler_params=limit(4),
         name="plan",
     )(meta, in_vmem(tiles))
+    moved_row, moved_col, moved_work, kept = pl.pallas_call(
+        lambda *refs: list_kernel(peers, slots, *refs),
+        in_specs=[SMEM],
+        out_specs=[SMEM] * 4,
+        out_shape=[small] * 4,
+        compiler_params=limit(4),
+        name="list",
+    )(meta)
     got = lax.all_to_all(sent, GY, split_axis=0, concat_axis=0, tiled=True)
 
     steps = 8
     span = blocks // ny
     i16 = jnp.int16
-    own, *coded_y = pl.pallas_call(
+
+    def line(count, more=8):
+        return vmem((count * order + more, width), i16)
+
+    f32_blocks = pltpu.HBM((span, order, width), jnp.float32)
+    own, rest, right, left = pl.pallas_call(
         lambda *refs: product_kernel(gx, peers, ny, steps, *refs),
         in_specs=[SMEM] * 3 + [VMEM] * 3,
-        out_specs=[VMEM] * ny,
-        out_shape=[vmem((span * order, width), jnp.float32)]
-        + [vmem((span * order + span, width), i16)] * (ny - 1),
+        out_specs=[ANY, ANY, VMEM, VMEM],
+        out_shape=[f32_blocks, f32_blocks, line(span, span), line(span, span)],
         scratch_shapes=[
             pltpu.VMEM((blocks, order, width), jnp.float32),
             pltpu.VMEM((gx * vblocks, order, width), jnp.bfloat16),
             pltpu.VMEM((slots // steps, order, width), jnp.float32),
             pltpu.VMEM((span, width), jnp.float32),
+            pltpu.SemaphoreType.DMA((3,)),
         ],
         compiler_params=limit(16),
         name="products",
     )(tile_row, tile_col, tile_work, *(in_vmem(f) for f in (tiles, feats, swapped)))
-    got_y = []
-    for k, q in enumerate(coded_y, 1):
-        got_y.append(shifted(q, "y", k))
-
-    def line(count):
-        return vmem((count * order + 8, width), i16)
-
-    part, *coded_z = pl.pallas_call(
+    low = shifted(right, "y", 1)
+    high = shifted(left, "y", -1)
+    right, left = pl.pallas_call(
+        lambda *refs: relay_kernel(order, *refs),
+        in_specs=[VMEM] * 3,
+        out_specs=[VMEM] * 2,
+        out_shape=[line(span // 2)] * 2,
+        scratch_shapes=[pltpu.VMEM((span, width), jnp.float32), pltpu.VMEM((span // 2, width), jnp.float32)],
+        compiler_params=limit(8),
+        name="relay",
+    )(rest, low, high)
+    low2, high2 = shifted(right, "y", 1), shifted(left, "y", -1)
+    own_z, *coded_z = pl.pallas_call(
         lambda *refs: middle_kernel(order, vblocks, *refs),
-        in_specs=[VMEM] * ny,
-        out_specs=[VMEM] * 3,
-        out_shape=[vmem((span * order, width), jnp.float32), line(1), line(1)],
-        scratch_shapes=[pltpu.VMEM((span * (ny - 1), width), jnp.float32), pltpu.VMEM((8, width), jnp.float32)],
-        compiler_params=limit(8),
+        in_specs=[VMEM] * 5,
+        out_specs=[VMEM] * nz,
+        out_shape=[vmem((vblocks * order, width), jnp.float32)] + [line(vblocks)] * (nz - 1),
+        scratch_shapes=[
+            pltpu.VMEM((span, order, width), jnp.float32),
+            pltpu.VMEM((2 * span, width), jnp.float32),
+            pltpu.VMEM((8, width), jnp.float32),
+        ],
+        compiler_params=limit(12),
         name="middle",
-    )(*(in_vmem(g) for g in (own, *got_y)))
-    for away in range(nz // 2 - 1, 0, -1):
-        ring = [shifted(coded_z[0], "z", 1), shifted(coded_z[1], "z", -1)]
-        first = away == nz // 2 - 1
-        coded_z = pl.pallas_call(
-            lambda *refs: ring_kernel(order, vblocks, away, first, *refs),
-            in_specs=[VMEM] * 3,
-            out_specs=[VMEM] * 2,
-            out_shape=[line(vblocks)] * 2,
-            scratch_shapes=[pltpu.VMEM((8, width), jnp.float32)],
-            compiler_params=limit(4),
-        )(*(in_vmem(g) for g in (part, *ring)))
-    ring = [shifted(coded_z[0], "z", 1), shifted(coded_z[1], "z", -1)]
+    )(own, low, high, low2, high2)
+    got_z = [shifted(q, "z", k) for k, q in enumerate(coded_z, 1)]
     product = pl.pallas_call(
         lambda *refs: last_kernel(order, vblocks, *refs),
-        in_specs=[VMEM] * 3,
+        in_specs=[VMEM] * nz,
         out_specs=VMEM,
         out_shape=jax.ShapeDtypeStruct((vblocks * order, width), jnp.float32),
         compiler_params=limit(4),
         name="last",
-    )(*(in_vmem(g) for g in (part, *ring)))
+    )(*(in_vmem(g) for g in (own_z, *got_z)))
 
     moved_vals = pl.pallas_call(
         lambda *refs: keep_kernel(owned, *refs),

time: 119 us -> 109 us (0.916)
  the two profiles are of different devices: /device:TPU:40 before, /device:TPU:56 now
where the time goes in v4:
time: 109 us; the launch traced here: 108 us
  waiting for transfers between devices  49.8 us (46%)
  starting transfers between devices  40.4 us (37%)
  Pallas kernels  16 us (15%)
  local copies, waits for them, and re-layouts  1.26 us (1%)
    ppermute x11, waiting for transfers between devices, shifted(): lax.ppermute(array, axis, [(i, (i + by) % size) for i in range(size)])  39.8 us
    ppermute x11, starting transfers between devices, shifted(): lax.ppermute(array, axis, [(i, (i + by) % size) for i in range(size)])  16 us
    all_to_all x1, starting transfers between devices, on_device(): meta = lax.all_to_all(told, GY, split_axis=0, concat_axis=0, tiled=True)  11.1 us
    all_to_all x1, starting transfers between devices, on_device(): got = lax.all_to_all(sent, GY, split_axis=0, concat_axis=0, tiled=True)  7.49 us
    ppermute x3, starting transfers between devices, on_device(): lax.ppermute(mine[0], 'gx', [(i, (i + cores * k) % gx) for i in range(gx)])  5.73 us
    all_to_all x1, waiting for transfers between devices, on_device(): meta = lax.all_to_all(told, GY, split_axis=0, concat_axis=0, tiled=True)  5.68 us
    pallas_call x1, Pallas kernels, on_device(): pl.pallas_call(lambda *refs: product_kernel(gx, peers, ny, steps, *refs),...  3.27 us
    ppermute x3, waiting for transfers between devices, on_device(): lax.ppermute(mine[0], 'gx', [(i, (i + cores * k) % gx) for i in range(gx)])  2.83 us
  transfers between devices with their start and end apart: 17, of which 10 were waited for; matrix products, arithmetic and copies ran while one was open for 0% of the time, Pallas kernels for 9%

profile of v4, /device:TPU:56, one launch (start us, length us, event | category | flops | bytes accessed | tf_op | source)
XLA Modules:
  0.0 108.3 jit_solution(9542280620024748994)
XLA Ops:
  0.6 1.4 %tell.1 = s32[32,2,128]{2,1,0:T(2,128)} custom-call(s32[64]{0:T(128)} %refs_0_.3, s32[64]{0:T(128)} %refs_1_.3, s32[64]{0:T(128)} %refs_2_.3), custom_call_target="tpu_custom_call" | custom-call | tf_op jit(solution)/shard_map/tell/pallas_call | solution.py:282
  2.1 11.1 %all-to-all-start = ((s32[32,2,128]{2,1,0:T(2,128)}), s32[32,2,128]{2,1,0:T(2,128)S(1)}, u32[]{:S(2)}, u32[]{:S(2)}) async-start(s32[32,2,128]{2,1,0:T(2,128)} %tell.1), calls=%async_computation | async-start | bytes 65536 | tf_op jit(solution)/shard_map/all_to_all | solution.py:296
  13.2 1.6 %stage.1.refs_3_.refs_1_ = bf16[64,128,128]{2,1,0:T(8,128)(2,1)S(1)} custom-call(bf16[64,128,128]{2,1,0:T(8,128)(2,1)} %vals_ref.1), custom_call_target="tpu_custom_call" | custom-call | tf_op jit(solution)/shard_map/stage/pallas_call | solution.py:299
  14.7 5.7 %all-to-all-done.refs_0_ = s32[32,2,128]{2,1,0:T(2,128)S(1)} async-done(((s32[32,2,128]{2,1,0:T(2,128)}), s32[32,2,128]{2,1,0:T(2,128)S(1)}, u32[]{:S(2)}, u32[]{:S(2)}) %all-to-all-start) | async-done | bytes 32800 | tf_op jit(solution)/shard_map/all_to_all | solution.py:296
  20.4 2.5 %plan.1 = bf16[64,128,128]{2,1,0:T(8,128)(2,1)} custom-call(s32[32,2,128]{2,1,0:T(2,128)S(1)} %all-to-all-done.refs_0_, bf16[64,128,128]{2,1,0:T(8,128)(2,1)S(1)} %stage.1.refs_3_.refs_1_), custom_call_target="tpu_custom_call" | custom-call | tf_op jit(solution)/shard_map/plan/pallas_call | solution.py:309
  23.0 7.5 %all-to-all-start.1 = ((bf16[64,128,128]{2,1,0:T(8,128)(2,1)}), bf16[64,128,128]{2,1,0:T(8,128)(2,1)}, u32[]{:S(2)}, u32[]{:S(2)}) async-start(bf16[64,128,128]{2,1,0:T(8,128)(2,1)} %plan.1), calls=%async_computation.1 | async-start | bytes 4194304 | tf_op jit(solution)/shard_map/all_to_all | solution.py:326
  30.5 1.6 %collective-permute-start = (bf16[2,128,128]{2,1,0:T(8,128)(2,1)S(1)}, bf16[2,128,128]{2,1,0:T(8,128)(2,1)S(1)}, u32[]{:S(2)}, u32[]{:S(2)}) collective-permute-start(bf16[2,128,128]{2,1,0:T(8,128)(2,1)S(1)} %bitcast.1), channel_id=1, source_target_pairs={{0,64},{32,96},{64,128},{96,160},{128,192},{160,224},{192,0},{224,... | collective-permute-start | bytes 196616 | tf_op jit(solution)/shard_map/ppermute | solution.py:295
  32.0 2.7 %collective-permute-start.1 = (bf16[2,128,128]{2,1,0:T(8,128)(2,1)S(1)}, bf16[2,128,128]{2,1,0:T(8,128)(2,1)S(1)}, u32[]{:S(2)}, u32[]{:S(2)}) collective-permute-start(bf16[2,128,128]{2,1,0:T(8,128)(2,1)S(1)} %bitcast.2), channel_id=1, source_target_pairs={{0,128},{32,160},{64,192},{96,224},{128,0},{160,32},{192,64},{224,... | collective-permute-start | bytes 196616 | tf_op jit(solution)/shard_map/ppermute | solution.py:295
  34.8 1.4 %collective-permute-start.2 = (bf16[2,128,128]{2,1,0:T(8,128)(2,1)S(1)}, bf16[2,128,128]{2,1,0:T(8,128)(2,1)S(1)}, u32[]{:S(2)}, u32[]{:S(2)}) collective-permute-start(bf16[2,128,128]{2,1,0:T(8,128)(2,1)S(1)} %bitcast.3), channel_id=1, source_target_pairs={{0,192},{32,224},{64,0},{96,32},{128,64},{160,96},{192,128},{224,1... | collective-permute-start | bytes 196616 | tf_op jit(solution)/shard_map/ppermute | solution.py:295
  36.2 1.6 %collective-permute-done.1 = bf16[2,128,128]{2,1,0:T(8,128)(2,1)S(1)} collective-permute-done((bf16[2,128,128]{2,1,0:T(8,128)(2,1)S(1)}, bf16[2,128,128]{2,1,0:T(8,128)(2,1)S(1)}, u32[]{:S(2)}, u32[]{:S(2)}) %collective-permute-start.1) | collective-permute-done | bytes 65568 | tf_op jit(solution)/shard_map/ppermute | solution.py:295
  37.8 1.2 %collective-permute-done.2 = bf16[2,128,128]{2,1,0:T(8,128)(2,1)S(1)} collective-permute-done((bf16[2,128,128]{2,1,0:T(8,128)(2,1)S(1)}, bf16[2,128,128]{2,1,0:T(8,128)(2,1)S(1)}, u32[]{:S(2)}, u32[]{:S(2)}) %collective-permute-start.2) | collective-permute-done | bytes 65568 | tf_op jit(solution)/shard_map/ppermute | solution.py:295
  39.2 1.5 %collective-permute-done.3.refs_5_ = bf16[8,128,128]{2,1,0:T(8,128)(2,1)S(1)} collective-permute-done((bf16[8,128,128]{2,1,0:T(8,128)(2,1)S(1)}, bf16[8,128,128]{2,1,0:T(8,128)(2,1)S(1)}, u32[]{:S(2)}, u32[]{:S(2)}) %collective-permute-start.3) | collective-permute-done | bytes 262176 | tf_op jit(solution)/shard_map/ppermute | solution.py:298
  40.7 3.3 %products.1 = (f32[16,128,128]{2,1,0:T(8,128)}, f32[16,128,128]{2,1,0:T(8,128)}, s16[2064,128]{1,0:T(8,128)(2,1)S(1)}, s16[2064,128]{1,0:T(8,128)(2,1)S(1)}) custom-call(s32[64]{0:T(128)S(1)} %copy-done.2, s32[64]{0:T(128)S(1)} %copy-done.3, s32[64]{0:T(128)S(1)} %copy-done.4, bf16[64,128,128]{2,1,0:T(8,128)(2,1)S(1)} %stage.1.refs_3_.refs_1_, ...), custom_call_target="tpu_custom_call" | custom-call | tf_op jit(solution)/shard_map/products/pallas_call | solution.py:336
  44.5 1.6 %collective-permute-start.5 = (s16[2064,128]{1,0:T(8,128)(2,1)S(1)}, s16[2064,128]{1,0:T(8,128)(2,1)S(1)}, u32[]{:S(2)}, u32[]{:S(2)}) collective-permute-start(s16[2064,128]{1,0:T(8,128)(2,1)S(1)} %get-tuple-element.25), channel_id=1, source_target_pairs={{0,24},{8,0},{16,8},{24,16},{1,25},{9,1},{17,9},{25,17},{2,26},{10... | collective-permute-start | bytes 1585160 | tf_op jit(solution)/shard_map/ppermute | solution.py:35
  46.1 22.1 %collective-permute-done.4.refs_1_ = s16[2064,128]{1,0:T(8,128)(2,1)S(1)} collective-permute-done((s16[2064,128]{1,0:T(8,128)(2,1)S(1)}, s16[2064,128]{1,0:T(8,128)(2,1)S(1)}, u32[]{:S(2)}, u32[]{:S(2)}) %collective-permute-start.4) | collective-permute-done | bytes 528416 | tf_op jit(solution)/shard_map/ppermute | solution.py:35
  68.2 1.7 %collective-permute-done.5.refs_2_ = s16[2064,128]{1,0:T(8,128)(2,1)S(1)} collective-permute-done((s16[2064,128]{1,0:T(8,128)(2,1)S(1)}, s16[2064,128]{1,0:T(8,128)(2,1)S(1)}, u32[]{:S(2)}, u32[]{:S(2)}) %collective-permute-start.5) | collective-permute-done | bytes 528416 | tf_op jit(solution)/shard_map/ppermute | solution.py:35
  70.0 1.2 %copy-done.1 = f32[16,128,128]{2,1,0:T(8,128)S(1)} copy-done((f32[16,128,128]{2,1,0:T(8,128)S(1)}, f32[16,128,128]{2,1,0:T(8,128)}, u32[]{:S(2)}) %copy-start.1) | copy-done | bytes 1048600
  71.2 0.5 relay.1
  72.1 1.7 %collective-permute-start.7 = (s16[1032,128]{1,0:T(8,128)(2,1)S(1)}, s16[1032,128]{1,0:T(8,128)(2,1)S(1)}, u32[]{:S(2)}, u32[]{:S(2)}) collective-permute-start(s16[1032,128]{1,0:T(8,128)(2,1)S(1)} %get-tuple-element.28), channel_id=1, source_target_pairs={{0,24},{8,0},{16,8},{24,16},{1,25},{9,1},{17,9},{25,17},{2,26},{10... | collective-permute-start | bytes 792584 | tf_op jit(solution)/shard_map/ppermute | solution.py:35
  73.8 7.2 %collective-permute-done.6.refs_3_ = s16[1032,128]{1,0:T(8,128)(2,1)S(1)} collective-permute-done((s16[1032,128]{1,0:T(8,128)(2,1)S(1)}, s16[1032,128]{1,0:T(8,128)(2,1)S(1)}, u32[]{:S(2)}, u32[]{:S(2)}) %collective-permute-start.6) | collective-permute-done | bytes 264224 | tf_op jit(solution)/shard_map/ppermute | solution.py:35
  81.0 1.5 %collective-permute-done.7.refs_4_ = s16[1032,128]{1,0:T(8,128)(2,1)S(1)} collective-permute-done((s16[1032,128]{1,0:T(8,128)(2,1)S(1)}, s16[1032,128]{1,0:T(8,128)(2,1)S(1)}, u32[]{:S(2)}, u32[]{:S(2)}) %collective-permute-start.7) | collective-permute-done | bytes 264224 | tf_op jit(solution)/shard_map/ppermute | solution.py:35
  82.5 0.5 middle.1
  83.0 2.7 %collective-permute-start.10 = (s16[264,128]{1,0:T(8,128)(2,1)S(1)}, s16[264,128]{1,0:T(8,128)(2,1)S(1)}, u32[]{:S(2)}, u32[]{:S(2)}) collective-permute-start(s16[264,128]{1,0:T(8,128)(2,1)S(1)} %get-tuple-element.32), channel_id=1, source_target_pairs={{0,3},{1,4},{2,5},{3,6},{4,7},{5,0},{6,1},{7,2},{8,11},{9,12},{10,... | collective-permute-start | bytes 202760 | tf_op jit(solution)/shard_map/ppermute | solution.py:35
  85.9 4.6 %collective-permute-start.12 = (s16[264,128]{1,0:T(8,128)(2,1)S(1)}, s16[264,128]{1,0:T(8,128)(2,1)S(1)}, u32[]{:S(2)}, u32[]{:S(2)}) collective-permute-start(s16[264,128]{1,0:T(8,128)(2,1)S(1)} %get-tuple-element.34), channel_id=1, source_target_pairs={{0,5},{1,6},{2,7},{3,0},{4,1},{5,2},{6,3},{7,4},{8,13},{9,14},{10,... | collective-permute-start | bytes 202760 | tf_op jit(solution)/shard_map/ppermute | solution.py:35
  90.5 2.3 %collective-permute-start.13 = (s16[264,128]{1,0:T(8,128)(2,1)S(1)}, s16[264,128]{1,0:T(8,128)(2,1)S(1)}, u32[]{:S(2)}, u32[]{:S(2)}) collective-permute-start(s16[264,128]{1,0:T(8,128)(2,1)S(1)} %get-tuple-element.35), channel_id=1, source_target_pairs={{0,6},{1,7},{2,0},{3,1},{4,2},{5,3},{6,4},{7,5},{8,14},{9,15},{10,... | collective-permute-start | bytes 202760 | tf_op jit(solution)/shard_map/ppermute | solution.py:35
  92.8 1.1 %collective-permute-start.14 = (s16[264,128]{1,0:T(8,128)(2,1)S(1)}, s16[264,128]{1,0:T(8,128)(2,1)S(1)}, u32[]{:S(2)}, u32[]{:S(2)}) collective-permute-start(s16[264,128]{1,0:T(8,128)(2,1)S(1)} %get-tuple-element.36), channel_id=1, source_target_pairs={{0,7},{1,0},{2,1},{3,2},{4,3},{5,4},{6,5},{7,6},{8,15},{9,8},{10,9... | collective-permute-start | bytes 202760 | tf_op jit(solution)/shard_map/ppermute | solution.py:35
  93.9 0.9 collective-permute-start.8
  94.9 3.7 %collective-permute-done.11.refs_4_ = s16[264,128]{1,0:T(8,128)(2,1)S(1)} collective-permute-done((s16[264,128]{1,0:T(8,128)(2,1)S(1)}, s16[264,128]{1,0:T(8,128)(2,1)S(1)}, u32[]{:S(2)}, u32[]{:S(2)}) %collective-permute-start.11) | collective-permute-done | bytes 67616 | tf_op jit(solution)/shard_map/ppermute | solution.py:35
  98.5 2.8 %list.1 = (s32[32]{0:T(128)}, s32[32]{0:T(128)}, s32[32]{0:T(128)}, s32[32]{0:T(128)S(1)}) custom-call(s32[32,2,128]{2,1,0:T(2,128)S(1)} %all-to-all-done.refs_0_), custom_call_target="tpu_custom_call" | custom-call | tf_op jit(solution)/shard_map/list/pallas_call | solution.py:318
  101.4 3.6 %collective-permute-done.9.refs_2_ = s16[264,128]{1,0:T(8,128)(2,1)S(1)} collective-permute-done((s16[264,128]{1,0:T(8,128)(2,1)S(1)}, s16[264,128]{1,0:T(8,128)(2,1)S(1)}, u32[]{:S(2)}, u32[]{:S(2)}) %collective-permute-start.9) | collective-permute-done | bytes 67616 | tf_op jit(solution)/shard_map/ppermute | solution.py:35
  104.9 0.8 last.1
  105.7 2.6 %keep.1 = bf16[32,128,128]{2,1,0:T(8,128)(2,1)} custom-call(s32[32]{0:T(128)S(1)} %get-tuple-element.37.refs_0_, bf16[64,128,128]{2,1,0:T(8,128)(2,1)} %all-to-all-done.1.refs_1_), custom_call_target="tpu_custom_call" | custom-call | tf_op jit(solution)/shard_map/keep/pallas_call | solution.py:386
  (24 shorter events, 1.1 us)
Async XLA Ops:
  2.1 18.4 %all-to-all-start = ((s32[32,2,128]{2,1,0:T(2,128)}), s32[32,2,128]{2,1,0:T(2,128)S(1)}, u32[]{:S(2)}, u32[]{:S(2)}) async-start(s32[32,2,128]{2,1,0:T(2,128)} %tell.1), calls=%async_computation | async-start | bytes 65536 | tf_op jit(solution)/shard_map/all_to_all | solution.py:296
  22.9 7.5 %copy-start.5 = (bf16[256,128]{1,0:T(8,128)(2,1)S(1)}, bf16[256,128]{1,0:T(8,128)(2,1)}, u32[]{:S(2)}) copy-start(bf16[256,128]{1,0:T(8,128)(2,1)} %param.5) | copy-start | bytes 196612
  22.9 17.8 %copy-start.2 = (s32[64]{0:T(128)S(1)}, s32[64]{0:T(128)}, u32[]{:S(2)}) copy-start(s32[64]{0:T(128)} %refs_0_.3) | copy-start | bytes 772
  22.9 17.8 %copy-start.3 = (s32[64]{0:T(128)S(1)}, s32[64]{0:T(128)}, u32[]{:S(2)}) copy-start(s32[64]{0:T(128)} %refs_1_.3) | copy-start | bytes 772
  22.9 17.8 %copy-start.4 = (s32[64]{0:T(128)S(1)}, s32[64]{0:T(128)}, u32[]{:S(2)}) copy-start(s32[64]{0:T(128)} %refs_2_.3) | copy-start | bytes 772
  23.0 82.8 %all-to-all-start.1 = ((bf16[64,128,128]{2,1,0:T(8,128)(2,1)}), bf16[64,128,128]{2,1,0:T(8,128)(2,1)}, u32[]{:S(2)}, u32[]{:S(2)}) async-start(bf16[64,128,128]{2,1,0:T(8,128)(2,1)} %plan.1), calls=%async_computation.1 | async-start | bytes 4194304 | tf_op jit(solution)/shard_map/all_to_all | solution.py:326
  30.5 5.7 %collective-permute-start = (bf16[2,128,128]{2,1,0:T(8,128)(2,1)S(1)}, bf16[2,128,128]{2,1,0:T(8,128)(2,1)S(1)}, u32[]{:S(2)}, u32[]{:S(2)}) collective-permute-start(bf16[2,128,128]{2,1,0:T(8,128)(2,1)S(1)} %bitcast.1), channel_id=1, source_target_pairs={{0,64},{32,96},{64,128},{96,160},{128,192},{160,224},{192,0},{224,... | collective-permute-start | bytes 196616 | tf_op jit(solution)/shard_map/ppermute | solution.py:295
  32.0 5.8 %collective-permute-start.1 = (bf16[2,128,128]{2,1,0:T(8,128)(2,1)S(1)}, bf16[2,128,128]{2,1,0:T(8,128)(2,1)S(1)}, u32[]{:S(2)}, u32[]{:S(2)}) collective-permute-start(bf16[2,128,128]{2,1,0:T(8,128)(2,1)S(1)} %bitcast.2), channel_id=1, source_target_pairs={{0,128},{32,160},{64,192},{96,224},{128,0},{160,32},{192,64},{224,... | collective-permute-start | bytes 196616 | tf_op jit(solution)/shard_map/ppermute | solution.py:295
  34.8 4.3 %collective-permute-start.2 = (bf16[2,128,128]{2,1,0:T(8,128)(2,1)S(1)}, bf16[2,128,128]{2,1,0:T(8,128)(2,1)S(1)}, u32[]{:S(2)}, u32[]{:S(2)}) collective-permute-start(bf16[2,128,128]{2,1,0:T(8,128)(2,1)S(1)} %bitcast.3), channel_id=1, source_target_pairs={{0,192},{32,224},{64,0},{96,32},{128,64},{160,96},{192,128},{224,1... | collective-permute-start | bytes 196616 | tf_op jit(solution)/shard_map/ppermute | solution.py:295
  39.1 1.6 %collective-permute-start.3 = (bf16[8,128,128]{2,1,0:T(8,128)(2,1)S(1)}, bf16[8,128,128]{2,1,0:T(8,128)(2,1)S(1)}, u32[]{:S(2)}, u32[]{:S(2)}) collective-permute-start(bf16[8,128,128]{2,1,0:T(8,128)(2,1)S(1)} %pad_maximum_fusion.refs_4_), channel_id=1, source_target_pairs={{0,32},{32,0},{64,96},{96,64},{128,160},{160,128},{192,224},{224,1... | collective-permute-start | bytes 786440 | tf_op jit(solution)/shard_map/ppermute | solution.py:298
  44.0 38.5 %copy-start = (f32[16,128,128]{2,1,0:T(8,128)S(1)}, f32[16,128,128]{2,1,0:T(8,128)}, u32[]{:S(2)}) copy-start(f32[16,128,128]{2,1,0:T(8,128)} %get-tuple-element.23.refs_0_) | copy-start | bytes 3145732
  44.0 24.2 %collective-permute-start.4 = (s16[2064,128]{1,0:T(8,128)(2,1)S(1)}, s16[2064,128]{1,0:T(8,128)(2,1)S(1)}, u32[]{:S(2)}, u32[]{:S(2)}) collective-permute-start(s16[2064,128]{1,0:T(8,128)(2,1)S(1)} %get-tuple-element.24), channel_id=1, source_target_pairs={{0,8},{8,16},{16,24},{24,0},{1,9},{9,17},{17,25},{25,1},{2,10},{10... | collective-permute-start | bytes 1585160 | tf_op jit(solution)/shard_map/ppermute | solution.py:35
  44.5 25.5 %collective-permute-start.5 = (s16[2064,128]{1,0:T(8,128)(2,1)S(1)}, s16[2064,128]{1,0:T(8,128)(2,1)S(1)}, u32[]{:S(2)}, u32[]{:S(2)}) collective-permute-start(s16[2064,128]{1,0:T(8,128)(2,1)S(1)} %get-tuple-element.25), channel_id=1, source_target_pairs={{0,24},{8,0},{16,8},{24,16},{1,25},{9,1},{17,9},{25,17},{2,26},{10... | collective-permute-start | bytes 1585160 | tf_op jit(solution)/shard_map/ppermute | solution.py:35
  70.0 1.2 %copy-start.1 = (f32[16,128,128]{2,1,0:T(8,128)S(1)}, f32[16,128,128]{2,1,0:T(8,128)}, u32[]{:S(2)}) copy-start(f32[16,128,128]{2,1,0:T(8,128)} %get-tuple-element.26.refs_0_) | copy-start | bytes 3145732
  71.7 9.3 %collective-permute-start.6 = (s16[1032,128]{1,0:T(8,128)(2,1)S(1)}, s16[1032,128]{1,0:T(8,128)(2,1)S(1)}, u32[]{:S(2)}, u32[]{:S(2)}) collective-permute-start(s16[1032,128]{1,0:T(8,128)(2,1)S(1)} %get-tuple-element.27), channel_id=1, source_target_pairs={{0,8},{8,16},{16,24},{24,0},{1,9},{9,17},{17,25},{25,1},{2,10},{10... | collective-permute-start | bytes 792584 | tf_op jit(solution)/shard_map/ppermute | solution.py:35
  72.1 10.4 %collective-permute-start.7 = (s16[1032,128]{1,0:T(8,128)(2,1)S(1)}, s16[1032,128]{1,0:T(8,128)(2,1)S(1)}, u32[]{:S(2)}, u32[]{:S(2)}) collective-permute-start(s16[1032,128]{1,0:T(8,128)(2,1)S(1)} %get-tuple-element.28), channel_id=1, source_target_pairs={{0,24},{8,0},{16,8},{24,16},{1,25},{9,1},{17,9},{25,17},{2,26},{10... | collective-permute-start | bytes 792584 | tf_op jit(solution)/shard_map/ppermute | solution.py:35
  83.0 10.9 %collective-permute-start.10 = (s16[264,128]{1,0:T(8,128)(2,1)S(1)}, s16[264,128]{1,0:T(8,128)(2,1)S(1)}, u32[]{:S(2)}, u32[]{:S(2)}) collective-permute-start(s16[264,128]{1,0:T(8,128)(2,1)S(1)} %get-tuple-element.32), channel_id=1, source_target_pairs={{0,3},{1,4},{2,5},{3,6},{4,7},{5,0},{6,1},{7,2},{8,11},{9,12},{10,... | collective-permute-start | bytes 202760 | tf_op jit(solution)/shard_map/ppermute | solution.py:35
  85.8 12.7 %collective-permute-start.11 = (s16[264,128]{1,0:T(8,128)(2,1)S(1)}, s16[264,128]{1,0:T(8,128)(2,1)S(1)}, u32[]{:S(2)}, u32[]{:S(2)}) collective-permute-start(s16[264,128]{1,0:T(8,128)(2,1)S(1)} %get-tuple-element.33), channel_id=1, source_target_pairs={{0,4},{1,5},{2,6},{3,7},{4,0},{5,1},{6,2},{7,3},{8,12},{9,13},{10,... | collective-permute-start | bytes 202760 | tf_op jit(solution)/shard_map/ppermute | solution.py:35
  85.9 15.5 %collective-permute-start.12 = (s16[264,128]{1,0:T(8,128)(2,1)S(1)}, s16[264,128]{1,0:T(8,128)(2,1)S(1)}, u32[]{:S(2)}, u32[]{:S(2)}) collective-permute-start(s16[264,128]{1,0:T(8,128)(2,1)S(1)} %get-tuple-element.34), channel_id=1, source_target_pairs={{0,5},{1,6},{2,7},{3,0},{4,1},{5,2},{6,3},{7,4},{8,13},{9,14},{10,... | collective-permute-start | bytes 202760 | tf_op jit(solution)/shard_map/ppermute | solution.py:35
  90.5 10.9 %collective-permute-start.13 = (s16[264,128]{1,0:T(8,128)(2,1)S(1)}, s16[264,128]{1,0:T(8,128)(2,1)S(1)}, u32[]{:S(2)}, u32[]{:S(2)}) collective-permute-start(s16[264,128]{1,0:T(8,128)(2,1)S(1)} %get-tuple-element.35), channel_id=1, source_target_pairs={{0,6},{1,7},{2,0},{3,1},{4,2},{5,3},{6,4},{7,5},{8,14},{9,15},{10,... | collective-permute-start | bytes 202760 | tf_op jit(solution)/shard_map/ppermute | solution.py:35
  92.8 8.5 %collective-permute-start.14 = (s16[264,128]{1,0:T(8,128)(2,1)S(1)}, s16[264,128]{1,0:T(8,128)(2,1)S(1)}, u32[]{:S(2)}, u32[]{:S(2)}) collective-permute-start(s16[264,128]{1,0:T(8,128)(2,1)S(1)} %get-tuple-element.36), channel_id=1, source_target_pairs={{0,7},{1,0},{2,1},{3,2},{4,3},{5,4},{6,5},{7,6},{8,15},{9,8},{10,9... | collective-permute-start | bytes 202760 | tf_op jit(solution)/shard_map/ppermute | solution.py:35
  93.9 7.4 %collective-permute-start.8 = (s16[264,128]{1,0:T(8,128)(2,1)S(1)}, s16[264,128]{1,0:T(8,128)(2,1)S(1)}, u32[]{:S(2)}, u32[]{:S(2)}) collective-permute-start(s16[264,128]{1,0:T(8,128)(2,1)S(1)} %get-tuple-element.30), channel_id=1, source_target_pairs={{0,1},{1,2},{2,3},{3,4},{4,5},{5,6},{6,7},{7,0},{8,9},{9,10},{10,1... | collective-permute-start | bytes 202760 | tf_op jit(solution)/shard_map/ppermute | solution.py:35
  98.5 6.4 %collective-permute-start.9 = (s16[264,128]{1,0:T(8,128)(2,1)S(1)}, s16[264,128]{1,0:T(8,128)(2,1)S(1)}, u32[]{:S(2)}, u32[]{:S(2)}) collective-permute-start(s16[264,128]{1,0:T(8,128)(2,1)S(1)} %get-tuple-element.31), channel_id=1, source_target_pairs={{0,2},{1,3},{2,4},{3,5},{4,6},{5,7},{6,0},{7,1},{8,10},{9,11},{10,... | collective-permute-start | bytes 202760 | tf_op jit(solution)/shard_map/ppermute | solution.py:35

commit v5 on v4

--- a/solution.py
+++ b/solution.py
@@ -114,13 +114,23 @@
     lax.fori_loop(0, peers, source, jnp.int32(0))
 
 
-def keep_kernel(owned, slot_ref, got_ref, out_ref, sems):
-    def start(k, carry):
-        pltpu.make_async_copy(got_ref.at[slot_ref[k]], out_ref.at[k], sems.at[0]).start()
-        return carry
-
-    lax.fori_loop(0, owned, start, 0)
-    pltpu.make_async_copy(got_ref.at[pl.ds(0, owned)], out_ref, sems.at[0]).wait()
+def keep_kernel(owned, slot_ref, got_ref, out_ref, held, sems, out_sems):
+    groups = sems.shape[0]
+    size = owned // groups
+
+    def piece(ref, g):
+        return ref.at[pl.ds(g * size, size)]
+
+    for k in range(owned):
+        pltpu.make_async_copy(got_ref.at[slot_ref[k]], held.at[k], sems.at[k // size]).start()
+    leaving = [
+        pltpu.make_async_copy(piece(held, g), piece(out_ref, g), out_sems.at[g]) for g in range(groups)
+    ]
+    for g, c in enumerate(leaving):
+        pltpu.make_async_copy(piece(got_ref, g), piece(held, g), sems.at[g]).wait()
+        c.start()
+    for c in leaving:
+        c.wait()
 
 
 def coded(x, q_ref, exps_ref, at, row):
@@ -385,13 +395,17 @@
 
     moved_vals = pl.pallas_call(
         lambda *refs: keep_kernel(owned, *refs),
-        in_specs=[SMEM, VMEM],
+        in_specs=[SMEM, ANY],
         out_specs=ANY,
         out_shape=jax.ShapeDtypeStruct((owned, *tile_vals.shape[1:]), tile_vals.dtype),
-        scratch_shapes=[pltpu.SemaphoreType.DMA((1,))],
+        scratch_shapes=[
+            pltpu.VMEM((owned, *tile_vals.shape[1:]), tile_vals.dtype),
+            pltpu.SemaphoreType.DMA((4,)),
+            pltpu.SemaphoreType.DMA((4,)),
+        ],
         compiler_params=limit(4),
         name="keep",
-    )(kept, in_vmem(got))
+    )(kept, in_hbm(got))
     return (product, moved_vals, moved_row, moved_col, moved_work)
 
 

time: 109 us -> 109 us (level)
  no operation moved by 1% of the time
where the time goes in v5:
time: 109 us; the launch traced here: 108 us
  waiting for transfers between devices  49.8 us (46%)
  starting transfers between devices  40.4 us (37%)
  Pallas kernels  15.9 us (15%)
  local copies, waits for them, and re-layouts  1.26 us (1%)
    ppermute x11, waiting for transfers between devices, shifted(): lax.ppermute(array, axis, [(i, (i + by) % size) for i in range(size)])  39.8 us
    ppermute x11, starting transfers between devices, shifted(): lax.ppermute(array, axis, [(i, (i + by) % size) for i in range(size)])  16 us
    all_to_all x1, starting transfers between devices, on_device(): meta = lax.all_to_all(told, GY, split_axis=0, concat_axis=0, tiled=True)  11.1 us
    all_to_all x1, starting transfers between devices, on_device(): got = lax.all_to_all(sent, GY, split_axis=0, concat_axis=0, tiled=True)  7.49 us
    ppermute x3, starting transfers between devices, on_device(): lax.ppermute(mine[0], 'gx', [(i, (i + cores * k) % gx) for i in range(gx)])  5.73 us
    all_to_all x1, waiting for transfers between devices, on_device(): meta = lax.all_to_all(told, GY, split_axis=0, concat_axis=0, tiled=True)  5.68 us
    pallas_call x1, Pallas kernels, on_device(): pl.pallas_call(lambda *refs: product_kernel(gx, peers, ny, steps, *refs),...  3.27 us
    ppermute x3, waiting for transfers between devices, on_device(): lax.ppermute(mine[0], 'gx', [(i, (i + cores * k) % gx) for i in range(gx)])  2.83 us
  transfers between devices with their start and end apart: 17, of which 10 were waited for; matrix products, arithmetic and copies ran while one was open for 0% of the time, Pallas kernels for 9%

profile of v5, /device:TPU:56, one launch (start us, length us, event | category | flops | bytes accessed | tf_op | source)
XLA Modules:
  0.0 108.2 jit_solution(13958794631197108674)
XLA Ops:
  0.6 1.4 %tell.1 = s32[32,2,128]{2,1,0:T(2,128)} custom-call(s32[64]{0:T(128)} %refs_0_.3, s32[64]{0:T(128)} %refs_1_.3, s32[64]{0:T(128)} %refs_2_.3), custom_call_target="tpu_custom_call" | custom-call | tf_op jit(solution)/shard_map/tell/pallas_call | solution.py:292
  2.1 11.1 %all-to-all-start = ((s32[32,2,128]{2,1,0:T(2,128)}), s32[32,2,128]{2,1,0:T(2,128)S(1)}, u32[]{:S(2)}, u32[]{:S(2)}) async-start(s32[32,2,128]{2,1,0:T(2,128)} %tell.1), calls=%async_computation | async-start | bytes 65536 | tf_op jit(solution)/shard_map/all_to_all | solution.py:306
  13.2 1.6 %stage.1.refs_3_.refs_1_ = bf16[64,128,128]{2,1,0:T(8,128)(2,1)S(1)} custom-call(bf16[64,128,128]{2,1,0:T(8,128)(2,1)} %vals_ref.1), custom_call_target="tpu_custom_call" | custom-call | tf_op jit(solution)/shard_map/stage/pallas_call | solution.py:309
  14.7 5.7 %all-to-all-done.refs_0_ = s32[32,2,128]{2,1,0:T(2,128)S(1)} async-done(((s32[32,2,128]{2,1,0:T(2,128)}), s32[32,2,128]{2,1,0:T(2,128)S(1)}, u32[]{:S(2)}, u32[]{:S(2)}) %all-to-all-start) | async-done | bytes 32800 | tf_op jit(solution)/shard_map/all_to_all | solution.py:306
  20.4 2.5 %plan.1 = bf16[64,128,128]{2,1,0:T(8,128)(2,1)} custom-call(s32[32,2,128]{2,1,0:T(2,128)S(1)} %all-to-all-done.refs_0_, bf16[64,128,128]{2,1,0:T(8,128)(2,1)S(1)} %stage.1.refs_3_.refs_1_), custom_call_target="tpu_custom_call" | custom-call | tf_op jit(solution)/shard_map/plan/pallas_call | solution.py:319
  23.0 7.5 %all-to-all-start.1 = ((bf16[64,128,128]{2,1,0:T(8,128)(2,1)}), bf16[64,128,128]{2,1,0:T(8,128)(2,1)}, u32[]{:S(2)}, u32[]{:S(2)}) async-start(bf16[64,128,128]{2,1,0:T(8,128)(2,1)} %plan.1), calls=%async_computation.1 | async-start | bytes 4194304 | tf_op jit(solution)/shard_map/all_to_all | solution.py:336
  30.5 1.6 %collective-permute-start = (bf16[2,128,128]{2,1,0:T(8,128)(2,1)S(1)}, bf16[2,128,128]{2,1,0:T(8,128)(2,1)S(1)}, u32[]{:S(2)}, u32[]{:S(2)}) collective-permute-start(bf16[2,128,128]{2,1,0:T(8,128)(2,1)S(1)} %bitcast.1), channel_id=1, source_target_pairs={{0,64},{32,96},{64,128},{96,160},{128,192},{160,224},{192,0},{224,... | collective-permute-start | bytes 196616 | tf_op jit(solution)/shard_map/ppermute | solution.py:305
  32.0 2.7 %collective-permute-start.1 = (bf16[2,128,128]{2,1,0:T(8,128)(2,1)S(1)}, bf16[2,128,128]{2,1,0:T(8,128)(2,1)S(1)}, u32[]{:S(2)}, u32[]{:S(2)}) collective-permute-start(bf16[2,128,128]{2,1,0:T(8,128)(2,1)S(1)} %bitcast.2), channel_id=1, source_target_pairs={{0,128},{32,160},{64,192},{96,224},{128,0},{160,32},{192,64},{224,... | collective-permute-start | bytes 196616 | tf_op jit(solution)/shard_map/ppermute | solution.py:305
  34.8 1.4 %collective-permute-start.2 = (bf16[2,128,128]{2,1,0:T(8,128)(2,1)S(1)}, bf16[2,128,128]{2,1,0:T(8,128)(2,1)S(1)}, u32[]{:S(2)}, u32[]{:S(2)}) collective-permute-start(bf16[2,128,128]{2,1,0:T(8,128)(2,1)S(1)} %bitcast.3), channel_id=1, source_target_pairs={{0,192},{32,224},{64,0},{96,32},{128,64},{160,96},{192,128},{224,1... | collective-permute-start | bytes 196616 | tf_op jit(solution)/shard_map/ppermute | solution.py:305
  36.2 1.6 %collective-permute-done.1 = bf16[2,128,128]{2,1,0:T(8,128)(2,1)S(1)} collective-permute-done((bf16[2,128,128]{2,1,0:T(8,128)(2,1)S(1)}, bf16[2,128,128]{2,1,0:T(8,128)(2,1)S(1)}, u32[]{:S(2)}, u32[]{:S(2)}) %collective-permute-start.1) | collective-permute-done | bytes 65568 | tf_op jit(solution)/shard_map/ppermute | solution.py:305
  37.8 1.2 %collective-permute-done.2 = bf16[2,128,128]{2,1,0:T(8,128)(2,1)S(1)} collective-permute-done((bf16[2,128,128]{2,1,0:T(8,128)(2,1)S(1)}, bf16[2,128,128]{2,1,0:T(8,128)(2,1)S(1)}, u32[]{:S(2)}, u32[]{:S(2)}) %collective-permute-start.2) | collective-permute-done | bytes 65568 | tf_op jit(solution)/shard_map/ppermute | solution.py:305
  39.2 1.5 %collective-permute-done.3.refs_5_ = bf16[8,128,128]{2,1,0:T(8,128)(2,1)S(1)} collective-permute-done((bf16[8,128,128]{2,1,0:T(8,128)(2,1)S(1)}, bf16[8,128,128]{2,1,0:T(8,128)(2,1)S(1)}, u32[]{:S(2)}, u32[]{:S(2)}) %collective-permute-start.3) | collective-permute-done | bytes 262176 | tf_op jit(solution)/shard_map/ppermute | solution.py:308
  40.7 3.3 %products.1 = (f32[16,128,128]{2,1,0:T(8,128)}, f32[16,128,128]{2,1,0:T(8,128)}, s16[2064,128]{1,0:T(8,128)(2,1)S(1)}, s16[2064,128]{1,0:T(8,128)(2,1)S(1)}) custom-call(s32[64]{0:T(128)S(1)} %copy-done.2, s32[64]{0:T(128)S(1)} %copy-done.3, s32[64]{0:T(128)S(1)} %copy-done.4, bf16[64,128,128]{2,1,0:T(8,128)(2,1)S(1)} %stage.1.refs_3_.refs_1_, ...), custom_call_target="tpu_custom_call" | custom-call | tf_op jit(solution)/shard_map/products/pallas_call | solution.py:346
  44.5 1.6 %collective-permute-start.5 = (s16[2064,128]{1,0:T(8,128)(2,1)S(1)}, s16[2064,128]{1,0:T(8,128)(2,1)S(1)}, u32[]{:S(2)}, u32[]{:S(2)}) collective-permute-start(s16[2064,128]{1,0:T(8,128)(2,1)S(1)} %get-tuple-element.25), channel_id=1, source_target_pairs={{0,24},{8,0},{16,8},{24,16},{1,25},{9,1},{17,9},{25,17},{2,26},{10... | collective-permute-start | bytes 1585160 | tf_op jit(solution)/shard_map/ppermute | solution.py:35
  46.1 22.1 %collective-permute-done.4.refs_1_ = s16[2064,128]{1,0:T(8,128)(2,1)S(1)} collective-permute-done((s16[2064,128]{1,0:T(8,128)(2,1)S(1)}, s16[2064,128]{1,0:T(8,128)(2,1)S(1)}, u32[]{:S(2)}, u32[]{:S(2)}) %collective-permute-start.4) | collective-permute-done | bytes 528416 | tf_op jit(solution)/shard_map/ppermute | solution.py:35
  68.2 1.7 %collective-permute-done.5.refs_2_ = s16[2064,128]{1,0:T(8,128)(2,1)S(1)} collective-permute-done((s16[2064,128]{1,0:T(8,128)(2,1)S(1)}, s16[2064,128]{1,0:T(8,128)(2,1)S(1)}, u32[]{:S(2)}, u32[]{:S(2)}) %collective-permute-start.5) | collective-permute-done | bytes 528416 | tf_op jit(solution)/shard_map/ppermute | solution.py:35
  70.0 1.2 %copy-done.1 = f32[16,128,128]{2,1,0:T(8,128)S(1)} copy-done((f32[16,128,128]{2,1,0:T(8,128)S(1)}, f32[16,128,128]{2,1,0:T(8,128)}, u32[]{:S(2)}) %copy-start.1) | copy-done | bytes 1048600
  71.2 0.5 relay.1
  72.1 1.7 %collective-permute-start.7 = (s16[1032,128]{1,0:T(8,128)(2,1)S(1)}, s16[1032,128]{1,0:T(8,128)(2,1)S(1)}, u32[]{:S(2)}, u32[]{:S(2)}) collective-permute-start(s16[1032,128]{1,0:T(8,128)(2,1)S(1)} %get-tuple-element.28), channel_id=1, source_target_pairs={{0,24},{8,0},{16,8},{24,16},{1,25},{9,1},{17,9},{25,17},{2,26},{10... | collective-permute-start | bytes 792584 | tf_op jit(solution)/shard_map/ppermute | solution.py:35
  73.8 7.2 %collective-permute-done.6.refs_3_ = s16[1032,128]{1,0:T(8,128)(2,1)S(1)} collective-permute-done((s16[1032,128]{1,0:T(8,128)(2,1)S(1)}, s16[1032,128]{1,0:T(8,128)(2,1)S(1)}, u32[]{:S(2)}, u32[]{:S(2)}) %collective-permute-start.6) | collective-permute-done | bytes 264224 | tf_op jit(solution)/shard_map/ppermute | solution.py:35
  81.0 1.5 %collective-permute-done.7.refs_4_ = s16[1032,128]{1,0:T(8,128)(2,1)S(1)} collective-permute-done((s16[1032,128]{1,0:T(8,128)(2,1)S(1)}, s16[1032,128]{1,0:T(8,128)(2,1)S(1)}, u32[]{:S(2)}, u32[]{:S(2)}) %collective-permute-start.7) | collective-permute-done | bytes 264224 | tf_op jit(solution)/shard_map/ppermute | solution.py:35
  82.5 0.5 middle.1
  83.0 2.7 %collective-permute-start.10 = (s16[264,128]{1,0:T(8,128)(2,1)S(1)}, s16[264,128]{1,0:T(8,128)(2,1)S(1)}, u32[]{:S(2)}, u32[]{:S(2)}) collective-permute-start(s16[264,128]{1,0:T(8,128)(2,1)S(1)} %get-tuple-element.32), channel_id=1, source_target_pairs={{0,3},{1,4},{2,5},{3,6},{4,7},{5,0},{6,1},{7,2},{8,11},{9,12},{10,... | collective-permute-start | bytes 202760 | tf_op jit(solution)/shard_map/ppermute | solution.py:35
  85.9 4.6 %collective-permute-start.12 = (s16[264,128]{1,0:T(8,128)(2,1)S(1)}, s16[264,128]{1,0:T(8,128)(2,1)S(1)}, u32[]{:S(2)}, u32[]{:S(2)}) collective-permute-start(s16[264,128]{1,0:T(8,128)(2,1)S(1)} %get-tuple-element.34), channel_id=1, source_target_pairs={{0,5},{1,6},{2,7},{3,0},{4,1},{5,2},{6,3},{7,4},{8,13},{9,14},{10,... | collective-permute-start | bytes 202760 | tf_op jit(solution)/shard_map/ppermute | solution.py:35
  90.5 2.3 %collective-permute-start.13 = (s16[264,128]{1,0:T(8,128)(2,1)S(1)}, s16[264,128]{1,0:T(8,128)(2,1)S(1)}, u32[]{:S(2)}, u32[]{:S(2)}) collective-permute-start(s16[264,128]{1,0:T(8,128)(2,1)S(1)} %get-tuple-element.35), channel_id=1, source_target_pairs={{0,6},{1,7},{2,0},{3,1},{4,2},{5,3},{6,4},{7,5},{8,14},{9,15},{10,... | collective-permute-start | bytes 202760 | tf_op jit(solution)/shard_map/ppermute | solution.py:35
  92.8 1.1 %collective-permute-start.14 = (s16[264,128]{1,0:T(8,128)(2,1)S(1)}, s16[264,128]{1,0:T(8,128)(2,1)S(1)}, u32[]{:S(2)}, u32[]{:S(2)}) collective-permute-start(s16[264,128]{1,0:T(8,128)(2,1)S(1)} %get-tuple-element.36), channel_id=1, source_target_pairs={{0,7},{1,0},{2,1},{3,2},{4,3},{5,4},{6,5},{7,6},{8,15},{9,8},{10,9... | collective-permute-start | bytes 202760 | tf_op jit(solution)/shard_map/ppermute | solution.py:35
  93.9 0.9 collective-permute-start.8
  94.9 3.7 %collective-permute-done.11.refs_4_ = s16[264,128]{1,0:T(8,128)(2,1)S(1)} collective-permute-done((s16[264,128]{1,0:T(8,128)(2,1)S(1)}, s16[264,128]{1,0:T(8,128)(2,1)S(1)}, u32[]{:S(2)}, u32[]{:S(2)}) %collective-permute-start.11) | collective-permute-done | bytes 67616 | tf_op jit(solution)/shard_map/ppermute | solution.py:35
  98.5 2.8 %list.1 = (s32[32]{0:T(128)}, s32[32]{0:T(128)}, s32[32]{0:T(128)}, s32[32]{0:T(128)S(1)}) custom-call(s32[32,2,128]{2,1,0:T(2,128)S(1)} %all-to-all-done.refs_0_), custom_call_target="tpu_custom_call" | custom-call | tf_op jit(solution)/shard_map/list/pallas_call | solution.py:328
  101.4 3.6 %collective-permute-done.9.refs_2_ = s16[264,128]{1,0:T(8,128)(2,1)S(1)} collective-permute-done((s16[264,128]{1,0:T(8,128)(2,1)S(1)}, s16[264,128]{1,0:T(8,128)(2,1)S(1)}, u32[]{:S(2)}, u32[]{:S(2)}) %collective-permute-start.9) | collective-permute-done | bytes 67616 | tf_op jit(solution)/shard_map/ppermute | solution.py:35
  104.9 0.8 last.1
  105.7 2.5 %keep.1 = bf16[32,128,128]{2,1,0:T(8,128)(2,1)} custom-call(s32[32]{0:T(128)S(1)} %get-tuple-element.37.refs_0_, bf16[64,128,128]{2,1,0:T(8,128)(2,1)} %all-to-all-done.1.refs_1_), custom_call_target="tpu_custom_call" | custom-call | tf_op jit(solution)/shard_map/keep/pallas_call | solution.py:396
  (24 shorter events, 1.1 us)
Async XLA Ops:
  2.1 18.4 %all-to-all-start = ((s32[32,2,128]{2,1,0:T(2,128)}), s32[32,2,128]{2,1,0:T(2,128)S(1)}, u32[]{:S(2)}, u32[]{:S(2)}) async-start(s32[32,2,128]{2,1,0:T(2,128)} %tell.1), calls=%async_computation | async-start | bytes 65536 | tf_op jit(solution)/shard_map/all_to_all | solution.py:306
  22.9 7.5 %copy-start.5 = (bf16[256,128]{1,0:T(8,128)(2,1)S(1)}, bf16[256,128]{1,0:T(8,128)(2,1)}, u32[]{:S(2)}) copy-start(bf16[256,128]{1,0:T(8,128)(2,1)} %param.5) | copy-start | bytes 196612
  22.9 17.8 %copy-start.2 = (s32[64]{0:T(128)S(1)}, s32[64]{0:T(128)}, u32[]{:S(2)}) copy-start(s32[64]{0:T(128)} %refs_0_.3) | copy-start | bytes 772
  22.9 17.8 %copy-start.3 = (s32[64]{0:T(128)S(1)}, s32[64]{0:T(128)}, u32[]{:S(2)}) copy-start(s32[64]{0:T(128)} %refs_1_.3) | copy-start | bytes 772
  22.9 17.8 %copy-start.4 = (s32[64]{0:T(128)S(1)}, s32[64]{0:T(128)}, u32[]{:S(2)}) copy-start(s32[64]{0:T(128)} %refs_2_.3) | copy-start | bytes 772
  23.0 82.8 %all-to-all-start.1 = ((bf16[64,128,128]{2,1,0:T(8,128)(2,1)}), bf16[64,128,128]{2,1,0:T(8,128)(2,1)}, u32[]{:S(2)}, u32[]{:S(2)}) async-start(bf16[64,128,128]{2,1,0:T(8,128)(2,1)} %plan.1), calls=%async_computation.1 | async-start | bytes 4194304 | tf_op jit(solution)/shard_map/all_to_all | solution.py:336
  30.5 5.7 %collective-permute-start = (bf16[2,128,128]{2,1,0:T(8,128)(2,1)S(1)}, bf16[2,128,128]{2,1,0:T(8,128)(2,1)S(1)}, u32[]{:S(2)}, u32[]{:S(2)}) collective-permute-start(bf16[2,128,128]{2,1,0:T(8,128)(2,1)S(1)} %bitcast.1), channel_id=1, source_target_pairs={{0,64},{32,96},{64,128},{96,160},{128,192},{160,224},{192,0},{224,... | collective-permute-start | bytes 196616 | tf_op jit(solution)/shard_map/ppermute | solution.py:305
  32.0 5.8 %collective-permute-start.1 = (bf16[2,128,128]{2,1,0:T(8,128)(2,1)S(1)}, bf16[2,128,128]{2,1,0:T(8,128)(2,1)S(1)}, u32[]{:S(2)}, u32[]{:S(2)}) collective-permute-start(bf16[2,128,128]{2,1,0:T(8,128)(2,1)S(1)} %bitcast.2), channel_id=1, source_target_pairs={{0,128},{32,160},{64,192},{96,224},{128,0},{160,32},{192,64},{224,... | collective-permute-start | bytes 196616 | tf_op jit(solution)/shard_map/ppermute | solution.py:305
  34.8 4.3 %collective-permute-start.2 = (bf16[2,128,128]{2,1,0:T(8,128)(2,1)S(1)}, bf16[2,128,128]{2,1,0:T(8,128)(2,1)S(1)}, u32[]{:S(2)}, u32[]{:S(2)}) collective-permute-start(bf16[2,128,128]{2,1,0:T(8,128)(2,1)S(1)} %bitcast.3), channel_id=1, source_target_pairs={{0,192},{32,224},{64,0},{96,32},{128,64},{160,96},{192,128},{224,1... | collective-permute-start | bytes 196616 | tf_op jit(solution)/shard_map/ppermute | solution.py:305
  39.1 1.6 %collective-permute-start.3 = (bf16[8,128,128]{2,1,0:T(8,128)(2,1)S(1)}, bf16[8,128,128]{2,1,0:T(8,128)(2,1)S(1)}, u32[]{:S(2)}, u32[]{:S(2)}) collective-permute-start(bf16[8,128,128]{2,1,0:T(8,128)(2,1)S(1)} %pad_maximum_fusion.refs_4_), channel_id=1, source_target_pairs={{0,32},{32,0},{64,96},{96,64},{128,160},{160,128},{192,224},{224,1... | collective-permute-start | bytes 786440 | tf_op jit(solution)/shard_map/ppermute | solution.py:308
  44.0 38.5 %copy-start = (f32[16,128,128]{2,1,0:T(8,128)S(1)}, f32[16,128,128]{2,1,0:T(8,128)}, u32[]{:S(2)}) copy-start(f32[16,128,128]{2,1,0:T(8,128)} %get-tuple-element.23.refs_0_) | copy-start | bytes 3145732
  44.0 24.2 %collective-permute-start.4 = (s16[2064,128]{1,0:T(8,128)(2,1)S(1)}, s16[2064,128]{1,0:T(8,128)(2,1)S(1)}, u32[]{:S(2)}, u32[]{:S(2)}) collective-permute-start(s16[2064,128]{1,0:T(8,128)(2,1)S(1)} %get-tuple-element.24), channel_id=1, source_target_pairs={{0,8},{8,16},{16,24},{24,0},{1,9},{9,17},{17,25},{25,1},{2,10},{10... | collective-permute-start | bytes 1585160 | tf_op jit(solution)/shard_map/ppermute | solution.py:35
  44.5 25.5 %collective-permute-start.5 = (s16[2064,128]{1,0:T(8,128)(2,1)S(1)}, s16[2064,128]{1,0:T(8,128)(2,1)S(1)}, u32[]{:S(2)}, u32[]{:S(2)}) collective-permute-start(s16[2064,128]{1,0:T(8,128)(2,1)S(1)} %get-tuple-element.25), channel_id=1, source_target_pairs={{0,24},{8,0},{16,8},{24,16},{1,25},{9,1},{17,9},{25,17},{2,26},{10... | collective-permute-start | bytes 1585160 | tf_op jit(solution)/shard_map/ppermute | solution.py:35
  70.0 1.2 %copy-start.1 = (f32[16,128,128]{2,1,0:T(8,128)S(1)}, f32[16,128,128]{2,1,0:T(8,128)}, u32[]{:S(2)}) copy-start(f32[16,128,128]{2,1,0:T(8,128)} %get-tuple-element.26.refs_0_) | copy-start | bytes 3145732
  71.7 9.3 %collective-permute-start.6 = (s16[1032,128]{1,0:T(8,128)(2,1)S(1)}, s16[1032,128]{1,0:T(8,128)(2,1)S(1)}, u32[]{:S(2)}, u32[]{:S(2)}) collective-permute-start(s16[1032,128]{1,0:T(8,128)(2,1)S(1)} %get-tuple-element.27), channel_id=1, source_target_pairs={{0,8},{8,16},{16,24},{24,0},{1,9},{9,17},{17,25},{25,1},{2,10},{10... | collective-permute-start | bytes 792584 | tf_op jit(solution)/shard_map/ppermute | solution.py:35
  72.1 10.4 %collective-permute-start.7 = (s16[1032,128]{1,0:T(8,128)(2,1)S(1)}, s16[1032,128]{1,0:T(8,128)(2,1)S(1)}, u32[]{:S(2)}, u32[]{:S(2)}) collective-permute-start(s16[1032,128]{1,0:T(8,128)(2,1)S(1)} %get-tuple-element.28), channel_id=1, source_target_pairs={{0,24},{8,0},{16,8},{24,16},{1,25},{9,1},{17,9},{25,17},{2,26},{10... | collective-permute-start | bytes 792584 | tf_op jit(solution)/shard_map/ppermute | solution.py:35
  83.0 10.9 %collective-permute-start.10 = (s16[264,128]{1,0:T(8,128)(2,1)S(1)}, s16[264,128]{1,0:T(8,128)(2,1)S(1)}, u32[]{:S(2)}, u32[]{:S(2)}) collective-permute-start(s16[264,128]{1,0:T(8,128)(2,1)S(1)} %get-tuple-element.32), channel_id=1, source_target_pairs={{0,3},{1,4},{2,5},{3,6},{4,7},{5,0},{6,1},{7,2},{8,11},{9,12},{10,... | collective-permute-start | bytes 202760 | tf_op jit(solution)/shard_map/ppermute | solution.py:35
  85.8 12.7 %collective-permute-start.11 = (s16[264,128]{1,0:T(8,128)(2,1)S(1)}, s16[264,128]{1,0:T(8,128)(2,1)S(1)}, u32[]{:S(2)}, u32[]{:S(2)}) collective-permute-start(s16[264,128]{1,0:T(8,128)(2,1)S(1)} %get-tuple-element.33), channel_id=1, source_target_pairs={{0,4},{1,5},{2,6},{3,7},{4,0},{5,1},{6,2},{7,3},{8,12},{9,13},{10,... | collective-permute-start | bytes 202760 | tf_op jit(solution)/shard_map/ppermute | solution.py:35
  85.9 15.5 %collective-permute-start.12 = (s16[264,128]{1,0:T(8,128)(2,1)S(1)}, s16[264,128]{1,0:T(8,128)(2,1)S(1)}, u32[]{:S(2)}, u32[]{:S(2)}) collective-permute-start(s16[264,128]{1,0:T(8,128)(2,1)S(1)} %get-tuple-element.34), channel_id=1, source_target_pairs={{0,5},{1,6},{2,7},{3,0},{4,1},{5,2},{6,3},{7,4},{8,13},{9,14},{10,... | collective-permute-start | bytes 202760 | tf_op jit(solution)/shard_map/ppermute | solution.py:35
  90.5 10.9 %collective-permute-start.13 = (s16[264,128]{1,0:T(8,128)(2,1)S(1)}, s16[264,128]{1,0:T(8,128)(2,1)S(1)}, u32[]{:S(2)}, u32[]{:S(2)}) collective-permute-start(s16[264,128]{1,0:T(8,128)(2,1)S(1)} %get-tuple-element.35), channel_id=1, source_target_pairs={{0,6},{1,7},{2,0},{3,1},{4,2},{5,3},{6,4},{7,5},{8,14},{9,15},{10,... | collective-permute-start | bytes 202760 | tf_op jit(solution)/shard_map/ppermute | solution.py:35
  92.8 8.5 %collective-permute-start.14 = (s16[264,128]{1,0:T(8,128)(2,1)S(1)}, s16[264,128]{1,0:T(8,128)(2,1)S(1)}, u32[]{:S(2)}, u32[]{:S(2)}) collective-permute-start(s16[264,128]{1,0:T(8,128)(2,1)S(1)} %get-tuple-element.36), channel_id=1, source_target_pairs={{0,7},{1,0},{2,1},{3,2},{4,3},{5,4},{6,5},{7,6},{8,15},{9,8},{10,9... | collective-permute-start | bytes 202760 | tf_op jit(solution)/shard_map/ppermute | solution.py:35
  93.9 7.4 %collective-permute-start.8 = (s16[264,128]{1,0:T(8,128)(2,1)S(1)}, s16[264,128]{1,0:T(8,128)(2,1)S(1)}, u32[]{:S(2)}, u32[]{:S(2)}) collective-permute-start(s16[264,128]{1,0:T(8,128)(2,1)S(1)} %get-tuple-element.30), channel_id=1, source_target_pairs={{0,1},{1,2},{2,3},{3,4},{4,5},{5,6},{6,7},{7,0},{8,9},{9,10},{10,1... | collective-permute-start | bytes 202760 | tf_op jit(solution)/shard_map/ppermute | solution.py:35
  98.5 6.4 %collective-permute-start.9 = (s16[264,128]{1,0:T(8,128)(2,1)S(1)}, s16[264,128]{1,0:T(8,128)(2,1)S(1)}, u32[]{:S(2)}, u32[]{:S(2)}) collective-permute-start(s16[264,128]{1,0:T(8,128)(2,1)S(1)} %get-tuple-element.31), channel_id=1, source_target_pairs={{0,2},{1,3},{2,4},{3,5},{4,6},{5,7},{6,0},{7,1},{8,10},{9,11},{10,... | collective-permute-start | bytes 202760 | tf_op jit(solution)/shard_map/ppermute | solution.py:35

commit v6 on v4

--- a/solution.py
+++ b/solution.py
@@ -133,13 +133,13 @@
 
 
 def product_kernel(gx, gy, groups, steps, row_ref, col_ref, work_ref, tiles, feats_ref, swap_ref, *refs):
-    own_ref, rest_ref, right_ref, left_ref, acc, held, made, exps, sems = refs
+    keep_ref, even_ref, odd_ref, acc, held, made, exps, sems = refs
     slots, order, _ = tiles.shape
     per_step = slots // steps
     vblocks = held.shape[0] // gx
     blocks = acc.shape[0]
     span = blocks // groups
-    a, y = lax.axis_index("gx"), lax.axis_index("y")
+    a = lax.axis_index("gx")
     cores = 2
 
     acc[...] = jnp.zeros_like(acc)
@@ -171,32 +171,28 @@
 
         lax.fori_loop(0, per_step, add, 0, unroll=True)
 
-    half = span // 2
-    there, behind = (lax.rem(y + k, groups) * span for k in (1, groups - 1))
-    far = lax.rem(y + groups // 2, groups) * span
-    leaving = [
-        pltpu.make_async_copy(acc.at[pl.ds(at, n)], ref, sems.at[i])
-        for i, (at, n, ref) in enumerate(
-            (
-                (y * span, span, own_ref),
-                (there, half, rest_ref.at[pl.ds(0, half)]),
-                (behind + half, half, rest_ref.at[pl.ds(half, half)]),
-            )
-        )
-    ]
-    for c in leaving:
-        c.start()
-    for q_ref, starts in ((right_ref, (far, there + half)), (left_ref, (far + half, behind))):
-        for n, base in enumerate(starts):
-
-            def code(i, carry):
-                coded(acc[base + i], q_ref, exps, (n * half + i) * order, n * half + i)
-                return carry
-
-            lax.fori_loop(0, half, code, 0, unroll=2)
-        store_exps(q_ref, exps, span, order)
-    for c in leaving:
-        c.wait()
+    owners = span // vblocks
+    pairs = owners // 2
+    side = lax.rem(lax.axis_index("z"), 2)
+
+    def leave(n, carry):
+        at = lax.div(n, pairs) * span + (2 * lax.rem(n, pairs) + side) * vblocks
+        pltpu.make_async_copy(
+            acc.at[pl.ds(at, vblocks)], keep_ref.at[pl.ds(n * vblocks, vblocks)], sems.at[0]
+        ).start()
+        return carry
+
+    lax.fori_loop(0, groups * pairs, leave, 0)
+    for v, q_ref in enumerate((even_ref, odd_ref)):
+
+        def code(n, carry):
+            at = lax.div(n, pairs) * span + (2 * lax.rem(n, pairs) + 1 - side) * vblocks + v
+            coded(acc[at], q_ref, exps, n * order, n)
+            return carry
+
+        lax.fori_loop(0, groups * pairs, code, 0, unroll=2)
+        store_exps(q_ref, exps, groups * pairs, order)
+    pltpu.make_async_copy(acc.at[pl.ds(0, keep_ref.shape[0])], keep_ref, sems.at[0]).wait()
 
 
 def scales_of(ref, at):
@@ -213,50 +209,70 @@
     q_ref[pl.ds(count * order, exps.shape[0]), :] = exps[...].astype(jnp.int32).astype(jnp.int16)
 
 
+def join_kernel(order, vblocks, groups, keep_ref, even_ref, odd_ref, own_ref, rest_ref, right_ref, left_ref, scales, exps):
+    span = keep_ref.shape[0] // groups
+    half = span // 2
+    lines = groups * span // vblocks
+    y = lax.axis_index("y")
+    got = (even_ref, odd_ref)
+    for v, g in enumerate(got):
+        scales[pl.ds(v * lines, lines), :] = scales_of(g, lines * order)
+
+    def total(chunk, pair, v):
+        n = chunk * (span // vblocks) + pair
+        x = got[v][pl.ds(n * order, order), :].astype(jnp.int32).astype(jnp.float32)
+        return keep_ref[n * vblocks + v] + x * scales[pl.ds(v * lines + n, 1), :]
+
+    there, far, behind = (lax.rem(y + k, groups) for k in range(1, groups))
+    low, high = 0, half // vblocks
+    for chunk, start, at in ((y, low, 0), (y, high, half)):
+        for i in range(half // vblocks):
+            for v in range(vblocks):
+                own_ref[at + i * vblocks + v] = total(chunk, start + i, v)
+    for chunk, start, at in ((there, low, 0), (behind, high, half)):
+        for i in range(half // vblocks):
+            for v in range(vblocks):
+                rest_ref[at + i * vblocks + v] = total(chunk, start + i, v)
+    for q_ref, parts in ((right_ref, ((far, low), (there, high))), (left_ref, ((far, high), (behind, low)))):
+        for n, (chunk, start) in enumerate(parts):
+            for i in range(half // vblocks):
+                for v in range(vblocks):
+                    row = n * half + i * vblocks + v
+                    coded(total(chunk, start + i, v), q_ref, exps, row * order, row)
+        store_exps(q_ref, exps, span, order)
+
+
 def relay_kernel(order, rest_ref, low_ref, high_ref, right_ref, left_ref, scales, exps):
     span = rest_ref.shape[0]
     half = span // 2
+    exps[...] = jnp.zeros_like(exps)
     for side, (got, q_ref) in enumerate(((low_ref, right_ref), (high_ref, left_ref))):
         scales[...] = scales_of(got, span * order)
-
-        def add(i, carry):
+        for i in range(half):
             part = got[pl.ds(i * order, order), :].astype(jnp.int32).astype(jnp.float32)
             x = rest_ref[side * half + i] + part * scales[pl.ds(i, 1), :]
             coded(x, q_ref, exps, i * order, i)
-            return carry
-
-        lax.fori_loop(0, half, add, 0, unroll=2)
         store_exps(q_ref, exps, half, order)
 
 
 def middle_kernel(order, vblocks, own_ref, low_ref, high_ref, low2_ref, high2_ref, out_ref, *refs):
-    q_refs, (total, scales, exps) = refs[:-3], refs[-3:]
+    q_refs, (total, exps) = refs[:-2], refs[-2:]
     span = own_ref.shape[0]
     half = span // 2
     owners = span // vblocks
-    z = lax.axis_index("z")
+    mine = lax.div(lax.axis_index("z"), 2)
     exps[...] = jnp.zeros_like(exps)
-    scales[pl.ds(0, half), :] = scales_of(high_ref, span * order)[half:, :]
-    scales[pl.ds(half, half), :] = scales_of(low_ref, span * order)[half:, :]
-    scales[pl.ds(span, half), :] = scales_of(low2_ref, half * order)
-    scales[pl.ds(span + half, half), :] = scales_of(high2_ref, half * order)
-
-    def part(ref, at, scale):
-        x = ref[pl.ds(at * order, order), :].astype(jnp.int32).astype(jnp.float32)
-        return x * scales[pl.ds(scale, 1), :]
-
     for side, (near, last) in enumerate(((high_ref, low2_ref), (low_ref, high2_ref))):
-
-        def add(i, carry):
-            at = side * half + i
-            total[at] = own_ref[at] + part(near, half + i, at) + part(last, i, span + at)
-            return carry
-
-        lax.fori_loop(0, half, add, 0, unroll=2)
+        near_scales, last_scales = scales_of(near, span * order), scales_of(last, half * order)
+        for i in range(half):
+            x = own_ref[side * half + i]
+            for ref, at, scale in ((near, half + i, near_scales[half + i : half + i + 1]), (last, i, last_scales[i : i + 1])):
+                x = x + ref[pl.ds(at * order, order), :].astype(jnp.int32).astype(jnp.float32) * scale
+            total[side * half + i] = x
     for v in range(vblocks):
-        out_ref[pl.ds(v * order, order), :] = total[z * vblocks + v]
+        out_ref[pl.ds(v * order, order), :] = total[mine * vblocks + v]
     for k, q_ref in enumerate(q_refs, 1):
-        base = lax.rem(z + k, owners) * vblocks
+        base = lax.rem(mine + k, owners) * vblocks
         for v in range(vblocks):
             coded(total[base + v], q_ref, exps, v * order, v)
         store_exps(q_ref, exps, vblocks, order)
@@ -332,30 +348,43 @@
     def line(count, more=8):
         return vmem((count * order + more, width), i16)
 
-    f32_blocks = pltpu.HBM((span, order, width), jnp.float32)
-    own, rest, right, left = pl.pallas_call(
+    lines = blocks // 2 // vblocks
+    few = span // 2
+    keep, even, odd = pl.pallas_call(
         lambda *refs: product_kernel(gx, peers, ny, steps, *refs),
         in_specs=[SMEM] * 3 + [VMEM] * 3,
-        out_specs=[ANY, ANY, VMEM, VMEM],
-        out_shape=[f32_blocks, f32_blocks, line(span, span), line(span, span)],
+        out_specs=[ANY, VMEM, VMEM],
+        out_shape=[pltpu.HBM((blocks // 2, order, width), jnp.float32), line(lines, lines), line(lines, lines)],
         scratch_shapes=[
             pltpu.VMEM((blocks, order, width), jnp.float32),
             pltpu.VMEM((gx * vblocks, order, width), jnp.bfloat16),
             pltpu.VMEM((slots // steps, order, width), jnp.float32),
-            pltpu.VMEM((span, width), jnp.float32),
-            pltpu.SemaphoreType.DMA((3,)),
+            pltpu.VMEM((lines, width), jnp.float32),
+            pltpu.SemaphoreType.DMA((1,)),
         ],
         compiler_params=limit(16),
         name="products",
     )(tile_row, tile_col, tile_work, *(in_vmem(f) for f in (tiles, feats, swapped)))
-    low = shifted(right, "y", 1)
-    high = shifted(left, "y", -1)
+    near = []
+    for v, q in enumerate((even, odd)):
+        near.append(lax.ppermute(q, "z", [(i, ((i + v) ^ 1) - v & nz - 1) for i in range(nz)]))
+    some = vmem((few, order, width), jnp.float32)
+    own, rest, right, left = pl.pallas_call(
+        lambda *refs: join_kernel(order, vblocks, ny, *refs),
+        in_specs=[VMEM] * 3,
+        out_specs=[VMEM] * 4,
+        out_shape=[some, some, line(few), line(few)],
+        scratch_shapes=[pltpu.VMEM((2 * lines, width), jnp.float32), pltpu.VMEM((8, width), jnp.float32)],
+        compiler_params=limit(12),
+        name="join",
+    )(keep, *near)
+    low, high = shifted(right, "y", 1), shifted(left, "y", -1)
     right, left = pl.pallas_call(
         lambda *refs: relay_kernel(order, *refs),
         in_specs=[VMEM] * 3,
         out_specs=[VMEM] * 2,
-        out_shape=[line(span // 2)] * 2,
-        scratch_shapes=[pltpu.VMEM((span, width), jnp.float32), pltpu.VMEM((span // 2, width), jnp.float32)],
+        out_shape=[line(few // 2)] * 2,
+        scratch_shapes=[pltpu.VMEM((8, width), jnp.float32), pltpu.VMEM((8, width), jnp.float32)],
         compiler_params=limit(8),
         name="relay",
     )(rest, low, high)
@@ -363,20 +392,18 @@
     own_z, *coded_z = pl.pallas_call(
         lambda *refs: middle_kernel(order, vblocks, *refs),
         in_specs=[VMEM] * 5,
-        out_specs=[VMEM] * nz,
-        out_shape=[vmem((vblocks * order, width), jnp.float32)] + [line(vblocks)] * (nz - 1),
-        scratch_shapes=[
-            pltpu.VMEM((span, order, width), jnp.float32),
-            pltpu.VMEM((2 * span, width), jnp.float32),
-            pltpu.VMEM((8, width), jnp.float32),
-        ],
-        compiler_params=limit(12),
+        out_specs=[VMEM] * (nz // 2),
+        out_shape=[vmem((vblocks * order, width), jnp.float32)] + [line(vblocks)] * (nz // 2 - 1),
+        scratch_shapes=[pltpu.VMEM((few, order, width), jnp.float32), pltpu.VMEM((8, width), jnp.float32)],
+        compiler_params=limit(8),
         name="middle",
     )(own, low, high, low2, high2)
-    got_z = [shifted(q, "z", k) for k, q in enumerate(coded_z, 1)]
+    got_z = []
+    for k, q in enumerate(coded_z, 1):
+        got_z.append(shifted(q, "z", 2 * k))
     product = pl.pallas_call(
         lambda *refs: last_kernel(order, vblocks, *refs),
-        in_specs=[VMEM] * nz,
+        in_specs=[VMEM] * (nz // 2),
         out_specs=VMEM,
         out_shape=jax.ShapeDtypeStruct((vblocks * order, width), jnp.float32),
         compiler_params=limit(4),

time: 109 us -> 122 us (1.12)
  the two profiles are of different devices: /device:TPU:56 before, /device:TPU:40 now
where the time goes in v6:
time: 122 us; the launch traced here: 120 us
  waiting for transfers between devices  63.5 us (52%)
  starting transfers between devices  38.6 us (32%)
  Pallas kernels  15.8 us (13%)
  local copies, waits for them, and re-layouts  1.62 us (1%)
    ppermute x2, waiting for transfers between devices, on_device(): lax.ppermute(q, 'z', [(i, (i + v ^ 1) - v & nz - 1) for i in range(nz)])  39.5 us
    ppermute x7, starting transfers between devices, shifted(): lax.ppermute(array, axis, [(i, (i + by) % size) for i in range(size)])  12.9 us
    ppermute x7, waiting for transfers between devices, shifted(): lax.ppermute(array, axis, [(i, (i + by) % size) for i in range(size)])  11.3 us
    all_to_all x1, starting transfers between devices, on_device(): meta = lax.all_to_all(told, GY, split_axis=0, concat_axis=0, tiled=True)  11.3 us
    all_to_all x1, starting transfers between devices, on_device(): got = lax.all_to_all(sent, GY, split_axis=0, concat_axis=0, tiled=True)  6.73 us
    all_to_all x1, waiting for transfers between devices, on_device(): meta = lax.all_to_all(told, GY, split_axis=0, concat_axis=0, tiled=True)  6.38 us
    ppermute x3, waiting for transfers between devices, on_device(): lax.ppermute(mine[0], 'gx', [(i, (i + cores * k) % gx) for i in range(gx)])  4.78 us
    ppermute x3, starting transfers between devices, on_device(): lax.ppermute(mine[0], 'gx', [(i, (i + cores * k) % gx) for i in range(gx)])  4.52 us
  transfers between devices with their start and end apart: 15, of which 12 were waited for; matrix products, arithmetic and copies ran while one was open for 0% of the time, Pallas kernels for 8%

profile of v6, /device:TPU:40, one launch (start us, length us, event | category | flops | bytes accessed | tf_op | source)
XLA Modules:
  0.0 120.3 jit_solution(7475229462650599919)
XLA Ops:
  0.6 1.4 %tell.1 = s32[32,2,128]{2,1,0:T(2,128)} custom-call(s32[64]{0:T(128)} %refs_0_.3, s32[64]{0:T(128)} %refs_1_.3, s32[64]{0:T(128)} %refs_2_.3), custom_call_target="tpu_custom_call" | custom-call | tf_op jit(solution)/shard_map/tell/pallas_call | solution.py:298
  2.1 11.3 %all-to-all-start = ((s32[32,2,128]{2,1,0:T(2,128)}), s32[32,2,128]{2,1,0:T(2,128)S(1)}, u32[]{:S(2)}, u32[]{:S(2)}) async-start(s32[32,2,128]{2,1,0:T(2,128)} %tell.1), calls=%async_computation | async-start | bytes 65536 | tf_op jit(solution)/shard_map/all_to_all | solution.py:312
  13.3 1.6 %stage.1.refs_3_.refs_1_ = bf16[64,128,128]{2,1,0:T(8,128)(2,1)S(1)} custom-call(bf16[64,128,128]{2,1,0:T(8,128)(2,1)} %vals_ref.1), custom_call_target="tpu_custom_call" | custom-call | tf_op jit(solution)/shard_map/stage/pallas_call | solution.py:315
  14.9 6.4 %all-to-all-done.refs_0_ = s32[32,2,128]{2,1,0:T(2,128)S(1)} async-done(((s32[32,2,128]{2,1,0:T(2,128)}), s32[32,2,128]{2,1,0:T(2,128)S(1)}, u32[]{:S(2)}, u32[]{:S(2)}) %all-to-all-start) | async-done | bytes 32800 | tf_op jit(solution)/shard_map/all_to_all | solution.py:312
  21.3 2.5 %plan.1 = bf16[64,128,128]{2,1,0:T(8,128)(2,1)} custom-call(s32[32,2,128]{2,1,0:T(2,128)S(1)} %all-to-all-done.refs_0_, bf16[64,128,128]{2,1,0:T(8,128)(2,1)S(1)} %stage.1.refs_3_.refs_1_), custom_call_target="tpu_custom_call" | custom-call | tf_op jit(solution)/shard_map/plan/pallas_call | solution.py:325
  23.8 6.7 %all-to-all-start.1 = ((bf16[64,128,128]{2,1,0:T(8,128)(2,1)}), bf16[64,128,128]{2,1,0:T(8,128)(2,1)}, u32[]{:S(2)}, u32[]{:S(2)}) async-start(bf16[64,128,128]{2,1,0:T(8,128)(2,1)} %plan.1), calls=%async_computation.1 | async-start | bytes 4194304 | tf_op jit(solution)/shard_map/all_to_all | solution.py:342
  30.6 2.8 %collective-permute-start.2 = (bf16[2,128,128]{2,1,0:T(8,128)(2,1)S(1)}, bf16[2,128,128]{2,1,0:T(8,128)(2,1)S(1)}, u32[]{:S(2)}, u32[]{:S(2)}) collective-permute-start(bf16[2,128,128]{2,1,0:T(8,128)(2,1)S(1)} %bitcast.1), channel_id=1, source_target_pairs={{0,192},{32,224},{64,0},{96,32},{128,64},{160,96},{192,128},{224,1... | collective-permute-start | bytes 196616 | tf_op jit(solution)/shard_map/ppermute | solution.py:311
  33.4 0.8 collective-permute-start.1
  34.2 0.9 collective-permute-start
  35.3 3.9 %collective-permute-done.1 = bf16[2,128,128]{2,1,0:T(8,128)(2,1)S(1)} collective-permute-done((bf16[2,128,128]{2,1,0:T(8,128)(2,1)S(1)}, bf16[2,128,128]{2,1,0:T(8,128)(2,1)S(1)}, u32[]{:S(2)}, u32[]{:S(2)}) %collective-permute-start.1) | collective-permute-done | bytes 65568 | tf_op jit(solution)/shard_map/ppermute | solution.py:311
  39.2 0.7 collective-permute-done
  40.0 1.5 %collective-permute-done.3.refs_5_ = bf16[8,128,128]{2,1,0:T(8,128)(2,1)S(1)} collective-permute-done((bf16[8,128,128]{2,1,0:T(8,128)(2,1)S(1)}, bf16[8,128,128]{2,1,0:T(8,128)(2,1)S(1)}, u32[]{:S(2)}, u32[]{:S(2)}) %collective-permute-start.3) | collective-permute-done | bytes 262176 | tf_op jit(solution)/shard_map/ppermute | solution.py:314
  41.6 3.3 %products.1 = (f32[32,128,128]{2,1,0:T(8,128)}, s16[2064,128]{1,0:T(8,128)(2,1)S(1)}, s16[2064,128]{1,0:T(8,128)(2,1)S(1)}) custom-call(s32[64]{0:T(128)S(1)} %copy-done.1, s32[64]{0:T(128)S(1)} %copy-done.2, s32[64]{0:T(128)S(1)} %copy-done.3, bf16[64,128,128]{2,1,0:T(8,128)(2,1)S(1)} %stage.1.refs_3_.refs_1_, ...), custom_call_target="tpu_custom_call" | custom-call | tf_op jit(solution)/shard_map/products/pallas_call | solution.py:353
  44.9 0.6 collective-permute-start.4
  45.5 2.4 %collective-permute-start.5 = (s16[2064,128]{1,0:T(8,128)(2,1)S(1)}, s16[2064,128]{1,0:T(8,128)(2,1)S(1)}, u32[]{:S(2)}, u32[]{:S(2)}) collective-permute-start(s16[2064,128]{1,0:T(8,128)(2,1)S(1)} %get-tuple-element.24), channel_id=1, source_target_pairs={{0,7},{1,2},{2,1},{3,4},{4,3},{5,6},{6,5},{7,0},{8,15},{9,10},{10,... | collective-permute-start | bytes 1585160 | tf_op jit(solution)/shard_map/ppermute | solution.py:370
  47.9 38.6 %collective-permute-done.4.refs_1_ = s16[2064,128]{1,0:T(8,128)(2,1)S(1)} collective-permute-done((s16[2064,128]{1,0:T(8,128)(2,1)S(1)}, s16[2064,128]{1,0:T(8,128)(2,1)S(1)}, u32[]{:S(2)}, u32[]{:S(2)}) %collective-permute-start.4) | collective-permute-done | bytes 528416 | tf_op jit(solution)/shard_map/ppermute | solution.py:370
  86.5 1.0 collective-permute-done.5.refs_2_
  87.4 1.6 %copy-done = f32[32,128,128]{2,1,0:T(8,128)S(1)} copy-done((f32[32,128,128]{2,1,0:T(8,128)S(1)}, f32[32,128,128]{2,1,0:T(8,128)}, u32[]{:S(2)}) %copy-start) | copy-done | bytes 2097176
  89.5 1.6 %collective-permute-start.6 = (s16[1032,128]{1,0:T(8,128)(2,1)S(1)}, s16[1032,128]{1,0:T(8,128)(2,1)S(1)}, u32[]{:S(2)}, u32[]{:S(2)}) collective-permute-start(s16[1032,128]{1,0:T(8,128)(2,1)S(1)} %get-tuple-element.26), channel_id=1, source_target_pairs={{0,8},{8,16},{16,24},{24,0},{1,9},{9,17},{17,25},{25,1},{2,10},{10... | collective-permute-start | bytes 792584 | tf_op jit(solution)/shard_map/ppermute | solution.py:35
  91.6 5.3 %collective-permute-done.6.refs_1_ = s16[1032,128]{1,0:T(8,128)(2,1)S(1)} collective-permute-done((s16[1032,128]{1,0:T(8,128)(2,1)S(1)}, s16[1032,128]{1,0:T(8,128)(2,1)S(1)}, u32[]{:S(2)}, u32[]{:S(2)}) %collective-permute-start.6) | collective-permute-done | bytes 264224 | tf_op jit(solution)/shard_map/ppermute | solution.py:35
  96.9 1.2 %collective-permute-done.7.refs_2_ = s16[1032,128]{1,0:T(8,128)(2,1)S(1)} collective-permute-done((s16[1032,128]{1,0:T(8,128)(2,1)S(1)}, s16[1032,128]{1,0:T(8,128)(2,1)S(1)}, u32[]{:S(2)}, u32[]{:S(2)}) %collective-permute-start.7) | collective-permute-done | bytes 264224 | tf_op jit(solution)/shard_map/ppermute | solution.py:35
  98.4 1.3 %collective-permute-start.8 = (s16[520,128]{1,0:T(8,128)(2,1)S(1)}, s16[520,128]{1,0:T(8,128)(2,1)S(1)}, u32[]{:S(2)}, u32[]{:S(2)}) collective-permute-start(s16[520,128]{1,0:T(8,128)(2,1)S(1)} %get-tuple-element.29), channel_id=1, source_target_pairs={{0,8},{8,16},{16,24},{24,0},{1,9},{9,17},{17,25},{25,1},{2,10},{10... | collective-permute-start | bytes 399368 | tf_op jit(solution)/shard_map/ppermute | solution.py:35
  99.7 0.8 collective-permute-start.9
  100.5 3.0 %collective-permute-done.8.refs_3_ = s16[520,128]{1,0:T(8,128)(2,1)S(1)} collective-permute-done((s16[520,128]{1,0:T(8,128)(2,1)S(1)}, s16[520,128]{1,0:T(8,128)(2,1)S(1)}, u32[]{:S(2)}, u32[]{:S(2)}) %collective-permute-start.8) | collective-permute-done | bytes 133152 | tf_op jit(solution)/shard_map/ppermute | solution.py:35
  103.4 1.2 %collective-permute-done.9.refs_4_ = s16[520,128]{1,0:T(8,128)(2,1)S(1)} collective-permute-done((s16[520,128]{1,0:T(8,128)(2,1)S(1)}, s16[520,128]{1,0:T(8,128)(2,1)S(1)}, u32[]{:S(2)}, u32[]{:S(2)}) %collective-permute-start.9) | collective-permute-done | bytes 133152 | tf_op jit(solution)/shard_map/ppermute | solution.py:35
  104.9 3.5 %collective-permute-start.10 = (s16[264,128]{1,0:T(8,128)(2,1)S(1)}, s16[264,128]{1,0:T(8,128)(2,1)S(1)}, u32[]{:S(2)}, u32[]{:S(2)}) collective-permute-start(s16[264,128]{1,0:T(8,128)(2,1)S(1)} %get-tuple-element.32), channel_id=1, source_target_pairs={{0,2},{1,3},{2,4},{3,5},{4,6},{5,7},{6,0},{7,1},{8,10},{9,11},{10,... | collective-permute-start | bytes 202760 | tf_op jit(solution)/shard_map/ppermute | solution.py:35
  108.4 1.2 %collective-permute-start.11 = (s16[264,128]{1,0:T(8,128)(2,1)S(1)}, s16[264,128]{1,0:T(8,128)(2,1)S(1)}, u32[]{:S(2)}, u32[]{:S(2)}) collective-permute-start(s16[264,128]{1,0:T(8,128)(2,1)S(1)} %get-tuple-element.33), channel_id=1, source_target_pairs={{0,4},{1,5},{2,6},{3,7},{4,0},{5,1},{6,2},{7,3},{8,12},{9,13},{10,... | collective-permute-start | bytes 202760 | tf_op jit(solution)/shard_map/ppermute | solution.py:35
  109.6 4.0 %collective-permute-start.12 = (s16[264,128]{1,0:T(8,128)(2,1)S(1)}, s16[264,128]{1,0:T(8,128)(2,1)S(1)}, u32[]{:S(2)}, u32[]{:S(2)}) collective-permute-start(s16[264,128]{1,0:T(8,128)(2,1)S(1)} %get-tuple-element.34), channel_id=1, source_target_pairs={{0,6},{1,7},{2,0},{3,1},{4,2},{5,3},{6,4},{7,5},{8,14},{9,15},{10,... | collective-permute-start | bytes 202760 | tf_op jit(solution)/shard_map/ppermute | solution.py:35
  113.7 2.8 %list.1 = (s32[32]{0:T(128)}, s32[32]{0:T(128)}, s32[32]{0:T(128)}, s32[32]{0:T(128)S(1)}) custom-call(s32[32,2,128]{2,1,0:T(2,128)S(1)} %all-to-all-done.refs_0_), custom_call_target="tpu_custom_call" | custom-call | tf_op jit(solution)/shard_map/list/pallas_call | solution.py:334
  116.5 0.5 collective-permute-done.11.refs_2_
  117.0 0.7 last.1
  117.7 2.6 %keep.1 = bf16[32,128,128]{2,1,0:T(8,128)(2,1)} custom-call(s32[32]{0:T(128)S(1)} %get-tuple-element.35.refs_0_, bf16[64,128,128]{2,1,0:T(8,128)(2,1)} %all-to-all-done.1.refs_1_), custom_call_target="tpu_custom_call" | custom-call | tf_op jit(solution)/shard_map/keep/pallas_call | solution.py:413
  (19 shorter events, 1.8 us)
Async XLA Ops:
  2.1 19.2 %all-to-all-start = ((s32[32,2,128]{2,1,0:T(2,128)}), s32[32,2,128]{2,1,0:T(2,128)S(1)}, u32[]{:S(2)}, u32[]{:S(2)}) async-start(s32[32,2,128]{2,1,0:T(2,128)} %tell.1), calls=%async_computation | async-start | bytes 65536 | tf_op jit(solution)/shard_map/all_to_all | solution.py:312
  23.8 6.8 %copy-start.4 = (bf16[256,128]{1,0:T(8,128)(2,1)S(1)}, bf16[256,128]{1,0:T(8,128)(2,1)}, u32[]{:S(2)}) copy-start(bf16[256,128]{1,0:T(8,128)(2,1)} %param.5) | copy-start | bytes 196612
  23.8 17.8 %copy-start.1 = (s32[64]{0:T(128)S(1)}, s32[64]{0:T(128)}, u32[]{:S(2)}) copy-start(s32[64]{0:T(128)} %refs_0_.3) | copy-start | bytes 772
  23.8 17.8 %copy-start.2 = (s32[64]{0:T(128)S(1)}, s32[64]{0:T(128)}, u32[]{:S(2)}) copy-start(s32[64]{0:T(128)} %refs_1_.3) | copy-start | bytes 772
  23.8 17.7 %copy-start.3 = (s32[64]{0:T(128)S(1)}, s32[64]{0:T(128)}, u32[]{:S(2)}) copy-start(s32[64]{0:T(128)} %refs_2_.3) | copy-start | bytes 772
  23.8 93.9 %all-to-all-start.1 = ((bf16[64,128,128]{2,1,0:T(8,128)(2,1)}), bf16[64,128,128]{2,1,0:T(8,128)(2,1)}, u32[]{:S(2)}, u32[]{:S(2)}) async-start(bf16[64,128,128]{2,1,0:T(8,128)(2,1)} %plan.1), calls=%async_computation.1 | async-start | bytes 4194304 | tf_op jit(solution)/shard_map/all_to_all | solution.py:342
  30.6 4.7 %collective-permute-start.2 = (bf16[2,128,128]{2,1,0:T(8,128)(2,1)S(1)}, bf16[2,128,128]{2,1,0:T(8,128)(2,1)S(1)}, u32[]{:S(2)}, u32[]{:S(2)}) collective-permute-start(bf16[2,128,128]{2,1,0:T(8,128)(2,1)S(1)} %bitcast.1), channel_id=1, source_target_pairs={{0,192},{32,224},{64,0},{96,32},{128,64},{160,96},{192,128},{224,1... | collective-permute-start | bytes 196616 | tf_op jit(solution)/shard_map/ppermute | solution.py:311
  33.4 5.8 %collective-permute-start.1 = (bf16[2,128,128]{2,1,0:T(8,128)(2,1)S(1)}, bf16[2,128,128]{2,1,0:T(8,128)(2,1)S(1)}, u32[]{:S(2)}, u32[]{:S(2)}) collective-permute-start(bf16[2,128,128]{2,1,0:T(8,128)(2,1)S(1)} %bitcast.2), channel_id=1, source_target_pairs={{0,128},{32,160},{64,192},{96,224},{128,0},{160,32},{192,64},{224,... | collective-permute-start | bytes 196616 | tf_op jit(solution)/shard_map/ppermute | solution.py:311
  34.2 5.7 %collective-permute-start = (bf16[2,128,128]{2,1,0:T(8,128)(2,1)S(1)}, bf16[2,128,128]{2,1,0:T(8,128)(2,1)S(1)}, u32[]{:S(2)}, u32[]{:S(2)}) collective-permute-start(bf16[2,128,128]{2,1,0:T(8,128)(2,1)S(1)} %bitcast.3), channel_id=1, source_target_pairs={{0,64},{32,96},{64,128},{96,160},{128,192},{160,224},{192,0},{224,... | collective-permute-start | bytes 196616 | tf_op jit(solution)/shard_map/ppermute | solution.py:311
  39.9 1.6 %collective-permute-start.3 = (bf16[8,128,128]{2,1,0:T(8,128)(2,1)S(1)}, bf16[8,128,128]{2,1,0:T(8,128)(2,1)S(1)}, u32[]{:S(2)}, u32[]{:S(2)}) collective-permute-start(bf16[8,128,128]{2,1,0:T(8,128)(2,1)S(1)} %pad_maximum_fusion.refs_4_), channel_id=1, source_target_pairs={{0,32},{32,0},{64,96},{96,64},{128,160},{160,128},{192,224},{224,1... | collective-permute-start | bytes 786440 | tf_op jit(solution)/shard_map/ppermute | solution.py:314
  44.9 41.6 %collective-permute-start.4 = (s16[2064,128]{1,0:T(8,128)(2,1)S(1)}, s16[2064,128]{1,0:T(8,128)(2,1)S(1)}, u32[]{:S(2)}, u32[]{:S(2)}) collective-permute-start(s16[2064,128]{1,0:T(8,128)(2,1)S(1)} %get-tuple-element.23), channel_id=1, source_target_pairs={{0,1},{1,0},{2,3},{3,2},{4,5},{5,4},{6,7},{7,6},{8,9},{9,8},{10,11... | collective-permute-start | bytes 1585160 | tf_op jit(solution)/shard_map/ppermute | solution.py:370
  45.5 41.9 %collective-permute-start.5 = (s16[2064,128]{1,0:T(8,128)(2,1)S(1)}, s16[2064,128]{1,0:T(8,128)(2,1)S(1)}, u32[]{:S(2)}, u32[]{:S(2)}) collective-permute-start(s16[2064,128]{1,0:T(8,128)(2,1)S(1)} %get-tuple-element.24), channel_id=1, source_target_pairs={{0,7},{1,2},{2,1},{3,4},{4,3},{5,6},{6,5},{7,0},{8,15},{9,10},{10,... | collective-permute-start | bytes 1585160 | tf_op jit(solution)/shard_map/ppermute | solution.py:370
  87.4 1.6 %copy-start = (f32[32,128,128]{2,1,0:T(8,128)S(1)}, f32[32,128,128]{2,1,0:T(8,128)}, u32[]{:S(2)}) copy-start(f32[32,128,128]{2,1,0:T(8,128)} %get-tuple-element.22.refs_0_) | copy-start | bytes 6291460
  89.5 7.4 %collective-permute-start.6 = (s16[1032,128]{1,0:T(8,128)(2,1)S(1)}, s16[1032,128]{1,0:T(8,128)(2,1)S(1)}, u32[]{:S(2)}, u32[]{:S(2)}) collective-permute-start(s16[1032,128]{1,0:T(8,128)(2,1)S(1)} %get-tuple-element.26), channel_id=1, source_target_pairs={{0,8},{8,16},{16,24},{24,0},{1,9},{9,17},{17,25},{25,1},{2,10},{10... | collective-permute-start | bytes 792584 | tf_op jit(solution)/shard_map/ppermute | solution.py:35
  91.1 7.1 %collective-permute-start.7 = (s16[1032,128]{1,0:T(8,128)(2,1)S(1)}, s16[1032,128]{1,0:T(8,128)(2,1)S(1)}, u32[]{:S(2)}, u32[]{:S(2)}) collective-permute-start(s16[1032,128]{1,0:T(8,128)(2,1)S(1)} %get-tuple-element.27), channel_id=1, source_target_pairs={{0,24},{8,0},{16,8},{24,16},{1,25},{9,1},{17,9},{25,17},{2,26},{10... | collective-permute-start | bytes 792584 | tf_op jit(solution)/shard_map/ppermute | solution.py:35
  98.4 5.1 %collective-permute-start.8 = (s16[520,128]{1,0:T(8,128)(2,1)S(1)}, s16[520,128]{1,0:T(8,128)(2,1)S(1)}, u32[]{:S(2)}, u32[]{:S(2)}) collective-permute-start(s16[520,128]{1,0:T(8,128)(2,1)S(1)} %get-tuple-element.29), channel_id=1, source_target_pairs={{0,8},{8,16},{16,24},{24,0},{1,9},{9,17},{17,25},{25,1},{2,10},{10... | collective-permute-start | bytes 399368 | tf_op jit(solution)/shard_map/ppermute | solution.py:35
  99.7 5.0 %collective-permute-start.9 = (s16[520,128]{1,0:T(8,128)(2,1)S(1)}, s16[520,128]{1,0:T(8,128)(2,1)S(1)}, u32[]{:S(2)}, u32[]{:S(2)}) collective-permute-start(s16[520,128]{1,0:T(8,128)(2,1)S(1)} %get-tuple-element.30), channel_id=1, source_target_pairs={{0,24},{8,0},{16,8},{24,16},{1,25},{9,1},{17,9},{25,17},{2,26},{10... | collective-permute-start | bytes 399368 | tf_op jit(solution)/shard_map/ppermute | solution.py:35
  104.9 11.5 %collective-permute-start.10 = (s16[264,128]{1,0:T(8,128)(2,1)S(1)}, s16[264,128]{1,0:T(8,128)(2,1)S(1)}, u32[]{:S(2)}, u32[]{:S(2)}) collective-permute-start(s16[264,128]{1,0:T(8,128)(2,1)S(1)} %get-tuple-element.32), channel_id=1, source_target_pairs={{0,2},{1,3},{2,4},{3,5},{4,6},{5,7},{6,0},{7,1},{8,10},{9,11},{10,... | collective-permute-start | bytes 202760 | tf_op jit(solution)/shard_map/ppermute | solution.py:35
  108.4 8.6 %collective-permute-start.11 = (s16[264,128]{1,0:T(8,128)(2,1)S(1)}, s16[264,128]{1,0:T(8,128)(2,1)S(1)}, u32[]{:S(2)}, u32[]{:S(2)}) collective-permute-start(s16[264,128]{1,0:T(8,128)(2,1)S(1)} %get-tuple-element.33), channel_id=1, source_target_pairs={{0,4},{1,5},{2,6},{3,7},{4,0},{5,1},{6,2},{7,3},{8,12},{9,13},{10,... | collective-permute-start | bytes 202760 | tf_op jit(solution)/shard_map/ppermute | solution.py:35
  109.6 7.4 %collective-permute-start.12 = (s16[264,128]{1,0:T(8,128)(2,1)S(1)}, s16[264,128]{1,0:T(8,128)(2,1)S(1)}, u32[]{:S(2)}, u32[]{:S(2)}) collective-permute-start(s16[264,128]{1,0:T(8,128)(2,1)S(1)} %get-tuple-element.34), channel_id=1, source_target_pairs={{0,6},{1,7},{2,0},{3,1},{4,2},{5,3},{6,4},{7,5},{8,14},{9,15},{10,... | collective-permute-start | bytes 202760 | tf_op jit(solution)/shard_map/ppermute | solution.py:35
